TPU v7x, 32 devices: a whole 2x2x4 slice. The times are simulated.
32 devices in a mesh: fsdp: 2 (over y), ctx: 4 (over x, core), tp: 4 (over z).
Axes of the slice: x: 2, y: 2, z: 4, core: 2. Of those that a mesh axis runs over, the one named last changes fastest.
Arguments:
- inputs: bfloat16 [6, 1536, 1024], P('fsdp', ('ctx', 'tp')), may hold values from -6 to 6
- teacher: bfloat16 [6, 1536, 1024], P('fsdp', ('ctx', 'tp')), may hold values from -6 to 6
- clips_dev: int32 [2], replicated, may hold values from 1 to 3, as said below
- ffn1_gain: float32 [1024], replicated, may hold values from 0.5 to 1.5
- ffn1_shift: float32 [1024], replicated, may hold values from -0.625 to 0.625
- ffn1_in: bfloat16 [1024, 4096], P(('fsdp', 'ctx'), 'tp'), may hold values from -0.1875 to 0.1875
- ffn1_in_bias: float32 [4096], replicated, may hold values from -0.625 to 0.625
- ffn1_out: bfloat16 [1024, 4096], P(('fsdp', 'ctx'), 'tp'), may hold values from -0.1875 to 0.1875
- ffn1_out_bias: float32 [1024], replicated, may hold values from -0.625 to 0.625
- attn_gain: float32 [1024], replicated, may hold values from 0.5 to 1.5
- attn_shift: float32 [1024], replicated, may hold values from -0.625 to 0.625
- query_weight: bfloat16 [1024, 1024], P(('fsdp', 'ctx'), 'tp'), may hold values from -0.1875 to 0.1875
- query_bias: float32 [1024], replicated, may hold values from -0.625 to 0.625
- key_weight: bfloat16 [1024, 1024], P(('fsdp', 'ctx'), 'tp'), may hold values from -0.1875 to 0.1875
- value_weight: bfloat16 [1024, 1024], P(('fsdp', 'ctx'), 'tp'), may hold values from -0.1875 to 0.1875
- value_bias: float32 [1024], replicated, may hold values from -0.625 to 0.625
- attn_out_weight: bfloat16 [1024, 1024], P(('fsdp', 'ctx'), 'tp'), may hold values from -0.75 to 0.75
- attn_out_bias: float32 [1024], replicated, may hold values from -0.625 to 0.625
- rel_table: bfloat16 [73, 64], replicated, may hold values from -6 to 6
- conv_gain: float32 [1024], replicated, may hold values from 0.5 to 1.5
- conv_shift: float32 [1024], replicated, may hold values from -0.625 to 0.625
- conv_value_weight: bfloat16 [1024, 1024], P(('fsdp', 'ctx'), 'tp'), may hold values from -0.1875 to 0.1875
- conv_gate_weight: bfloat16 [1024, 1024], P(('fsdp', 'ctx'), 'tp'), may hold values from -0.1875 to 0.1875
- conv_depth: float32 [31, 1024], replicated, may hold values from -1 to 1
- conv_inner_gain: float32 [1024], replicated, may hold values from 0.5 to 1.5
- conv_inner_shift: float32 [1024], replicated, may hold values from -0.625 to 0.625
- conv_out_weight: bfloat16 [1024, 1024], P(('fsdp', 'ctx'), 'tp'), may hold values from -0.1875 to 0.1875
- ffn2_gain: float32 [1024], replicated, may hold values from 0.5 to 1.5
- ffn2_shift: float32 [1024], replicated, may hold values from -0.625 to 0.625
- ffn2_in: bfloat16 [1024, 4096], P(('fsdp', 'ctx'), 'tp'), may hold values from -0.1875 to 0.1875
- ffn2_in_bias: float32 [4096], replicated, may hold values from -0.625 to 0.625
- ffn2_out: bfloat16 [1024, 4096], P(('fsdp', 'ctx'), 'tp'), may hold values from -0.1875 to 0.1875
- ffn2_out_bias: float32 [1024], replicated, may hold values from -0.625 to 0.625
- final_gain: float32 [1024], replicated, may hold values from 0.5 to 1.5
- final_shift: float32 [1024], replicated, may hold values from -0.625 to 0.625
Outputs:
- layer_out: bfloat16 [6, 1536, 1024], P('fsdp', ('ctx', 'tp'))
- loss: float32 [], replicated
- input_grad: float32 [6, 1536, 1024], P('fsdp', ('ctx', 'tp'))
- grad_ffn1_gain: float32 [1024], replicated
- grad_ffn1_shift: float32 [1024], replicated
- grad_ffn1_in: float32 [1024, 4096], P(('fsdp', 'ctx'), 'tp')
- grad_ffn1_in_bias: float32 [4096], replicated
- grad_ffn1_out: float32 [1024, 4096], P(('fsdp', 'ctx'), 'tp')
- grad_ffn1_out_bias: float32 [1024], replicated
- grad_attn_gain: float32 [1024], replicated
- grad_attn_shift: float32 [1024], replicated
- grad_query_weight: float32 [1024, 1024], P(('fsdp', 'ctx'), 'tp')
- grad_query_bias: float32 [1024], replicated
- grad_key_weight: float32 [1024, 1024], P(('fsdp', 'ctx'), 'tp')
- grad_value_weight: float32 [1024, 1024], P(('fsdp', 'ctx'), 'tp')
- grad_value_bias: float32 [1024], replicated
- grad_attn_out_weight: float32 [1024, 1024], P(('fsdp', 'ctx'), 'tp')
- grad_attn_out_bias: float32 [1024], replicated
- grad_rel_table: float32 [73, 64], replicated
- grad_conv_gain: float32 [1024], replicated
- grad_conv_shift: float32 [1024], replicated
- grad_conv_value_weight: float32 [1024, 1024], P(('fsdp', 'ctx'), 'tp')
- grad_conv_gate_weight: float32 [1024, 1024], P(('fsdp', 'ctx'), 'tp')
- grad_conv_depth: float32 [31, 1024], replicated
- grad_conv_inner_gain: float32 [1024], replicated
- grad_conv_inner_shift: float32 [1024], replicated
- grad_conv_out_weight: float32 [1024, 1024], P(('fsdp', 'ctx'), 'tp')
- grad_ffn2_gain: float32 [1024], replicated
- grad_ffn2_shift: float32 [1024], replicated
- grad_ffn2_in: float32 [1024, 4096], P(('fsdp', 'ctx'), 'tp')
- grad_ffn2_in_bias: float32 [4096], replicated
- grad_ffn2_out: float32 [1024, 4096], P(('fsdp', 'ctx'), 'tp')
- grad_ffn2_out_bias: float32 [1024], replicated
- grad_final_gain: float32 [1024], replicated
- grad_final_shift: float32 [1024], replicated
Inputs may be any that keep to these rules, and one draw needn't show every extreme that they name: clips_dev[f] counts the clips of fsdp index f, which fill its first slots; some index holds 3, some other index fewer.
All inputs are finite; a program needn't handle non-finite values.
Results may differ from a plain program's by a relative error of at most 0.028.
Values may be sent and summed in bfloat16 or wider, within the bound.
A program may use at most 384 MiB of HBM per device.

v0:
```python
import math

import jax
import jax.numpy as jnp
from jax import lax
from jax.sharding import PartitionSpec as P

D = 1024
LEFT = 64
HEAD = 64
SEQ = 1536


epsilon = 1e-05


def from_behind(shard, axis, by):
    devices = lax.axis_size(axis)
    pairs = [(i, i + by) for i in range(devices) if 0 <= i + by < devices]
    return lax.ppermute(shard, axis, pairs)


def norm_forward(stream, norm_gain, norm_shift):
    centred = stream - jnp.mean(stream, axis=-1, keepdims=True)
    inverse = lax.rsqrt(jnp.mean(centred * centred, axis=-1, keepdims=True) + epsilon)
    standard = centred * inverse
    return (standard * norm_gain + norm_shift, standard, inverse)


def norm_backward(grad_out, standard, inverse, norm_gain):
    grad_standard = grad_out * norm_gain
    mean_first = jnp.mean(grad_standard, axis=-1, keepdims=True)
    mean_second = jnp.mean(grad_standard * standard, axis=-1, keepdims=True)
    grad_in = inverse * (grad_standard - mean_first - standard * mean_second)
    return (grad_in, jnp.sum(grad_out * standard, axis=(0, 1)), jnp.sum(grad_out, axis=(0, 1)))


def silu_slope(hidden_pre):
    gate_sig = jax.nn.sigmoid(hidden_pre)
    return gate_sig * (1.0 + hidden_pre * (1.0 - gate_sig))


def rows_in(left_reach, right_reach):
    return jnp.einsum("zub,bx->zux", left_reach, right_reach, preferred_element_type=jnp.float32)


def rows_out(left_reach, right_reach):
    return jnp.einsum("anp,op->ano", left_reach, right_reach, preferred_element_type=jnp.float32)


def weight_sum(left_reach, right_reach):
    return jnp.einsum("zbt,zbm->tm", left_reach, right_reach, preferred_element_type=jnp.float32)


def widen(normed):
    return lax.all_gather(normed.astype(jnp.bfloat16), "tp", axis=1, tiled=True)


def narrow(partial_rows):
    return lax.psum_scatter(
        partial_rows.astype(jnp.bfloat16), "tp", scatter_dimension=1, tiled=True
    ).astype(jnp.float32)


def widen_grad(grad_branch):
    return lax.all_gather(grad_branch, "tp", axis=1, tiled=True)


def narrow_grad(partial_rows):
    return lax.psum_scatter(
        partial_rows.astype(jnp.bfloat16), "tp", scatter_dimension=1, tiled=True
    ).astype(jnp.float32)


def local_cut(full_array, tp_rank, size_local):
    return lax.dynamic_slice_in_dim(
        full_array, tp_rank * size_local, size_local, full_array.ndim - 1
    )


def local_put(local_array, tp_rank, full_size):
    shape_full = local_array.shape[:-1] + (full_size,)
    return lax.dynamic_update_slice_in_dim(
        jnp.zeros(shape_full, jnp.float32),
        local_array,
        tp_rank * local_array.shape[-1],
        local_array.ndim - 1,
    )


def band_bias(rel_scores, query_start, key_count):
    lead = rel_scores.shape[:3]
    row_count = lead[2]
    extent = key_count + row_count
    left_edge = jnp.broadcast_to(rel_scores[..., :1], lead + (key_count,))
    right_edge = jnp.broadcast_to(rel_scores[..., -1:], lead + (key_count + row_count,))
    extended = jnp.concatenate([left_edge, rel_scores, right_edge], axis=3)
    start = key_count + LEFT - (row_count - 1) - query_start
    skewed = lax.dynamic_slice_in_dim(extended, start, extent, 3)
    flat = skewed.reshape(lead[:2] + (row_count * extent,))
    sheared = flat[..., row_count - 1 : row_count - 1 + row_count * (extent - 1)]
    return sheared.reshape(lead[:2] + (row_count, extent - 1))[..., :key_count]


def attention_logits(query_heads, key_heads, rel_table, query_start):
    rel_scores = jnp.einsum(
        "slhe,re->shlr", query_heads, rel_table, preferred_element_type=jnp.float32
    )
    bias_entries = band_bias(rel_scores, query_start, key_heads.shape[1])
    dots = jnp.einsum("slhe,smhe->shlm", query_heads, key_heads, preferred_element_type=jnp.float32)
    return ((dots + bias_entries) * (1.0 / math.sqrt(HEAD)), rel_scores)


def ffn_forward(stream, norm_gain, norm_shift, weight_in, bias_in, weight_out, bias_out):
    normed, standard, inverse = norm_forward(stream, norm_gain, norm_shift)
    wide_rows = widen(normed)
    hidden_pre = rows_in(wide_rows, weight_in) + bias_in
    active = jax.nn.silu(hidden_pre).astype(jnp.bfloat16)
    branch = narrow(rows_out(active, weight_out)) + bias_out
    return (stream + 0.5 * branch, (standard, inverse, wide_rows, hidden_pre))


def ffn_backward(grad_stream, saved, norm_gain, weight_in, weight_out):
    standard, inverse, wide_rows, hidden_pre = saved
    grad_branch = (0.5 * grad_stream).astype(jnp.bfloat16)
    out_bias_grad = jnp.sum(grad_branch.astype(jnp.float32), axis=(0, 1))
    wide_grad = widen_grad(grad_branch)
    active = jax.nn.silu(hidden_pre).astype(jnp.bfloat16)
    out_grad = weight_sum(wide_grad, active)
    grad_pre = (rows_in(wide_grad, weight_out) * silu_slope(hidden_pre)).astype(jnp.bfloat16)
    in_bias_grad = jnp.sum(grad_pre.astype(jnp.float32), axis=(0, 1))
    in_grad = weight_sum(wide_rows, grad_pre)
    grad_normed = narrow_grad(rows_out(grad_pre, weight_in))
    grad_in, gain_grad, shift_grad = norm_backward(grad_normed, standard, inverse, norm_gain)
    return (
        grad_stream + grad_in,
        (gain_grad, shift_grad, in_grad, in_bias_grad, out_grad, out_bias_grad),
    )


def attn_forward(stream, norm_gain, norm_shift, weights, biases, rel_table, ctx_rank):
    query_w, key_w, value_w, out_w = weights
    query_b, value_b, out_b = biases
    normed, standard, inverse = norm_forward(stream, norm_gain, norm_shift)
    wide_rows = widen(normed)
    queries = (rows_in(wide_rows, query_w) + query_b).astype(jnp.bfloat16)
    keys_local = rows_in(wide_rows, key_w).astype(jnp.bfloat16)
    values_local = (rows_in(wide_rows, value_w) + value_b).astype(jnp.bfloat16)
    keys_all, values_all = (
        lax.all_gather(keys_local, "ctx", axis=1, tiled=True),
        lax.all_gather(values_local, "ctx", axis=1, tiled=True),
    )
    slot_count, row_count, width_local = queries.shape
    key_count = keys_all.shape[1]
    head_count = width_local // HEAD
    query_heads = queries.reshape(slot_count, row_count, head_count, HEAD)
    key_heads = keys_all.reshape(slot_count, key_count, head_count, HEAD)
    value_heads = values_all.reshape(slot_count, key_count, head_count, HEAD)
    scores, rel_scores = attention_logits(query_heads, key_heads, rel_table, ctx_rank * row_count)
    row_max = jnp.max(scores, axis=-1, keepdims=True)
    log_total = row_max + jnp.log(jnp.sum(jnp.exp(scores - row_max), axis=-1, keepdims=True))
    attn_probs = jnp.exp(scores - log_total).astype(jnp.bfloat16)
    mixed_heads = jnp.einsum(
        "shlm,smhe->slhe", attn_probs, value_heads, preferred_element_type=jnp.float32
    )
    mixed_token_rows = mixed_heads.astype(jnp.bfloat16).reshape(slot_count, row_count, width_local)
    branch = narrow(rows_out(mixed_token_rows, out_w)) + out_b
    return (
        stream + branch,
        (standard, inverse, wide_rows, queries, keys_all, values_all, mixed_token_rows, log_total),
    )


def attn_backward(grad_stream, saved, norm_gain, weights, rel_table, ctx_rank):
    query_w, key_w, value_w, out_w = weights
    standard, inverse, wide_rows, queries, keys_all, values_all, mixed_token_rows, log_total = saved
    grad_branch = grad_stream.astype(jnp.bfloat16)
    out_bias_grad = jnp.sum(grad_branch.astype(jnp.float32), axis=(0, 1))
    wide_grad = widen_grad(grad_branch)
    out_grad = weight_sum(wide_grad, mixed_token_rows)
    grad_mixed = rows_in(wide_grad, out_w).astype(jnp.bfloat16)
    slot_count, row_count, width_local = queries.shape
    key_count = keys_all.shape[1]
    head_count = width_local // HEAD
    query_heads = queries.reshape(slot_count, row_count, head_count, HEAD)
    key_heads = keys_all.reshape(slot_count, key_count, head_count, HEAD)
    value_heads = values_all.reshape(slot_count, key_count, head_count, HEAD)
    grad_heads = grad_mixed.reshape(slot_count, row_count, head_count, HEAD)
    query_start = ctx_rank * row_count
    rel_scores = jnp.einsum(
        "slhe,re->shlr", query_heads, rel_table, preferred_element_type=jnp.float32
    )
    bias_entries, pick_back = jax.vjp(
        lambda table_scores: band_bias(table_scores, query_start, key_count), rel_scores
    )
    dots = jnp.einsum("slhe,smhe->shlm", query_heads, key_heads, preferred_element_type=jnp.float32)
    scale_factor = 1.0 / math.sqrt(HEAD)
    scores = (dots + bias_entries) * scale_factor
    attn_probs = jnp.exp(scores - log_total)
    grad_probs = jnp.einsum(
        "slhe,smhe->shlm", grad_heads, value_heads, preferred_element_type=jnp.float32
    )
    row_dot = jnp.sum(attn_probs * grad_probs, axis=-1, keepdims=True)
    grad_scores = (attn_probs * (grad_probs - row_dot)).astype(jnp.bfloat16)
    value_terms = jnp.einsum(
        "shlm,slhe->smhe",
        attn_probs.astype(jnp.bfloat16),
        grad_heads,
        preferred_element_type=jnp.float32,
    )
    key_terms = (
        jnp.einsum("shlm,slhe->smhe", grad_scores, query_heads, preferred_element_type=jnp.float32)
        * scale_factor
    )
    key_grad, value_grad = (
        lax.psum_scatter(
            key_terms.reshape(slot_count, key_count, width_local).astype(jnp.bfloat16),
            "ctx",
            scatter_dimension=1,
            tiled=True,
        ).astype(jnp.float32),
        lax.psum_scatter(
            value_terms.reshape(slot_count, key_count, width_local).astype(jnp.bfloat16),
            "ctx",
            scatter_dimension=1,
            tiled=True,
        ).astype(jnp.float32),
    )
    rel_grad = pick_back(grad_scores.astype(jnp.float32) * scale_factor)[0]
    query_grad = (
        jnp.einsum("shlm,smhe->slhe", grad_scores, key_heads, preferred_element_type=jnp.float32)
        * scale_factor
    )
    query_grad = query_grad + jnp.einsum(
        "shlr,re->slhe", rel_grad, rel_table.astype(jnp.float32), precision=lax.Precision.HIGHEST
    )
    table_grad = jnp.einsum(
        "shlr,slhe->re", rel_grad, query_heads.astype(jnp.float32), precision=lax.Precision.HIGHEST
    )
    query_low = query_grad.reshape(slot_count, row_count, width_local).astype(jnp.bfloat16)
    key_low = key_grad.astype(jnp.bfloat16)
    value_low = value_grad.astype(jnp.bfloat16)
    query_bias_grad = jnp.sum(query_low.astype(jnp.float32), axis=(0, 1))
    value_bias_grad = jnp.sum(value_low.astype(jnp.float32), axis=(0, 1))
    query_w_grad = weight_sum(wide_rows, query_low)
    key_w_grad = weight_sum(wide_rows, key_low)
    value_w_grad = weight_sum(wide_rows, value_low)
    grad_normed = narrow_grad(
        rows_out(query_low, query_w) + rows_out(key_low, key_w) + rows_out(value_low, value_w)
    )
    grad_in, gain_grad, shift_grad = norm_backward(grad_normed, standard, inverse, norm_gain)
    return (
        grad_stream + grad_in,
        (
            gain_grad,
            shift_grad,
            query_w_grad,
            query_bias_grad,
            key_w_grad,
            value_w_grad,
            value_bias_grad,
            out_grad,
            out_bias_grad,
            table_grad,
        ),
    )


def conv_forward(stream, norm_gain, norm_shift, weights, depth_local, inner_gain, inner_offset):
    value_w, gate_w, out_w = weights
    normed, standard, inverse = norm_forward(stream, norm_gain, norm_shift)
    wide_rows = widen(normed)
    part_value = rows_in(wide_rows, value_w)
    part_gate = rows_in(wide_rows, gate_w)
    gated_rows = (part_value * jax.nn.sigmoid(part_gate)).astype(jnp.bfloat16)
    row_count = gated_rows.shape[1]
    reach_rows = depth_local.shape[0] - 1
    halo_rows = from_behind(gated_rows[:, row_count - reach_rows :, :], "ctx", 1)
    padded = jnp.concatenate([halo_rows, gated_rows], axis=1)
    padded_float = padded.astype(jnp.float32)
    convolved = depth_local[0] * padded_float[:, 0:row_count, :]
    for tap_index in range(1, depth_local.shape[0]):
        convolved = (
            convolved
            + depth_local[tap_index] * padded_float[:, tap_index : tap_index + row_count, :]
        )
    row_sums = lax.psum(
        (jnp.sum(convolved, axis=-1), jnp.sum(convolved * convolved, axis=-1)), "tp"
    )
    row_mean = (row_sums[0] / D)[..., None]
    row_var = (row_sums[1] / D)[..., None] - row_mean * row_mean
    inner_inverse = lax.rsqrt(row_var + epsilon)
    inner_standard = (convolved - row_mean) * inner_inverse
    inner_pre = inner_standard * inner_gain + inner_offset
    active = jax.nn.silu(inner_pre).astype(jnp.bfloat16)
    branch = narrow(rows_out(active, out_w))
    return (
        stream + branch,
        (
            standard,
            inverse,
            wide_rows,
            part_value,
            part_gate,
            padded,
            inner_standard,
            inner_inverse,
            inner_pre,
        ),
    )


def conv_backward(grad_stream, saved, norm_gain, weights, depth_local, inner_gain):
    value_w, gate_w, out_w = weights
    (
        standard,
        inverse,
        wide_rows,
        part_value,
        part_gate,
        padded,
        inner_standard,
        inner_inverse,
        inner_pre,
    ) = saved
    grad_branch = grad_stream.astype(jnp.bfloat16)
    wide_grad = widen_grad(grad_branch)
    active = jax.nn.silu(inner_pre).astype(jnp.bfloat16)
    out_grad = weight_sum(wide_grad, active)
    grad_inner = rows_in(wide_grad, out_w) * silu_slope(inner_pre)
    inner_gain_grad = jnp.sum(grad_inner * inner_standard, axis=(0, 1))
    inner_shift_grad = jnp.sum(grad_inner, axis=(0, 1))
    grad_standard = grad_inner * inner_gain
    row_sums = lax.psum(
        (jnp.sum(grad_standard, axis=-1), jnp.sum(grad_standard * inner_standard, axis=-1)), "tp"
    )
    grad_conv = inner_inverse * (
        grad_standard - (row_sums[0] / D)[..., None] - inner_standard * (row_sums[1] / D)[..., None]
    )
    row_count = grad_conv.shape[1]
    tap_count = depth_local.shape[0]
    reach_rows = tap_count - 1
    padded_float = padded.astype(jnp.float32)
    depth_grad = jnp.stack(
        [
            jnp.sum(grad_conv * padded_float[:, tap_index : tap_index + row_count, :], axis=(0, 1))
            for tap_index in range(tap_count)
        ]
    )
    grad_padded = jnp.zeros(padded.shape, jnp.float32)
    for tap_index in range(tap_count):
        grad_padded = grad_padded.at[:, tap_index : tap_index + row_count, :].add(
            depth_local[tap_index] * grad_conv
        )
    back_halo = from_behind(grad_padded[:, :reach_rows, :].astype(jnp.bfloat16), "ctx", -1).astype(
        jnp.float32
    )
    grad_gated = grad_padded[:, reach_rows:, :] + jnp.pad(
        back_halo, ((0, 0), (row_count - reach_rows, 0), (0, 0))
    )
    gate_sig = jax.nn.sigmoid(part_gate)
    grad_value = (grad_gated * gate_sig).astype(jnp.bfloat16)
    grad_gate = (grad_gated * part_value * gate_sig * (1.0 - gate_sig)).astype(jnp.bfloat16)
    value_w_grad = weight_sum(wide_rows, grad_value)
    gate_w_grad = weight_sum(wide_rows, grad_gate)
    grad_normed = narrow_grad(rows_out(grad_value, value_w) + rows_out(grad_gate, gate_w))
    grad_in, gain_grad, shift_grad = norm_backward(grad_normed, standard, inverse, norm_gain)
    return (
        grad_stream + grad_in,
        (
            gain_grad,
            shift_grad,
            value_w_grad,
            gate_w_grad,
            depth_grad,
            inner_gain_grad,
            inner_shift_grad,
            out_grad,
        ),
    )


def body(
    inputs,
    teacher,
    clips_dev,
    ffn1_gain,
    ffn1_shift,
    ffn1_in,
    ffn1_in_bias,
    ffn1_out,
    ffn1_out_bias,
    attn_gain,
    attn_shift,
    query_weight,
    query_bias,
    key_weight,
    value_weight,
    value_bias,
    attn_out_weight,
    attn_out_bias,
    rel_table,
    conv_gain,
    conv_shift,
    conv_value_weight,
    conv_gate_weight,
    conv_depth,
    conv_inner_gain,
    conv_inner_shift,
    conv_out_weight,
    ffn2_gain,
    ffn2_shift,
    ffn2_in,
    ffn2_in_bias,
    ffn2_out,
    ffn2_out_bias,
    final_gain,
    final_shift,
):
    gathered = (
        lax.all_gather(ffn1_in, ("fsdp", "ctx"), axis=0, tiled=True),
        lax.all_gather(ffn1_out, ("fsdp", "ctx"), axis=0, tiled=True),
        lax.all_gather(query_weight, ("fsdp", "ctx"), axis=0, tiled=True),
        lax.all_gather(key_weight, ("fsdp", "ctx"), axis=0, tiled=True),
        lax.all_gather(value_weight, ("fsdp", "ctx"), axis=0, tiled=True),
        lax.all_gather(attn_out_weight, ("fsdp", "ctx"), axis=0, tiled=True),
        lax.all_gather(conv_value_weight, ("fsdp", "ctx"), axis=0, tiled=True),
        lax.all_gather(conv_gate_weight, ("fsdp", "ctx"), axis=0, tiled=True),
        lax.all_gather(conv_out_weight, ("fsdp", "ctx"), axis=0, tiled=True),
        lax.all_gather(ffn2_in, ("fsdp", "ctx"), axis=0, tiled=True),
        lax.all_gather(ffn2_out, ("fsdp", "ctx"), axis=0, tiled=True),
    )
    tp_rank = lax.axis_index("tp")
    ctx_rank = lax.axis_index("ctx")
    hidden_local = gathered[0].shape[1]
    width_local = gathered[2].shape[1]
    ffn1_bias_local = local_cut(ffn1_in_bias, tp_rank, hidden_local)
    ffn2_bias_local = local_cut(ffn2_in_bias, tp_rank, hidden_local)
    query_bias_local = local_cut(query_bias, tp_rank, width_local)
    value_bias_local = local_cut(value_bias, tp_rank, width_local)
    depth_local = local_cut(conv_depth, tp_rank, width_local)
    inner_gain_local = local_cut(conv_inner_gain, tp_rank, width_local)
    inner_shift_local = local_cut(conv_inner_shift, tp_rank, width_local)
    stream_zero = inputs.astype(jnp.float32)
    stream_one, saved_one = ffn_forward(
        stream_zero, ffn1_gain, ffn1_shift, gathered[0], ffn1_bias_local, gathered[1], ffn1_out_bias
    )
    stream_two, saved_two = attn_forward(
        stream_one,
        attn_gain,
        attn_shift,
        (gathered[2], gathered[3], gathered[4], gathered[5]),
        (query_bias_local, value_bias_local, attn_out_bias),
        rel_table,
        ctx_rank,
    )
    stream_three, saved_three = conv_forward(
        stream_two,
        conv_gain,
        conv_shift,
        (gathered[6], gathered[7], gathered[8]),
        depth_local,
        inner_gain_local,
        inner_shift_local,
    )
    stream_four, saved_four = ffn_forward(
        stream_three,
        ffn2_gain,
        ffn2_shift,
        gathered[9],
        ffn2_bias_local,
        gathered[10],
        ffn2_out_bias,
    )
    final_out, final_standard, final_inverse = norm_forward(stream_four, final_gain, final_shift)
    live_slots = (
        jnp.arange(final_out.shape[0], dtype=jnp.int32) < clips_dev[lax.axis_index("fsdp")]
    ).astype(jnp.float32)
    misfit = (final_out - teacher.astype(jnp.float32)) * live_slots[:, None, None]
    sse_local = jnp.sum(misfit * misfit)
    gradient_fourth, final_gain_grad, final_shift_grad = norm_backward(
        2.0 * misfit, final_standard, final_inverse, final_gain
    )
    back_weights = (
        lax.all_gather(ffn1_in, ("fsdp", "ctx"), axis=0, tiled=True),
        lax.all_gather(ffn1_out, ("fsdp", "ctx"), axis=0, tiled=True),
        lax.all_gather(query_weight, ("fsdp", "ctx"), axis=0, tiled=True),
        lax.all_gather(key_weight, ("fsdp", "ctx"), axis=0, tiled=True),
        lax.all_gather(value_weight, ("fsdp", "ctx"), axis=0, tiled=True),
        lax.all_gather(attn_out_weight, ("fsdp", "ctx"), axis=0, tiled=True),
        lax.all_gather(conv_value_weight, ("fsdp", "ctx"), axis=0, tiled=True),
        lax.all_gather(conv_gate_weight, ("fsdp", "ctx"), axis=0, tiled=True),
        lax.all_gather(conv_out_weight, ("fsdp", "ctx"), axis=0, tiled=True),
        lax.all_gather(ffn2_in, ("fsdp", "ctx"), axis=0, tiled=True),
        lax.all_gather(ffn2_out, ("fsdp", "ctx"), axis=0, tiled=True),
    )
    grad_three, ffn2_grads = ffn_backward(
        gradient_fourth, saved_four, ffn2_gain, back_weights[9], back_weights[10]
    )
    grad_two, conv_grads = conv_backward(
        grad_three,
        saved_three,
        conv_gain,
        (back_weights[6], back_weights[7], back_weights[8]),
        depth_local,
        inner_gain_local,
    )
    grad_one, attn_grads = attn_backward(
        grad_two,
        saved_two,
        attn_gain,
        (back_weights[2], back_weights[3], back_weights[4], back_weights[5]),
        rel_table,
        ctx_rank,
    )
    grad_zero, ffn1_grads = ffn_backward(
        grad_one, saved_one, ffn1_gain, back_weights[0], back_weights[1]
    )
    weight_parts = (
        lax.psum_scatter(ffn1_grads[2], ("fsdp", "ctx"), scatter_dimension=0, tiled=True),
        lax.psum_scatter(ffn1_grads[4], ("fsdp", "ctx"), scatter_dimension=0, tiled=True),
        lax.psum_scatter(attn_grads[2], ("fsdp", "ctx"), scatter_dimension=0, tiled=True),
        lax.psum_scatter(attn_grads[4], ("fsdp", "ctx"), scatter_dimension=0, tiled=True),
        lax.psum_scatter(attn_grads[5], ("fsdp", "ctx"), scatter_dimension=0, tiled=True),
        lax.psum_scatter(attn_grads[7], ("fsdp", "ctx"), scatter_dimension=0, tiled=True),
        lax.psum_scatter(conv_grads[2], ("fsdp", "ctx"), scatter_dimension=0, tiled=True),
        lax.psum_scatter(conv_grads[3], ("fsdp", "ctx"), scatter_dimension=0, tiled=True),
        lax.psum_scatter(conv_grads[7], ("fsdp", "ctx"), scatter_dimension=0, tiled=True),
        lax.psum_scatter(ffn2_grads[2], ("fsdp", "ctx"), scatter_dimension=0, tiled=True),
        lax.psum_scatter(ffn2_grads[4], ("fsdp", "ctx"), scatter_dimension=0, tiled=True),
    )
    full_hidden = ffn1_in_bias.shape[0]
    full_width = query_bias.shape[0]
    shared = lax.psum(
        (
            ffn1_grads[0],
            ffn1_grads[1],
            local_put(ffn1_grads[3], tp_rank, full_hidden),
            ffn1_grads[5],
            attn_grads[0],
            attn_grads[1],
            local_put(attn_grads[3], tp_rank, full_width),
            local_put(attn_grads[6], tp_rank, full_width),
            attn_grads[8],
            attn_grads[9],
            conv_grads[0],
            conv_grads[1],
            local_put(conv_grads[4], tp_rank, full_width),
            local_put(conv_grads[5], tp_rank, full_width),
            local_put(conv_grads[6], tp_rank, full_width),
            ffn2_grads[0],
            ffn2_grads[1],
            local_put(ffn2_grads[3], tp_rank, full_hidden),
            ffn2_grads[5],
            final_gain_grad,
            final_shift_grad,
            sse_local,
        ),
        ("fsdp", "ctx", "tp"),
    )
    token_count = (jnp.sum(clips_dev) * SEQ).astype(jnp.float32)
    loss = shared[21] / token_count
    return (
        final_out.astype(jnp.bfloat16),
        loss,
        grad_zero,
        shared[0],
        shared[1],
        weight_parts[0],
        shared[2],
        weight_parts[1],
        shared[3],
        shared[4],
        shared[5],
        weight_parts[2],
        shared[6],
        weight_parts[3],
        weight_parts[4],
        shared[7],
        weight_parts[5],
        shared[8],
        shared[9],
        shared[10],
        shared[11],
        weight_parts[6],
        weight_parts[7],
        shared[12],
        shared[13],
        shared[14],
        weight_parts[8],
        shared[15],
        shared[16],
        weight_parts[9],
        shared[17],
        weight_parts[10],
        shared[18],
        shared[19],
        shared[20],
    )


def solution(mesh):
    in_specs = (
        P("fsdp", ("ctx", "tp"), None),
        P("fsdp", ("ctx", "tp"), None),
        P(),
        P(),
        P(),
        P(("fsdp", "ctx"), "tp"),
        P(),
        P(("fsdp", "ctx"), "tp"),
        P(),
        P(),
        P(),
        P(("fsdp", "ctx"), "tp"),
        P(),
        P(("fsdp", "ctx"), "tp"),
        P(("fsdp", "ctx"), "tp"),
        P(),
        P(("fsdp", "ctx"), "tp"),
        P(),
        P(),
        P(),
        P(),
        P(("fsdp", "ctx"), "tp"),
        P(("fsdp", "ctx"), "tp"),
        P(),
        P(),
        P(),
        P(("fsdp", "ctx"), "tp"),
        P(),
        P(),
        P(("fsdp", "ctx"), "tp"),
        P(),
        P(("fsdp", "ctx"), "tp"),
        P(),
        P(),
        P(),
    )
    out_specs = (
        P("fsdp", ("ctx", "tp"), None),
        P(),
        P("fsdp", ("ctx", "tp"), None),
        P(),
        P(),
        P(("fsdp", "ctx"), "tp"),
        P(),
        P(("fsdp", "ctx"), "tp"),
        P(),
        P(),
        P(),
        P(("fsdp", "ctx"), "tp"),
        P(),
        P(("fsdp", "ctx"), "tp"),
        P(("fsdp", "ctx"), "tp"),
        P(),
        P(("fsdp", "ctx"), "tp"),
        P(),
        P(),
        P(),
        P(),
        P(("fsdp", "ctx"), "tp"),
        P(("fsdp", "ctx"), "tp"),
        P(),
        P(),
        P(),
        P(("fsdp", "ctx"), "tp"),
        P(),
        P(),
        P(("fsdp", "ctx"), "tp"),
        P(),
        P(("fsdp", "ctx"), "tp"),
        P(),
        P(),
        P(),
    )
    return jax.shard_map(body, mesh=mesh, in_specs=in_specs, out_specs=out_specs, check_vma=False)
```

profile of v0, /device:TPU:0, one launch (start us, length us, event | category | flops | bytes accessed | tf_op | source)
XLA Modules:
  0.0 2624.6 jit_solution(7400003995590315496)
XLA Ops:
  14.0 50.6 %all-gather.15.cloned.1.call-done = bf16[3,384,1024]{2,1,0:T(8,128)(2,1)} async-done(((bf16[3,96,1024]{2,1,0:T(8,128)(2,1)}), bf16[3,384,1024]{2,1,0:T(8,128)(2,1)}) %all-gather.15.cloned.1.call-update) | async-done | bytes 2359312 | tf_op jit(solution)/shard_map/all_gather | solution.py:56
  130.0 47.8 %reduce-scatter.22.cloned.1.call-done = bf16[3,96,1024]{2,1,0:T(8,128)(2,1)} async-done(((bf16[3,384,1024]{2,1,0:T(8,128)(2,1)}), bf16[3,96,1024]{2,1,0:T(8,128)(2,1)}) %reduce-scatter.22.cloned.1.call-update) | async-done | bytes 589840 | tf_op jit(solution)/shard_map/reduce_scatter | solution.py:60
  300.2 70.2 %concatenate.69 = f32[3,4,384,3529]{3,2,1,0:T(8,128)} concatenate(f32[3,4,384,1536]{3,2,1,0:T(8,128)} %broadcast_in_dim.17, f32[3,4,384,73]{3,2,1,0:T(8,128)S(1)} %copy.89, f32[3,4,384,1920]{3,2,1,0:T(8,128)} %broadcast_in_dim.19), dimensions={3} | concatenate | bytes 130093056 | tf_op jit(solution)/shard_map/concatenate | solution.py:97
  400.2 42.5 %reshape.1157 = f32[3,4,737280]{2,1,0:T(4,128)} reshape(f32[3,4,384,1920]{3,2,1,0:T(8,128)} %constant_dynamic-slice_fusion.1) | data formatting | bytes 70778880 | tf_op jit(solution)/shard_map/reshape | solution.py:100
  467.1 81.2 %reshape.1158 = f32[3,4,384,1919]{3,2,1,0:T(8,128)} reshape(f32[3,4,736896]{2,1,0:T(4,128)} %slice.1113) | data formatting | bytes 70742016 | tf_op jit(solution)/shard_map/reshape | solution.py:102
  605.1 46.0 %reduce-scatter.24.cloned.1.call-done = bf16[3,96,1024]{2,1,0:T(8,128)(2,1)} async-done(((bf16[3,384,1024]{2,1,0:T(8,128)(2,1)}), bf16[3,96,1024]{2,1,0:T(8,128)(2,1)}) %reduce-scatter.24.cloned.1.call-update) | async-done | bytes 589840 | tf_op jit(solution)/shard_map/reduce_scatter | solution.py:60
  738.7 45.8 %reduce-scatter.26.cloned.1.call-done = bf16[3,96,1024]{2,1,0:T(8,128)(2,1)} async-done(((bf16[3,384,1024]{2,1,0:T(8,128)(2,1)}), bf16[3,96,1024]{2,1,0:T(8,128)(2,1)}) %reduce-scatter.26.cloned.1.call-update) | async-done | bytes 589840 | tf_op jit(solution)/shard_map/reduce_scatter | solution.py:60
  813.6 52.0 %all-gather.29.cloned.1.call-done = bf16[3,384,1024]{2,1,0:T(8,128)(2,1)} async-done(((bf16[3,96,1024]{2,1,0:T(8,128)(2,1)}), bf16[3,384,1024]{2,1,0:T(8,128)(2,1)}) %all-gather.29.cloned.1.call-update) | async-done | bytes 2359312 | tf_op jit(solution)/shard_map/all_gather | solution.py:56
  903.1 46.0 %reduce-scatter.28.cloned.1.call-done = bf16[3,96,1024]{2,1,0:T(8,128)(2,1)} async-done(((bf16[3,384,1024]{2,1,0:T(8,128)(2,1)}), bf16[3,96,1024]{2,1,0:T(8,128)(2,1)}) %reduce-scatter.28.cloned.1.call-update) | async-done | bytes 589840 | tf_op jit(solution)/shard_map/reduce_scatter | solution.py:60
  955.9 49.2 %all-gather.35.cloned.1.call-done = bf16[3,384,1024]{2,1,0:T(8,128)(2,1)} async-done(((bf16[3,96,1024]{2,1,0:T(8,128)(2,1)}), bf16[3,384,1024]{2,1,0:T(8,128)(2,1)}) %all-gather.35.cloned.1.call-update) | async-done | bytes 2359312 | tf_op jit(solution)/shard_map/all_gather | solution.py:66
  1018.7 46.6 %reduce-scatter.30.cloned.1.call-done = bf16[3,96,1024]{2,1,0:T(8,128)(2,1)} async-done(((bf16[3,384,1024]{2,1,0:T(8,128)(2,1)}), bf16[3,96,1024]{2,1,0:T(8,128)(2,1)}) %reduce-scatter.30.cloned.1.call-update) | async-done | bytes 589840 | tf_op jit(solution)/shard_map/reduce_scatter | solution.py:70
  1069.8 49.5 %all-gather.37.cloned.1.call-done = bf16[3,384,1024]{2,1,0:T(8,128)(2,1)} async-done(((bf16[3,96,1024]{2,1,0:T(8,128)(2,1)}), bf16[3,384,1024]{2,1,0:T(8,128)(2,1)}) %all-gather.37.cloned.1.call-update) | async-done | bytes 2359312 | tf_op jit(solution)/shard_map/all_gather | solution.py:66
  1356.6 46.6 %reduce-scatter.32.cloned.1.call-done = bf16[3,96,1024]{2,1,0:T(8,128)(2,1)} async-done(((bf16[3,384,1024]{2,1,0:T(8,128)(2,1)}), bf16[3,96,1024]{2,1,0:T(8,128)(2,1)}) %reduce-scatter.32.cloned.1.call-update) | async-done | bytes 589840 | tf_op jit(solution)/shard_map/reduce_scatter | solution.py:70
  1410.1 49.4 %all-gather.39.cloned.1.call-done = bf16[3,384,1024]{2,1,0:T(8,128)(2,1)} async-done(((bf16[3,96,1024]{2,1,0:T(8,128)(2,1)}), bf16[3,384,1024]{2,1,0:T(8,128)(2,1)}) %all-gather.39.cloned.1.call-update) | async-done | bytes 2359312 | tf_op jit(solution)/shard_map/all_gather | solution.py:66
  1559.1 61.2 %reshape.1161 = f32[3,4,736896]{2,1,0:T(4,128)} reshape(f32[3,4,384,1919]{3,2,1,0:T(8,128)} %pad.84) | data formatting | bytes 70742016 | tf_op jit(solution)/shard_map/transpose(jvp())/reshape | solution.py:102
  1644.7 50.2 %reshape.1162 = f32[3,4,384,1920]{3,2,1,0:T(8,128)} reshape(f32[3,4,737280]{2,1,0:T(4,128)} %pad.85) | data formatting | bytes 70778880 | tf_op jit(solution)/shard_map/transpose(jvp())/reshape | solution.py:100
  1694.9 41.3 %copy.92 = f32[3,4,384,1920]{2,1,0,3:T(4,128)} copy(f32[3,4,384,1920]{3,2,1,0:T(8,128)} %reshape.1162) | data formatting | bytes 70778880 | tf_op jit(solution)/shard_map/transpose(jvp())/reshape | solution.py:100
  1828.8 45.9 %reduce-scatter.38.cloned.1.call-done = bf16[3,96,1024]{2,1,0:T(8,128)(2,1)} async-done(((bf16[3,384,1024]{2,1,0:T(8,128)(2,1)}), bf16[3,96,1024]{2,1,0:T(8,128)(2,1)}) %reduce-scatter.38.cloned.1.call-update) | async-done | bytes 589840 | tf_op jit(solution)/shard_map/reduce_scatter | solution.py:70
  1878.4 49.5 %all-gather.41.cloned.1.call-done = bf16[3,384,1024]{2,1,0:T(8,128)(2,1)} async-done(((bf16[3,96,1024]{2,1,0:T(8,128)(2,1)}), bf16[3,384,1024]{2,1,0:T(8,128)(2,1)}) %all-gather.41.cloned.1.call-update) | async-done | bytes 2359312 | tf_op jit(solution)/shard_map/all_gather | solution.py:66
  2008.4 43.6 %all-reduce.13 = (f32[]{:T(128)}, f32[1024]{0:T(1024)}, f32[1024]{0:T(1024)}, f32[4096]{0:T(1024)}, f32[1024]{0:T(1024)}, /*index=5*/f32[1024]{0:T(1024)}, f32[1...) all-reduce(f32[]{:T(128)} %get-tuple-element.444, ...), channel_id=1, replica_groups=mesh['fsdp'=2,'ctx'=4,'tp'=4] {'fsdp','ctx','tp'}, use_global_device_ids=true, to_apply=%region_21.22 | all-reduce | flops 30273 | bytes 242184 | tf_op jit(solution)/shard_map/psum | solution.py:534
  2055.8 42.0 %reduce-scatter.60.cloned.1.call-done = f32[128,1024]{1,0:T(8,128)} async-done(((f32[1024,1024]{1,0:T(8,128)}), f32[128,1024]{1,0:T(8,128)}) %reduce-scatter.60.cloned.1.call-update) | async-done | bytes 524304 | tf_op jit(solution)/shard_map/reduce_scatter | solution.py:529
  2097.7 130.4 %all-reduce.12.cloned.1.call-done = f32[31,1024]{1,0:T(8,128)} async-done(((f32[31,1024]{1,0:T(8,128)}), f32[31,1024]{1,0:T(8,128)}) %all-reduce.12.cloned.1.call-update) | async-done | bytes 126992 | tf_op jit(solution)/shard_map/psum | solution.py:534
  2505.1 55.1 %reduce-scatter.44.cloned.1.call-done = f32[128,1024]{1,0:T(8,128)} async-done(((f32[1024,1024]{1,0:T(8,128)}), f32[128,1024]{1,0:T(8,128)}) %reduce-scatter.44.cloned.1.call-update) | async-done | bytes 524304 | tf_op jit(solution)/shard_map/reduce_scatter | solution.py:521
  2560.2 55.0 %reduce-scatter.42.cloned.1.call-done = f32[128,1024]{1,0:T(8,128)} async-done(((f32[1024,1024]{1,0:T(8,128)}), f32[128,1024]{1,0:T(8,128)}) %reduce-scatter.42.cloned.1.call-update) | async-done | bytes 524304 | tf_op jit(solution)/shard_map/reduce_scatter | solution.py:520
  (650 shorter events, 1308.2 us)
Async XLA Ops:
  12.5 110.3 %all-gather.19.cloned.1.call-start = ((), (), s32[]{:S(2)}) async-start(), calls=%async_computation.23 | async-start | bytes 2359296 | tf_op jit(solution)/shard_map/all_gather | solution.py:422
  13.2 164.6 %reduce-scatter.22.cloned.1.call-start = ((), (), s32[]{:S(2)}) async-start(), calls=%async_computation.24 | async-start | bytes 2949120 | tf_op jit(solution)/shard_map/reduce_scatter | solution.py:60
  181.6 368.4 %all-gather.25.cloned.1.call-start = ((), (), s32[]{:S(2)}) async-start(), calls=%async_computation.27 | async-start | bytes 2949120 | tf_op jit(solution)/shard_map/all_gather | solution.py:150
  234.4 352.2 %all-gather.23.cloned.1.call-start = ((), (), s32[]{:S(2)}) async-start(), calls=%async_computation.26 | async-start | bytes 2949120 | tf_op jit(solution)/shard_map/all_gather | solution.py:151
  654.8 129.8 %reduce-scatter.26.cloned.1.call-start = ((), (), s32[]{:S(2)}) async-start(), calls=%async_computation.30 | async-start | bytes 2949120 | tf_op jit(solution)/shard_map/reduce_scatter | solution.py:60
  738.7 126.9 %all-gather.29.cloned.1.call-start = ((), (), s32[]{:S(2)}) async-start(), calls=%async_computation.31 | async-start | bytes 2949120 | tf_op jit(solution)/shard_map/all_gather | solution.py:56
  788.8 160.3 %reduce-scatter.28.cloned.1.call-start = ((), (), s32[]{:S(2)}) async-start(), calls=%async_computation.34 | async-start | bytes 2949120 | tf_op jit(solution)/shard_map/reduce_scatter | solution.py:60
  1069.8 333.4 %reduce-scatter.32.cloned.1.call-start = ((), (), s32[]{:S(2)}) async-start(), calls=%async_computation.38 | async-start | bytes 2949120 | tf_op jit(solution)/shard_map/reduce_scatter | solution.py:70
  1410.1 408.3 %reduce-scatter.34.cloned.1.call-start = ((), (), s32[]{:S(2)}) async-start(), calls=%async_computation.40 | async-start | bytes 2949120 | tf_op jit(solution)/shard_map/reduce_scatter | solution.py:216
  1520.5 302.0 %reduce-scatter.36.cloned.1.call-start = ((), (), s32[]{:S(2)}) async-start(), calls=%async_computation.41 | async-start | bytes 2949120 | tf_op jit(solution)/shard_map/reduce_scatter | solution.py:222
  1736.2 138.5 %reduce-scatter.38.cloned.1.call-start = ((), (), s32[]{:S(2)}) async-start(), calls=%async_computation.42 | async-start | bytes 2949120 | tf_op jit(solution)/shard_map/reduce_scatter | solution.py:70
  1878.3 128.3 %reduce-scatter.40.cloned.1.call-start = ((), (), s32[]{:S(2)}) async-start(), calls=%async_computation.44 | async-start | bytes 2949120 | tf_op jit(solution)/shard_map/reduce_scatter | solution.py:70
  1940.7 115.0 %reduce-scatter.62.cloned.1.call-start = ((), (), s32[]{:S(2)}) async-start(), calls=%async_computation.56 | async-start | bytes 4718592 | tf_op jit(solution)/shard_map/reduce_scatter | solution.py:530
  1949.4 148.3 %reduce-scatter.60.cloned.1.call-start = ((), (), s32[]{:S(2)}) async-start(), calls=%async_computation.55 | async-start | bytes 4718592 | tf_op jit(solution)/shard_map/reduce_scatter | solution.py:529
  1957.2 271.0 %all-reduce.12.cloned.1.call-start = ((), (), s32[]{:S(2)}) async-start(), calls=%async_computation.53 | async-start | bytes 262144 | tf_op jit(solution)/shard_map/psum | solution.py:534
  1958.6 308.3 %reduce-scatter.58.cloned.1.call-start = ((), (), s32[]{:S(2)}) async-start(), calls=%async_computation.54 | async-start | bytes 1179648 | tf_op jit(solution)/shard_map/reduce_scatter | solution.py:528
  1963.1 343.6 %reduce-scatter.54.cloned.1.call-start = ((), (), s32[]{:S(2)}) async-start(), calls=%async_computation.51 | async-start | bytes 1179648 | tf_op jit(solution)/shard_map/reduce_scatter | solution.py:526
  1966.8 379.4 %reduce-scatter.56.cloned.1.call-start = ((), (), s32[]{:S(2)}) async-start(), calls=%async_computation.52 | async-start | bytes 1179648 | tf_op jit(solution)/shard_map/reduce_scatter | solution.py:527
  1970.4 415.6 %reduce-scatter.52.cloned.1.call-start = ((), (), s32[]{:S(2)}) async-start(), calls=%async_computation.50 | async-start | bytes 1179648 | tf_op jit(solution)/shard_map/reduce_scatter | solution.py:525
  1974.2 451.6 %reduce-scatter.46.cloned.1.call-start = ((), (), s32[]{:S(2)}) async-start(), calls=%async_computation.47 | async-start | bytes 1179648 | tf_op jit(solution)/shard_map/reduce_scatter | solution.py:522
  1978.0 487.4 %reduce-scatter.50.cloned.1.call-start = ((), (), s32[]{:S(2)}) async-start(), calls=%async_computation.49 | async-start | bytes 1179648 | tf_op jit(solution)/shard_map/reduce_scatter | solution.py:524
  1982.0 523.1 %reduce-scatter.48.cloned.1.call-start = ((), (), s32[]{:S(2)}) async-start(), calls=%async_computation.48 | async-start | bytes 1179648 | tf_op jit(solution)/shard_map/reduce_scatter | solution.py:523
  1985.7 574.5 %reduce-scatter.44.cloned.1.call-start = ((), (), s32[]{:S(2)}) async-start(), calls=%async_computation.46 | async-start | bytes 4718592 | tf_op jit(solution)/shard_map/reduce_scatter | solution.py:521
  1994.0 621.2 %reduce-scatter.42.cloned.1.call-start = ((), (), s32[]{:S(2)}) async-start(), calls=%async_computation.45 | async-start | bytes 4718592 | tf_op jit(solution)/shard_map/reduce_scatter | solution.py:520
  (185 other events, 7335.9 us)
Sparse Core Ops, SparseCore 0:
  11.8 52.6 all-gather.14
  130.0 47.6 reduce-scatter.21
  181.8 49.3 all-gather.20
  605.1 45.9 reduce-scatter.23
  654.9 49.3 all-gather.26
  738.1 46.4 reduce-scatter.25
  815.6 49.9 all-gather.28
  901.3 47.6 reduce-scatter.27
  955.8 49.3 all-gather.34
  1018.8 46.4 reduce-scatter.29
  1069.9 49.3 all-gather.36
  1356.6 46.4 reduce-scatter.31
  1410.2 49.3 all-gather.38
  1828.9 45.7 reduce-scatter.37
  1878.4 49.3 all-gather.40
  1940.9 46.4 reduce-scatter.39
  1991.3 51.4 reduce-scatter.61
  2046.6 51.0 reduce-scatter.59
  2103.7 124.4 all-reduce.11
  2270.7 35.9 reduce-scatter.53
  2429.4 35.9 reduce-scatter.49
  2469.1 35.9 reduce-scatter.47
  2509.1 51.1 reduce-scatter.43
  2564.0 51.1 reduce-scatter.41
  (12 shorter events, 360.4 us)
where the time goes:
time: 2640 us; the launch traced here: 2620 us
  waiting for transfers between devices  1350 us (51%)
  local copies, waits for them, and re-layouts  684 us (26%)
  matrix products  233 us (9%)
  other arithmetic  188 us (7%)
  blocking collectives  150 us (6%)
    all_gather x4, waiting for transfers between devices, widen_grad(): return lax.all_gather(grad_branch, 'tp', axis=1, tiled=True)  198 us
    reduce_scatter x4, waiting for transfers between devices, narrow(): lax.psum_scatter(partial_rows.astype(jnp.bfloat16), 'tp', scatter_dimensi...  186 us
    all_gather x4, waiting for transfers between devices, widen(): return lax.all_gather(normed.astype(jnp.bfloat16), 'tp', axis=1, tiled=True)  162 us
    reshape x2, local copies, waits for them, and re-layouts, band_bias(): return sheared.reshape(lead[:2] + (row_count, extent - 1))[..., :key_count]  142 us
    reduce_scatter x4, waiting for transfers between devices, narrow_grad(): lax.psum_scatter(partial_rows.astype(jnp.bfloat16), 'tp', scatter_dimensi...  139 us
    reshape x3, local copies, waits for them, and re-layouts, band_bias(): flat = skewed.reshape(lead[:2] + (row_count * extent,))  134 us
    psum x1, waiting for transfers between devices, body(): lax.psum((ffn1_grads[0], ffn1_grads[1], local_put(ffn1_grads[3], tp_rank,...  130 us
    scatter-add x27, local copies, waits for them, and re-layouts, conv_backward(): grad_padded.at[:, tap_index:tap_index + row_count, :]  126 us
  transfers between devices with their start and end apart: 38, of which 31 were waited for; matrix products, arithmetic and copies ran while one was open for 27% of the time, Pallas kernels for 0%

commit v1 on v0

--- a/solution.py
+++ b/solution.py
@@ -377,6 +377,54 @@
             inner_shift_grad,
             out_grad,
         ),
+    )
+
+
+def gather_rows(shard):
+    return lax.all_gather(shard, ("fsdp", "ctx"), axis=0, tiled=True)
+
+
+def scatter_sum(*grads):
+    joined = jnp.concatenate([grad.astype(jnp.bfloat16) for grad in grads], axis=1)
+    part = lax.psum_scatter(joined, ("fsdp", "ctx"), scatter_dimension=0, tiled=True)
+    pieces = []
+    start = 0
+    for grad in grads:
+        pieces.append(part[:, start : start + grad.shape[1]].astype(jnp.float32))
+        start += grad.shape[1]
+    return tuple(pieces)
+
+
+def sum_small(whole_parts, split_parts, tp_rank):
+    tp_count = lax.axis_size("tp")
+    split = jnp.concatenate([part.reshape(-1) for part in split_parts])
+    spread = lax.dynamic_update_slice(
+        jnp.zeros((tp_count, split.shape[0]), jnp.float32), split[None], (tp_rank, 0)
+    )
+    flat = jnp.concatenate([part.reshape(-1) for part in whole_parts] + [spread.reshape(-1)])
+    count = flat.shape[0]
+    flat = jnp.pad(flat, (0, -count % 1024)).reshape(-1, 128)
+    total = lax.psum(flat, ("fsdp", "ctx", "tp")).reshape(-1)
+    whole = []
+    start = 0
+    for part in whole_parts:
+        whole.append(total[start : start + part.size].reshape(part.shape))
+        start += part.size
+    spread = total[start : start + tp_count * split.shape[0]].reshape(tp_count, -1)
+    pieces = []
+    start = 0
+    for part in split_parts:
+        piece = spread[:, start : start + part.size]
+        if part.ndim == 1:
+            pieces.append(piece.reshape(-1))
+        else:
+            piece = piece.reshape((tp_count,) + part.shape)
+            pieces.append(piece.transpose(1, 0, 2).reshape(part.shape[0], -1))
+        start += part.size
+    w, p = whole, pieces
+    return (
+        w[0], w[1], p[0], w[2], w[3], w[4], p[1], p[2], w[5], w[6], w[7], w[8],
+        p[3], p[4], p[5], w[9], w[10], p[6], w[11], w[12], w[13], w[14],
     )
 
 
@@ -417,18 +465,29 @@
     final_gain,
     final_shift,
 ):
+    ffn1_in_all = gather_rows(ffn1_in)
+    ffn1_out_all = gather_rows(ffn1_out)
+    attn_all = gather_rows(
+        jnp.concatenate([query_weight, key_weight, value_weight, attn_out_weight], axis=1)
+    )
+    conv_all = gather_rows(
+        jnp.concatenate([conv_value_weight, conv_gate_weight, conv_out_weight], axis=1)
+    )
+    ffn2_in_all = gather_rows(ffn2_in)
+    ffn2_out_all = gather_rows(ffn2_out)
+    width = query_weight.shape[1]
     gathered = (
-        lax.all_gather(ffn1_in, ("fsdp", "ctx"), axis=0, tiled=True),
-        lax.all_gather(ffn1_out, ("fsdp", "ctx"), axis=0, tiled=True),
-        lax.all_gather(query_weight, ("fsdp", "ctx"), axis=0, tiled=True),
-        lax.all_gather(key_weight, ("fsdp", "ctx"), axis=0, tiled=True),
-        lax.all_gather(value_weight, ("fsdp", "ctx"), axis=0, tiled=True),
-        lax.all_gather(attn_out_weight, ("fsdp", "ctx"), axis=0, tiled=True),
-        lax.all_gather(conv_value_weight, ("fsdp", "ctx"), axis=0, tiled=True),
-        lax.all_gather(conv_gate_weight, ("fsdp", "ctx"), axis=0, tiled=True),
-        lax.all_gather(conv_out_weight, ("fsdp", "ctx"), axis=0, tiled=True),
-        lax.all_gather(ffn2_in, ("fsdp", "ctx"), axis=0, tiled=True),
-        lax.all_gather(ffn2_out, ("fsdp", "ctx"), axis=0, tiled=True),
+        ffn1_in_all,
+        ffn1_out_all,
+        attn_all[:, :width],
+        attn_all[:, width : 2 * width],
+        attn_all[:, 2 * width : 3 * width],
+        attn_all[:, 3 * width :],
+        conv_all[:, :width],
+        conv_all[:, width : 2 * width],
+        conv_all[:, 2 * width :],
+        ffn2_in_all,
+        ffn2_out_all,
     )
     tp_rank = lax.axis_index("tp")
     ctx_rank = lax.axis_index("ctx")
@@ -481,19 +540,7 @@
     gradient_fourth, final_gain_grad, final_shift_grad = norm_backward(
         2.0 * misfit, final_standard, final_inverse, final_gain
     )
-    back_weights = (
-        lax.all_gather(ffn1_in, ("fsdp", "ctx"), axis=0, tiled=True),
-        lax.all_gather(ffn1_out, ("fsdp", "ctx"), axis=0, tiled=True),
-        lax.all_gather(query_weight, ("fsdp", "ctx"), axis=0, tiled=True),
-        lax.all_gather(key_weight, ("fsdp", "ctx"), axis=0, tiled=True),
-        lax.all_gather(value_weight, ("fsdp", "ctx"), axis=0, tiled=True),
-        lax.all_gather(attn_out_weight, ("fsdp", "ctx"), axis=0, tiled=True),
-        lax.all_gather(conv_value_weight, ("fsdp", "ctx"), axis=0, tiled=True),
-        lax.all_gather(conv_gate_weight, ("fsdp", "ctx"), axis=0, tiled=True),
-        lax.all_gather(conv_out_weight, ("fsdp", "ctx"), axis=0, tiled=True),
-        lax.all_gather(ffn2_in, ("fsdp", "ctx"), axis=0, tiled=True),
-        lax.all_gather(ffn2_out, ("fsdp", "ctx"), axis=0, tiled=True),
-    )
+    back_weights = gathered
     grad_three, ffn2_grads = ffn_backward(
         gradient_fourth, saved_four, ffn2_gain, back_weights[9], back_weights[10]
     )
@@ -516,47 +563,39 @@
     grad_zero, ffn1_grads = ffn_backward(
         grad_one, saved_one, ffn1_gain, back_weights[0], back_weights[1]
     )
-    weight_parts = (
-        lax.psum_scatter(ffn1_grads[2], ("fsdp", "ctx"), scatter_dimension=0, tiled=True),
-        lax.psum_scatter(ffn1_grads[4], ("fsdp", "ctx"), scatter_dimension=0, tiled=True),
-        lax.psum_scatter(attn_grads[2], ("fsdp", "ctx"), scatter_dimension=0, tiled=True),
-        lax.psum_scatter(attn_grads[4], ("fsdp", "ctx"), scatter_dimension=0, tiled=True),
-        lax.psum_scatter(attn_grads[5], ("fsdp", "ctx"), scatter_dimension=0, tiled=True),
-        lax.psum_scatter(attn_grads[7], ("fsdp", "ctx"), scatter_dimension=0, tiled=True),
-        lax.psum_scatter(conv_grads[2], ("fsdp", "ctx"), scatter_dimension=0, tiled=True),
-        lax.psum_scatter(conv_grads[3], ("fsdp", "ctx"), scatter_dimension=0, tiled=True),
-        lax.psum_scatter(conv_grads[7], ("fsdp", "ctx"), scatter_dimension=0, tiled=True),
-        lax.psum_scatter(ffn2_grads[2], ("fsdp", "ctx"), scatter_dimension=0, tiled=True),
-        lax.psum_scatter(ffn2_grads[4], ("fsdp", "ctx"), scatter_dimension=0, tiled=True),
-    )
-    full_hidden = ffn1_in_bias.shape[0]
-    full_width = query_bias.shape[0]
-    shared = lax.psum(
+    ffn2_parts = scatter_sum(ffn2_grads[2], ffn2_grads[4])
+    conv_parts = scatter_sum(conv_grads[2], conv_grads[3], conv_grads[7])
+    attn_parts = scatter_sum(attn_grads[2], attn_grads[4], attn_grads[5], attn_grads[7])
+    ffn1_parts = scatter_sum(ffn1_grads[2], ffn1_grads[4])
+    weight_parts = ffn1_parts + attn_parts + conv_parts + ffn2_parts
+    shared = sum_small(
         (
             ffn1_grads[0],
             ffn1_grads[1],
-            local_put(ffn1_grads[3], tp_rank, full_hidden),
             ffn1_grads[5],
             attn_grads[0],
             attn_grads[1],
-            local_put(attn_grads[3], tp_rank, full_width),
-            local_put(attn_grads[6], tp_rank, full_width),
             attn_grads[8],
             attn_grads[9],
             conv_grads[0],
             conv_grads[1],
-            local_put(conv_grads[4], tp_rank, full_width),
-            local_put(conv_grads[5], tp_rank, full_width),
-            local_put(conv_grads[6], tp_rank, full_width),
             ffn2_grads[0],
             ffn2_grads[1],
-            local_put(ffn2_grads[3], tp_rank, full_hidden),
             ffn2_grads[5],
             final_gain_grad,
             final_shift_grad,
             sse_local,
         ),
-        ("fsdp", "ctx", "tp"),
+        (
+            ffn1_grads[3],
+            attn_grads[3],
+            attn_grads[6],
+            conv_grads[4],
+            conv_grads[5],
+            conv_grads[6],
+            ffn2_grads[3],
+        ),
+        tp_rank,
     )
     token_count = (jnp.sum(clips_dev) * SEQ).astype(jnp.float32)
     loss = shared[21] / token_count

time: 2640 us -> 2370 us (0.90)
  waiting for transfers between devices: 1350 us -> 1120 us
  blocking collectives: 150 us -> 34.5 us
  local copies, waits for them, and re-layouts: 684 us -> 768 us
    reduce_scatter x13 -> x0, waiting for transfers between devices: 429 us -> none  [the longest x1 55.1 us: body(): lax.psum_scatter(ffn1_grads[4], ('fsdp', 'ctx'), scatter_dimension=0, til...]
    unnamed x36 -> x37, waiting for transfers between devices: 3.28 us -> 134 us
    all_gather x7 -> x0, blocking collectives: 72.3 us -> none  [the longest x1 12.4 us: body(): lax.all_gather(value_weight, ('fsdp', 'ctx'), axis=0, tiled=True)]
    unnamed x345 -> x384, local copies, waits for them, and re-layouts: 16.3 us -> 82.5 us
    all_gather x4 -> x6, waiting for transfers between devices: 96.5 us -> 144 us  [gather_rows(): return lax.all_gather(shard, ('fsdp', 'ctx'), axis=0, tiled=True)]
    all_gather x4, waiting for transfers between devices: 162 us -> 207 us  [widen(): return lax.all_gather(normed.astype(jnp.bfloat16), 'tp', axis=1, tiled=True)]
    psum x1 -> x0, blocking collectives: 43.6 us -> none  [body(): lax.psum((ffn1_grads[0], ffn1_grads[1], local_put(ffn1_grads[3], tp_rank,...]
  transfers between devices with their start and end apart: 38 -> 33, of which waited for: 31 -> 27; matrix products, arithmetic and copies ran while one was open for 27% -> 34% of each run, Pallas kernels for 0% -> 0%
where the time goes in v1:
time: 2370 us; the launch traced here: 2360 us
  waiting for transfers between devices  1120 us (47%)
  local copies, waits for them, and re-layouts  768 us (32%)
  matrix products  213 us (9%)
  other arithmetic  203 us (9%)
  blocking collectives  34.5 us (1%)
    all_gather x4, waiting for transfers between devices, widen(): return lax.all_gather(normed.astype(jnp.bfloat16), 'tp', axis=1, tiled=True)  207 us
    all_gather x4, waiting for transfers between devices, widen_grad(): return lax.all_gather(grad_branch, 'tp', axis=1, tiled=True)  198 us
    reduce_scatter x4, waiting for transfers between devices, narrow(): lax.psum_scatter(partial_rows.astype(jnp.bfloat16), 'tp', scatter_dimensi...  183 us
    all_gather x6, waiting for transfers between devices, gather_rows(): return lax.all_gather(shard, ('fsdp', 'ctx'), axis=0, tiled=True)  144 us
    reshape x2, local copies, waits for them, and re-layouts, band_bias(): return sheared.reshape(lead[:2] + (row_count, extent - 1))[..., :key_count]  142 us
    reduce_scatter x4, waiting for transfers between devices, narrow_grad(): lax.psum_scatter(partial_rows.astype(jnp.bfloat16), 'tp', scatter_dimensi...  139 us
    reshape x3, local copies, waits for them, and re-layouts, band_bias(): flat = skewed.reshape(lead[:2] + (row_count * extent,))  134 us
    unnamed x37, waiting for transfers between devices  134 us
  transfers between devices with their start and end apart: 33, of which 27 were waited for; matrix products, arithmetic and copies ran while one was open for 34% of the time, Pallas kernels for 0%

profile of v1, /device:TPU:0, one launch (start us, length us, event | category | flops | bytes accessed | tf_op | source)
XLA Modules:
  0.0 2362.9 jit_solution(17396104791334271107)
XLA Ops:
  14.0 50.6 %all-gather.17.cloned.1.call-done = bf16[3,384,1024]{2,1,0:T(8,128)(2,1)} async-done(((bf16[3,96,1024]{2,1,0:T(8,128)(2,1)}), bf16[3,384,1024]{2,1,0:T(8,128)(2,1)}) %all-gather.17.cloned.1.call-update) | async-done | bytes 2359312 | tf_op jit(solution)/shard_map/all_gather | solution.py:56
  131.7 46.1 %reduce-scatter.27.cloned.1.call-done = bf16[3,96,1024]{2,1,0:T(8,128)(2,1)} async-done(((bf16[3,384,1024]{2,1,0:T(8,128)(2,1)}), bf16[3,96,1024]{2,1,0:T(8,128)(2,1)}) %reduce-scatter.27.cloned.1.call-update) | async-done | bytes 589840 | tf_op jit(solution)/shard_map/reduce_scatter | solution.py:60
  207.3 52.0 %all-gather.23.cloned.1.call-done = bf16[3,384,1024]{2,1,0:T(8,128)(2,1)} async-done(((bf16[3,96,1024]{2,1,0:T(8,128)(2,1)}), bf16[3,384,1024]{2,1,0:T(8,128)(2,1)}) %all-gather.23.cloned.1.call-update) | async-done | bytes 2359312 | tf_op jit(solution)/shard_map/all_gather | solution.py:56
  294.4 70.2 %concatenate.94 = f32[3,4,384,3529]{3,2,1,0:T(8,128)} concatenate(f32[3,4,384,1536]{3,2,1,0:T(8,128)} %broadcast_in_dim.19, f32[3,4,384,73]{3,2,1,0:T(8,128)S(1)} %copy.137, f32[3,4,384,1920]{3,2,1,0:T(8,128)} %broadcast_in_dim.21), dimensions={3} | concatenate | bytes 130093056 | tf_op jit(solution)/shard_map/concatenate | solution.py:97
  394.4 42.5 %reshape.1214 = f32[3,4,737280]{2,1,0:T(4,128)} reshape(f32[3,4,384,1920]{3,2,1,0:T(8,128)} %constant_dynamic-slice_fusion.1) | data formatting | bytes 70778880 | tf_op jit(solution)/shard_map/reshape | solution.py:100
  461.4 81.1 %reshape.1215 = f32[3,4,384,1919]{3,2,1,0:T(8,128)} reshape(f32[3,4,736896]{2,1,0:T(4,128)} %slice.1308) | data formatting | bytes 70742016 | tf_op jit(solution)/shard_map/reshape | solution.py:102
  603.0 45.1 %reduce-scatter.29.cloned.1.call-done = bf16[3,96,1024]{2,1,0:T(8,128)(2,1)} async-done(((bf16[3,384,1024]{2,1,0:T(8,128)(2,1)}), bf16[3,96,1024]{2,1,0:T(8,128)(2,1)}) %reduce-scatter.29.cloned.1.call-update) | async-done | bytes 589840 | tf_op jit(solution)/shard_map/reduce_scatter | solution.py:60
  675.4 52.2 %all-gather.31.cloned.1.call-done = bf16[3,384,1024]{2,1,0:T(8,128)(2,1)} async-done(((bf16[3,96,1024]{2,1,0:T(8,128)(2,1)}), bf16[3,384,1024]{2,1,0:T(8,128)(2,1)}) %all-gather.31.cloned.1.call-update) | async-done | bytes 2359312 | tf_op jit(solution)/shard_map/all_gather | solution.py:56
  764.8 45.8 %reduce-scatter.31.cloned.1.call-done = bf16[3,96,1024]{2,1,0:T(8,128)(2,1)} async-done(((bf16[3,384,1024]{2,1,0:T(8,128)(2,1)}), bf16[3,96,1024]{2,1,0:T(8,128)(2,1)}) %reduce-scatter.31.cloned.1.call-update) | async-done | bytes 589840 | tf_op jit(solution)/shard_map/reduce_scatter | solution.py:60
  839.7 52.0 %all-gather.35.cloned.1.call-done = bf16[3,384,1024]{2,1,0:T(8,128)(2,1)} async-done(((bf16[3,96,1024]{2,1,0:T(8,128)(2,1)}), bf16[3,384,1024]{2,1,0:T(8,128)(2,1)}) %all-gather.35.cloned.1.call-update) | async-done | bytes 2359312 | tf_op jit(solution)/shard_map/all_gather | solution.py:56
  929.1 46.0 %reduce-scatter.33.cloned.1.call-done = bf16[3,96,1024]{2,1,0:T(8,128)(2,1)} async-done(((bf16[3,384,1024]{2,1,0:T(8,128)(2,1)}), bf16[3,96,1024]{2,1,0:T(8,128)(2,1)}) %reduce-scatter.33.cloned.1.call-update) | async-done | bytes 589840 | tf_op jit(solution)/shard_map/reduce_scatter | solution.py:60
  982.1 49.3 %all-gather.41.cloned.1.call-done = bf16[3,384,1024]{2,1,0:T(8,128)(2,1)} async-done(((bf16[3,96,1024]{2,1,0:T(8,128)(2,1)}), bf16[3,384,1024]{2,1,0:T(8,128)(2,1)}) %all-gather.41.cloned.1.call-update) | async-done | bytes 2359312 | tf_op jit(solution)/shard_map/all_gather | solution.py:66
  1045.0 46.6 %reduce-scatter.35.cloned.1.call-done = bf16[3,96,1024]{2,1,0:T(8,128)(2,1)} async-done(((bf16[3,384,1024]{2,1,0:T(8,128)(2,1)}), bf16[3,96,1024]{2,1,0:T(8,128)(2,1)}) %reduce-scatter.35.cloned.1.call-update) | async-done | bytes 589840 | tf_op jit(solution)/shard_map/reduce_scatter | solution.py:70
  1096.1 49.5 %all-gather.43.cloned.1.call-done = bf16[3,384,1024]{2,1,0:T(8,128)(2,1)} async-done(((bf16[3,96,1024]{2,1,0:T(8,128)(2,1)}), bf16[3,384,1024]{2,1,0:T(8,128)(2,1)}) %all-gather.43.cloned.1.call-update) | async-done | bytes 2359312 | tf_op jit(solution)/shard_map/all_gather | solution.py:66
  1382.0 46.6 %reduce-scatter.37.cloned.1.call-done = bf16[3,96,1024]{2,1,0:T(8,128)(2,1)} async-done(((bf16[3,384,1024]{2,1,0:T(8,128)(2,1)}), bf16[3,96,1024]{2,1,0:T(8,128)(2,1)}) %reduce-scatter.37.cloned.1.call-update) | async-done | bytes 589840 | tf_op jit(solution)/shard_map/reduce_scatter | solution.py:70
  1435.5 49.4 %all-gather.45.cloned.1.call-done = bf16[3,384,1024]{2,1,0:T(8,128)(2,1)} async-done(((bf16[3,96,1024]{2,1,0:T(8,128)(2,1)}), bf16[3,384,1024]{2,1,0:T(8,128)(2,1)}) %all-gather.45.cloned.1.call-update) | async-done | bytes 2359312 | tf_op jit(solution)/shard_map/all_gather | solution.py:66
  1593.7 60.9 %reshape.1218 = f32[3,4,736896]{2,1,0:T(4,128)} reshape(f32[3,4,384,1919]{3,2,1,0:T(8,128)} %pad.88) | data formatting | bytes 70742016 | tf_op jit(solution)/shard_map/transpose(jvp())/reshape | solution.py:102
  1679.1 50.1 %reshape.1219 = f32[3,4,384,1920]{3,2,1,0:T(8,128)} reshape(f32[3,4,737280]{2,1,0:T(4,128)} %pad.89) | data formatting | bytes 70778880 | tf_op jit(solution)/shard_map/transpose(jvp())/reshape | solution.py:100
  1729.2 41.3 %copy.140 = f32[3,4,384,1920]{2,1,0,3:T(4,128)} copy(f32[3,4,384,1920]{3,2,1,0:T(8,128)} %reshape.1219) | data formatting | bytes 70778880 | tf_op jit(solution)/shard_map/transpose(jvp())/reshape | solution.py:100
  1865.1 46.2 %reduce-scatter.39.cloned.1.call-done = bf16[3,96,1024]{2,1,0:T(8,128)(2,1)} async-done(((bf16[3,384,1024]{2,1,0:T(8,128)(2,1)}), bf16[3,96,1024]{2,1,0:T(8,128)(2,1)}) %reduce-scatter.39.cloned.1.call-update) | async-done | bytes 589840 | tf_op jit(solution)/shard_map/reduce_scatter | solution.py:70
  1916.2 49.5 %all-gather.47.cloned.1.call-done = bf16[3,384,1024]{2,1,0:T(8,128)(2,1)} async-done(((bf16[3,96,1024]{2,1,0:T(8,128)(2,1)}), bf16[3,384,1024]{2,1,0:T(8,128)(2,1)}) %all-gather.47.cloned.1.call-update) | async-done | bytes 2359312 | tf_op jit(solution)/shard_map/all_gather | solution.py:66
  2082.5 38.4 %reduce-scatter.51.cloned.1.call-done = bf16[128,768]{1,0:T(8,128)(2,1)} async-done(((bf16[1024,768]{1,0:T(8,128)(2,1)}), bf16[128,768]{1,0:T(8,128)(2,1)}) %reduce-scatter.51.cloned.1.call-update) | async-done | bytes 196624
  2183.8 113.3 %all-reduce.11.cloned.1.call-done = f32[488,128]{1,0:T(8,128)} async-done(((f32[488,128]{1,0:T(8,128)}), f32[488,128]{1,0:T(8,128)}) %all-reduce.11.cloned.1.call-update) | async-done | bytes 249872 | tf_op jit(solution)/shard_map/psum | solution.py:407
  2306.8 44.6 %reduce-scatter.47.cloned.1.call-done = bf16[128,2048]{1,0:T(8,128)(2,1)} async-done(((bf16[1024,2048]{1,0:T(8,128)(2,1)}), bf16[128,2048]{1,0:T(8,128)(2,1)}) %reduce-scatter.47.cloned.1.call-update) | async-done | bytes 524304
  (677 shorter events, 1074.1 us)
Async XLA Ops:
  12.5 110.3 %all-gather.21.cloned.1.call-start = ((), (), s32[]{:S(2)}) async-start(), calls=%async_computation.16 | async-start | bytes 2359296 | tf_op jit(solution)/shard_map/all_gather | solution.py:384
  13.2 164.6 %reduce-scatter.27.cloned.1.call-start = ((), (), s32[]{:S(2)}) async-start(), calls=%async_computation.17 | async-start | bytes 2949120 | tf_op jit(solution)/shard_map/reduce_scatter | solution.py:60
  131.6 127.7 %all-gather.23.cloned.1.call-start = ((), (), s32[]{:S(2)}) async-start(), calls=%async_computation.18 | async-start | bytes 2949120 | tf_op jit(solution)/shard_map/all_gather | solution.py:56
  181.7 363.6 %all-gather.29.cloned.1.call-start = ((), (), s32[]{:S(2)}) async-start(), calls=%async_computation.21 | async-start | bytes 2949120 | tf_op jit(solution)/shard_map/all_gather | solution.py:150
  262.9 319.1 %all-gather.27.cloned.1.call-start = ((), (), s32[]{:S(2)}) async-start(), calls=%async_computation.20 | async-start | bytes 2949120 | tf_op jit(solution)/shard_map/all_gather | solution.py:151
  545.2 102.9 %reduce-scatter.29.cloned.1.call-start = ((), (), s32[]{:S(2)}) async-start(), calls=%async_computation.22 | async-start | bytes 2949120 | tf_op jit(solution)/shard_map/reduce_scatter | solution.py:60
  602.9 124.6 %all-gather.31.cloned.1.call-start = ((), (), s32[]{:S(2)}) async-start(), calls=%async_computation.23 | async-start | bytes 2949120 | tf_op jit(solution)/shard_map/all_gather | solution.py:56
  652.3 158.3 %reduce-scatter.31.cloned.1.call-start = ((), (), s32[]{:S(2)}) async-start(), calls=%async_computation.25 | async-start | bytes 2949120 | tf_op jit(solution)/shard_map/reduce_scatter | solution.py:60
  764.8 126.9 %all-gather.35.cloned.1.call-start = ((), (), s32[]{:S(2)}) async-start(), calls=%async_computation.26 | async-start | bytes 2949120 | tf_op jit(solution)/shard_map/all_gather | solution.py:56
  814.2 105.9 %all-gather.39.cloned.1.call-start = ((), (), s32[]{:S(2)}) async-start(), calls=%async_computation.28 | async-start | bytes 2359296 | tf_op jit(solution)/shard_map/all_gather | solution.py:384
  814.8 160.2 %reduce-scatter.33.cloned.1.call-start = ((), (), s32[]{:S(2)}) async-start(), calls=%async_computation.29 | async-start | bytes 2949120 | tf_op jit(solution)/shard_map/reduce_scatter | solution.py:60
  927.1 104.2 %all-gather.41.cloned.1.call-start = ((), (), s32[]{:S(2)}) async-start(), calls=%async_computation.30 | async-start | bytes 2949120 | tf_op jit(solution)/shard_map/all_gather | solution.py:66
  981.9 109.7 %reduce-scatter.35.cloned.1.call-start = ((), (), s32[]{:S(2)}) async-start(), calls=%async_computation.31 | async-start | bytes 2949120 | tf_op jit(solution)/shard_map/reduce_scatter | solution.py:70
  1044.9 100.7 %all-gather.43.cloned.1.call-start = ((), (), s32[]{:S(2)}) async-start(), calls=%async_computation.32 | async-start | bytes 2949120 | tf_op jit(solution)/shard_map/all_gather | solution.py:66
  1096.1 332.5 %reduce-scatter.37.cloned.1.call-start = ((), (), s32[]{:S(2)}) async-start(), calls=%async_computation.33 | async-start | bytes 2949120 | tf_op jit(solution)/shard_map/reduce_scatter | solution.py:70
  1381.9 103.0 %all-gather.45.cloned.1.call-start = ((), (), s32[]{:S(2)}) async-start(), calls=%async_computation.34 | async-start | bytes 2949120 | tf_op jit(solution)/shard_map/all_gather | solution.py:66
  1435.4 418.5 %reduce-scatter.45.cloned.1.call-start = ((), (), s32[]{:S(2)}) async-start(), calls=%async_computation.40 | async-start | bytes 2949120
  1528.6 327.5 %reduce-scatter.43.cloned.1.call-start = ((), (), s32[]{:S(2)}) async-start(), calls=%async_computation.39 | async-start | bytes 2949120
  1770.5 140.9 %reduce-scatter.39.cloned.1.call-start = ((), (), s32[]{:S(2)}) async-start(), calls=%async_computation.35 | async-start | bytes 2949120 | tf_op jit(solution)/shard_map/reduce_scatter | solution.py:70
  1916.1 124.4 %reduce-scatter.41.cloned.1.call-start = ((), (), s32[]{:S(2)}) async-start(), calls=%async_computation.37 | async-start | bytes 2949120 | tf_op jit(solution)/shard_map/reduce_scatter | solution.py:70
  1999.5 121.4 %reduce-scatter.51.cloned.1.call-start = ((), (), s32[]{:S(2)}) async-start(), calls=%async_computation.43 | async-start | bytes 1769472
  2009.8 155.5 %reduce-scatter.49.cloned.1.call-start = ((), (), s32[]{:S(2)}) async-start(), calls=%async_computation.42 | async-start | bytes 2359296
  2021.7 275.4 %all-reduce.11.cloned.1.call-start = ((), (), s32[]{:S(2)}) async-start(), calls=%async_computation.38 | async-start | bytes 499712 | tf_op jit(solution)/shard_map/psum | solution.py:407
  2055.1 296.2 %reduce-scatter.47.cloned.1.call-start = ((), (), s32[]{:S(2)}) async-start(), calls=%async_computation.41 | async-start | bytes 4718592
  (175 other events, 6397.6 us)
Sparse Core Ops, SparseCore 0:
  11.8 52.6 all-gather.16
  94.9 27.7 all-gather.20
  130.1 47.6 reduce-scatter.26
  209.3 49.9 all-gather.22
  601.5 46.5 reduce-scatter.28
  677.6 49.9 all-gather.30
  764.2 46.4 reduce-scatter.30
  841.7 49.9 all-gather.34
  927.3 47.6 reduce-scatter.32
  982.0 49.3 all-gather.40
  1045.0 46.4 reduce-scatter.34
  1096.2 49.3 all-gather.42
  1382.0 46.4 reduce-scatter.36
  1435.5 49.3 all-gather.44
  1528.7 31.5 reduce-scatter.44
  1770.6 31.1 reduce-scatter.42
  1865.2 46.1 reduce-scatter.38
  1916.3 49.3 all-gather.46
  1978.9 46.4 reduce-scatter.40
  2028.6 50.5 reduce-scatter.52
  2082.5 38.3 reduce-scatter.50
  2124.2 41.0 reduce-scatter.48
  2171.3 125.8 all-reduce.10
  2300.5 50.8 reduce-scatter.46
  (7 shorter events, 177.5 us)

commit v2 on v1

--- a/solution.py
+++ b/solution.py
@@ -1,8 +1,11 @@
+import functools
 import math
 
 import jax
 import jax.numpy as jnp
 from jax import lax
+from jax.experimental import pallas as pl
+from jax.experimental.pallas import tpu as pltpu
 from jax.sharding import PartitionSpec as P
 
 D = 1024
@@ -88,27 +91,187 @@
     )
 
 
-def band_bias(rel_scores, query_start, key_count):
-    lead = rel_scores.shape[:3]
-    row_count = lead[2]
-    extent = key_count + row_count
-    left_edge = jnp.broadcast_to(rel_scores[..., :1], lead + (key_count,))
-    right_edge = jnp.broadcast_to(rel_scores[..., -1:], lead + (key_count + row_count,))
-    extended = jnp.concatenate([left_edge, rel_scores, right_edge], axis=3)
-    start = key_count + LEFT - (row_count - 1) - query_start
-    skewed = lax.dynamic_slice_in_dim(extended, start, extent, 3)
-    flat = skewed.reshape(lead[:2] + (row_count * extent,))
-    sheared = flat[..., row_count - 1 : row_count - 1 + row_count * (extent - 1)]
-    return sheared.reshape(lead[:2] + (row_count, extent - 1))[..., :key_count]
-
-
-def attention_logits(query_heads, key_heads, rel_table, query_start):
-    rel_scores = jnp.einsum(
-        "slhe,re->shlr", query_heads, rel_table, preferred_element_type=jnp.float32
-    )
-    bias_entries = band_bias(rel_scores, query_start, key_heads.shape[1])
-    dots = jnp.einsum("slhe,smhe->shlm", query_heads, key_heads, preferred_element_type=jnp.float32)
-    return ((dots + bias_entries) * (1.0 / math.sqrt(HEAD)), rel_scores)
+BAND = 384
+
+
+def wide_table(rel_table):
+    before = jnp.broadcast_to(rel_table[:1], (LEFT, HEAD))
+    after = jnp.broadcast_to(rel_table[-1:], (BAND - LEFT - rel_table.shape[0], HEAD))
+    return jnp.concatenate([before, rel_table, after], axis=0)
+
+
+def dot_t(left, right):
+    return lax.dot_general(left, right, (((1,), (1,)), ((), ())), preferred_element_type=jnp.float32)
+
+
+def dot_n(left, right):
+    return lax.dot_general(left, right, (((1,), (0,)), ((), ())), preferred_element_type=jnp.float32)
+
+
+def scaled_scores(query_block, keys, table, place, rows_at, reach):
+    rows = query_block.shape[0]
+    key_count = keys.shape[0]
+    near = dot_t(query_block, table)
+    left, right = near[:, :1], near[:, BAND - 1 :]
+    row = lax.broadcasted_iota(jnp.int32, (rows, key_count), 0)
+    col = lax.broadcasted_iota(jnp.int32, (rows, key_count), 1)
+    place[:, 128 : 128 + key_count] = dot_t(query_block, keys) + jnp.where(
+        col < row + rows_at, left, right
+    )
+    rolled = pltpu.roll(near, 0, 1, stride=1, stride_axis=0)
+    apart = band_distance(rows)
+    band = jnp.where(apart <= -LEFT, left, jnp.where(apart >= reach, right, rolled))
+    window = pl.ds(pl.multiple_of(rows_at, 128), BAND)
+    place[:, window] += band - jnp.where(apart < 0, left, right)
+    return place[:, 128 : 128 + key_count]
+
+
+def band_distance(rows):
+    row = lax.broadcasted_iota(jnp.int32, (rows, BAND), 0)
+    col = lax.broadcasted_iota(jnp.int32, (rows, BAND), 1)
+    return col - 128 - row
+
+
+def attend_kernel(reach, start_ref, query_ref, key_ref, value_ref, table_ref, mixed_ref, total_ref, place):
+    rows = query_ref.shape[1]
+    rows_at = start_ref[0] + pl.program_id(2) * rows
+    table = table_ref[...]
+    for half in range(query_ref.shape[2] // HEAD):
+        lanes = slice(half * HEAD, (half + 1) * HEAD)
+        query_block = query_ref[0, :, lanes] * jnp.bfloat16(1.0 / math.sqrt(HEAD))
+        scores = scaled_scores(query_block, key_ref[0, :, lanes], table, place, rows_at, reach)
+        top = jnp.max(scores, axis=-1, keepdims=True)
+        powers = jnp.exp(scores - top)
+        row_sum = jnp.sum(powers, axis=-1, keepdims=True)
+        probs = (powers * (1.0 / row_sum)).astype(jnp.bfloat16)
+        mixed_ref[0, :, lanes] = dot_n(probs, value_ref[0, :, lanes]).astype(jnp.bfloat16)
+        total_ref[0, :, lanes] = jnp.broadcast_to(top + jnp.log(row_sum), (rows, HEAD))
+
+
+def attend_back_kernel(
+    reach, start_ref, query_ref, key_ref, value_ref, table_ref, total_ref, grad_ref,
+    query_grad_ref, key_grad_ref, value_grad_ref, table_grad_ref, place, key_sum, value_sum,
+):
+    rows = query_ref.shape[1]
+    key_count = key_ref.shape[1]
+    block = pl.program_id(2)
+    rows_at = start_ref[0] + block * rows
+    table = table_ref[...]
+    scale = jnp.bfloat16(1.0 / math.sqrt(HEAD))
+
+    @pl.when(block == 0)
+    def _():
+        key_sum[...] = jnp.zeros_like(key_sum)
+        value_sum[...] = jnp.zeros_like(value_sum)
+
+    @pl.when((block == 0) & (pl.program_id(0) == 0) & (pl.program_id(1) == 0))
+    def _():
+        table_grad_ref[...] = jnp.zeros_like(table_grad_ref)
+
+    for half in range(query_ref.shape[2] // HEAD):
+        lanes = slice(half * HEAD, (half + 1) * HEAD)
+        query_block = query_ref[0, :, lanes] * scale
+        keys = key_ref[0, :, lanes]
+        grad_block = grad_ref[0, :, lanes]
+        scores = scaled_scores(query_block, keys, table, place, rows_at, reach)
+        probs = jnp.exp(scores - total_ref[0, :, half * HEAD : half * HEAD + 1])
+        grad_probs = dot_t(grad_block, value_ref[0, :, lanes])
+        row_dot = jnp.sum(probs * grad_probs, axis=-1, keepdims=True)
+        grad_scores = (probs * (grad_probs - row_dot)).astype(jnp.bfloat16)
+        value_sum[lanes, :] += dot_n(grad_block.T, probs.astype(jnp.bfloat16))
+        key_sum[lanes, :] += dot_n(query_block.T, grad_scores)
+        wide = grad_scores.astype(jnp.float32)
+        place[:, 128 : 128 + key_count] = wide
+        apart_all = (
+            lax.broadcasted_iota(jnp.int32, wide.shape, 1)
+            - lax.broadcasted_iota(jnp.int32, wide.shape, 0)
+            - rows_at
+        )
+        far_left = jnp.sum(jnp.where(apart_all <= -LEFT, wide, 0.0), axis=-1, keepdims=True)
+        far_right = jnp.sum(jnp.where(apart_all >= reach, wide, 0.0), axis=-1, keepdims=True)
+        window = place[:, pl.ds(pl.multiple_of(rows_at, 128), BAND)]
+        window_col = lax.broadcasted_iota(jnp.int32, window.shape, 1) + rows_at - 128
+        apart = band_distance(rows)
+        inside = (apart > -LEFT) & (apart < reach) & (window_col >= 0) & (window_col < key_count)
+        turned = jnp.where(inside, window, 0.0)
+        row = lax.broadcasted_iota(jnp.int32, turned.shape, 0)
+        for bit in range((rows - 1).bit_length()):
+            moved = pltpu.roll(turned, BAND - (1 << bit), 1)
+            turned = jnp.where(((row >> bit) & 1) == 1, moved, turned)
+        lane = lax.broadcasted_iota(jnp.int32, turned.shape, 1)
+        by_row = jnp.where(lane == LEFT, far_left, jnp.where(lane == 2 * LEFT + reach, far_right, turned))
+        coarse = by_row.astype(jnp.bfloat16)
+        fine = (by_row - coarse.astype(jnp.float32)).astype(jnp.bfloat16)
+        query_grad = dot_n(grad_scores, keys) + dot_n(coarse, table) + dot_n(fine, table)
+        query_grad_ref[0, :, lanes] = (query_grad * (1.0 / math.sqrt(HEAD))).astype(jnp.bfloat16)
+        query_turned = query_block.T
+        table_grad_ref[...] += dot_n(query_turned, coarse) + dot_n(query_turned, fine)
+
+    @pl.when(block == pl.num_programs(2) - 1)
+    def _():
+        key_grad_ref[0] = key_sum[...].T.astype(jnp.bfloat16)
+        value_grad_ref[0] = value_sum[...].T.astype(jnp.bfloat16)
+
+
+def attend_specs(queries, keys):
+    slots, rows, width = queries.shape
+    lanes = 2 * HEAD
+    block = 128
+    grid = (slots, width // lanes, rows // block)
+    by_query = pl.BlockSpec((1, block, lanes), lambda s, p, b, *_: (s, b, p))
+    by_key = pl.BlockSpec((1, keys.shape[1], lanes), lambda s, p, b, *_: (s, 0, p))
+    table = pl.BlockSpec((BAND, HEAD), lambda s, p, b, *_: (0, 0))
+    place = pltpu.VMEM((block, keys.shape[1] + 256), jnp.float32)
+    flops = slots * rows * keys.shape[1] * width * 4
+    return grid, by_query, by_key, table, place, flops
+
+
+def attend(queries, keys, values, table, reach, query_start):
+    grid, by_query, by_key, by_table, place, flops = attend_specs(queries, keys)
+    return pl.pallas_call(
+        functools.partial(attend_kernel, reach),
+        out_shape=(
+            jax.ShapeDtypeStruct(queries.shape, jnp.bfloat16),
+            jax.ShapeDtypeStruct(queries.shape, jnp.float32),
+        ),
+        grid_spec=pltpu.PrefetchScalarGridSpec(
+            num_scalar_prefetch=1,
+            grid=grid,
+            in_specs=[by_query, by_key, by_key, by_table],
+            out_specs=(by_query, by_query),
+            scratch_shapes=[place],
+        ),
+        cost_estimate=pl.CostEstimate(flops=2 * flops, bytes_accessed=8 << 20, transcendentals=flops >> 8),
+        name="attend",
+    )(query_start.reshape(1), queries, keys, values, table)
+
+
+def attend_back(queries, keys, values, table, totals, grad_mixed, reach, query_start):
+    grid, by_query, by_key, by_table, place, flops = attend_specs(queries, keys)
+    turned = pltpu.VMEM((2 * HEAD, keys.shape[1]), jnp.float32)
+    return pl.pallas_call(
+        functools.partial(attend_back_kernel, reach),
+        out_shape=(
+            jax.ShapeDtypeStruct(queries.shape, jnp.bfloat16),
+            jax.ShapeDtypeStruct(keys.shape, jnp.bfloat16),
+            jax.ShapeDtypeStruct(keys.shape, jnp.bfloat16),
+            jax.ShapeDtypeStruct((HEAD, BAND), jnp.float32),
+        ),
+        grid_spec=pltpu.PrefetchScalarGridSpec(
+            num_scalar_prefetch=1,
+            grid=grid,
+            in_specs=[by_query, by_key, by_key, by_table, by_query, by_query],
+            out_specs=(
+                by_query,
+                by_key,
+                by_key,
+                pl.BlockSpec((HEAD, BAND), lambda s, p, b, *_: (0, 0)),
+            ),
+            scratch_shapes=[place, turned, turned],
+        ),
+        cost_estimate=pl.CostEstimate(flops=5 * flops, bytes_accessed=16 << 20, transcendentals=flops >> 8),
+        name="attend_back",
+    )(query_start.reshape(1), queries, keys, values, table, totals, grad_mixed)
 
 
 def ffn_forward(stream, norm_gain, norm_shift, weight_in, bias_in, weight_out, bias_out):
@@ -150,20 +313,10 @@
         lax.all_gather(keys_local, "ctx", axis=1, tiled=True),
         lax.all_gather(values_local, "ctx", axis=1, tiled=True),
     )
-    slot_count, row_count, width_local = queries.shape
-    key_count = keys_all.shape[1]
-    head_count = width_local // HEAD
-    query_heads = queries.reshape(slot_count, row_count, head_count, HEAD)
-    key_heads = keys_all.reshape(slot_count, key_count, head_count, HEAD)
-    value_heads = values_all.reshape(slot_count, key_count, head_count, HEAD)
-    scores, rel_scores = attention_logits(query_heads, key_heads, rel_table, ctx_rank * row_count)
-    row_max = jnp.max(scores, axis=-1, keepdims=True)
-    log_total = row_max + jnp.log(jnp.sum(jnp.exp(scores - row_max), axis=-1, keepdims=True))
-    attn_probs = jnp.exp(scores - log_total).astype(jnp.bfloat16)
-    mixed_heads = jnp.einsum(
-        "shlm,smhe->slhe", attn_probs, value_heads, preferred_element_type=jnp.float32
-    )
-    mixed_token_rows = mixed_heads.astype(jnp.bfloat16).reshape(slot_count, row_count, width_local)
+    reach = rel_table.shape[0] - 1 - LEFT
+    mixed_token_rows, log_total = attend(
+        queries, keys_all, values_all, wide_table(rel_table), reach, ctx_rank * queries.shape[1]
+    )
     branch = narrow(rows_out(mixed_token_rows, out_w)) + out_b
     return (
         stream + branch,
@@ -179,65 +332,22 @@
     wide_grad = widen_grad(grad_branch)
     out_grad = weight_sum(wide_grad, mixed_token_rows)
     grad_mixed = rows_in(wide_grad, out_w).astype(jnp.bfloat16)
-    slot_count, row_count, width_local = queries.shape
-    key_count = keys_all.shape[1]
-    head_count = width_local // HEAD
-    query_heads = queries.reshape(slot_count, row_count, head_count, HEAD)
-    key_heads = keys_all.reshape(slot_count, key_count, head_count, HEAD)
-    value_heads = values_all.reshape(slot_count, key_count, head_count, HEAD)
-    grad_heads = grad_mixed.reshape(slot_count, row_count, head_count, HEAD)
-    query_start = ctx_rank * row_count
-    rel_scores = jnp.einsum(
-        "slhe,re->shlr", query_heads, rel_table, preferred_element_type=jnp.float32
-    )
-    bias_entries, pick_back = jax.vjp(
-        lambda table_scores: band_bias(table_scores, query_start, key_count), rel_scores
-    )
-    dots = jnp.einsum("slhe,smhe->shlm", query_heads, key_heads, preferred_element_type=jnp.float32)
-    scale_factor = 1.0 / math.sqrt(HEAD)
-    scores = (dots + bias_entries) * scale_factor
-    attn_probs = jnp.exp(scores - log_total)
-    grad_probs = jnp.einsum(
-        "slhe,smhe->shlm", grad_heads, value_heads, preferred_element_type=jnp.float32
-    )
-    row_dot = jnp.sum(attn_probs * grad_probs, axis=-1, keepdims=True)
-    grad_scores = (attn_probs * (grad_probs - row_dot)).astype(jnp.bfloat16)
-    value_terms = jnp.einsum(
-        "shlm,slhe->smhe",
-        attn_probs.astype(jnp.bfloat16),
-        grad_heads,
-        preferred_element_type=jnp.float32,
-    )
-    key_terms = (
-        jnp.einsum("shlm,slhe->smhe", grad_scores, query_heads, preferred_element_type=jnp.float32)
-        * scale_factor
-    )
+    reach = rel_table.shape[0] - 1 - LEFT
+    query_low, key_terms, value_terms, table_turned = attend_back(
+        queries,
+        keys_all,
+        values_all,
+        wide_table(rel_table),
+        log_total,
+        grad_mixed,
+        reach,
+        ctx_rank * queries.shape[1],
+    )
+    table_grad = table_turned[:, LEFT : LEFT + rel_table.shape[0]].T
     key_grad, value_grad = (
-        lax.psum_scatter(
-            key_terms.reshape(slot_count, key_count, width_local).astype(jnp.bfloat16),
-            "ctx",
-            scatter_dimension=1,
-            tiled=True,
-        ).astype(jnp.float32),
-        lax.psum_scatter(
-            value_terms.reshape(slot_count, key_count, width_local).astype(jnp.bfloat16),
-            "ctx",
-            scatter_dimension=1,
-            tiled=True,
-        ).astype(jnp.float32),
-    )
-    rel_grad = pick_back(grad_scores.astype(jnp.float32) * scale_factor)[0]
-    query_grad = (
-        jnp.einsum("shlm,smhe->slhe", grad_scores, key_heads, preferred_element_type=jnp.float32)
-        * scale_factor
-    )
-    query_grad = query_grad + jnp.einsum(
-        "shlr,re->slhe", rel_grad, rel_table.astype(jnp.float32), precision=lax.Precision.HIGHEST
-    )
-    table_grad = jnp.einsum(
-        "shlr,slhe->re", rel_grad, query_heads.astype(jnp.float32), precision=lax.Precision.HIGHEST
-    )
-    query_low = query_grad.reshape(slot_count, row_count, width_local).astype(jnp.bfloat16)
+        lax.psum_scatter(key_terms, "ctx", scatter_dimension=1, tiled=True),
+        lax.psum_scatter(value_terms, "ctx", scatter_dimension=1, tiled=True),
+    )
     key_low = key_grad.astype(jnp.bfloat16)
     value_low = value_grad.astype(jnp.bfloat16)
     query_bias_grad = jnp.sum(query_low.astype(jnp.float32), axis=(0, 1))

time: 2370 us -> 1900 us (0.80)
  local copies, waits for them, and re-layouts: 768 us -> 223 us
  Pallas kernels: 0 us -> 104 us
  waiting for transfers between devices: 1120 us -> 1220 us
  matrix products: 213 us -> 136 us
  other arithmetic: 203 us -> 142 us
    reshape x5 -> x0, local copies, waits for them, and re-layouts: 276 us -> none  [the longest x2 142 us: band_bias(): return sheared.reshape(lead[:2] + (row_count, extent - 1))[..., :key_count]]
    pallas_call x0 -> x2, Pallas kernels: none -> 104 us  [the longest x1 69.8 us: attend_back(): pl.pallas_call(functools.partial(attend_back_kernel, reach), out_shape=(j...]
    dot_general x9 -> x0, matrix products: 84.9 us -> none  [the longest x1 22.5 us: attention_logits(): jnp.einsum('slhe,smhe->shlm', query_heads, key_heads, preferred_element_t...]
    concatenate x1 -> x0, local copies, waits for them, and re-layouts: 70.2 us -> none  [band_bias(): extended = jnp.concatenate([left_edge, rel_scores, right_edge], axis=3)]
    reduce_scatter x0 -> x2, waiting for transfers between devices: none -> 58.3 us  [the longest x1 31.4 us: attn_backward(): lax.psum_scatter(value_terms, 'ctx', scatter_dimension=1, tiled=True)]
    pad x2 -> x0, local copies, waits for them, and re-layouts: 47.3 us -> none  [the longest x1 24.5 us: band_bias(): sheared = flat[..., row_count - 1:row_count - 1 + row_count * (extent - 1)]]
    broadcast_in_dim x3 -> x2, local copies, waits for them, and re-layouts: 45.1 us -> 0.02 us  [the longest x1 0.01 us: wide_table(): jnp.broadcast_to(rel_table[-1:], (BAND - LEFT - rel_table.shape[0], HEAD))]
    reduce_sum x3 -> x1, other arithmetic: 32.6 us -> 1.29 us  [attn_backward(): query_bias_grad = jnp.sum(query_low.astype(jnp.float32), axis=(0, 1))]
  transfers between devices with their start and end apart: 33 -> 33, of which waited for: 27 -> 31; matrix products, arithmetic and copies ran while one was open for 34% -> 9% of each run, Pallas kernels for 0% -> 0%
where the time goes in v2:
time: 1900 us; the launch traced here: 1880 us
  waiting for transfers between devices  1220 us (64%)
  local copies, waits for them, and re-layouts  223 us (12%)
  other arithmetic  142 us (7%)
  matrix products  136 us (7%)
  Pallas kernels  104 us (5%)
  blocking collectives  34 us (2%)
    all_gather x4, waiting for transfers between devices, widen(): return lax.all_gather(normed.astype(jnp.bfloat16), 'tp', axis=1, tiled=True)  207 us
    all_gather x4, waiting for transfers between devices, widen_grad(): return lax.all_gather(grad_branch, 'tp', axis=1, tiled=True)  198 us
    reduce_scatter x4, waiting for transfers between devices, narrow(): lax.psum_scatter(partial_rows.astype(jnp.bfloat16), 'tp', scatter_dimensi...  184 us
    all_gather x6, waiting for transfers between devices, gather_rows(): return lax.all_gather(shard, ('fsdp', 'ctx'), axis=0, tiled=True)  144 us
    reduce_scatter x4, waiting for transfers between devices, narrow_grad(): lax.psum_scatter(partial_rows.astype(jnp.bfloat16), 'tp', scatter_dimensi...  141 us
    unnamed x35, waiting for transfers between devices  130 us
    scatter-add x27, local copies, waits for them, and re-layouts, conv_backward(): grad_padded.at[:, tap_index:tap_index + row_count, :]  126 us
    psum x1, waiting for transfers between devices, sum_small(): total = lax.psum(flat, ('fsdp', 'ctx', 'tp')).reshape(-1)  113 us
  transfers between devices with their start and end apart: 33, of which 31 were waited for; matrix products, arithmetic and copies ran while one was open for 9% of the time, Pallas kernels for 0%

profile of v2, /device:TPU:0, one launch (start us, length us, event | category | flops | bytes accessed | tf_op | source)
XLA Modules:
  0.0 1880.2 jit_solution(10126185966684734290)
XLA Ops:
  13.9 50.6 %all-gather.17.cloned.1.call-done = bf16[3,384,1024]{2,1,0:T(8,128)(2,1)} async-done(((bf16[3,96,1024]{2,1,0:T(8,128)(2,1)}), bf16[3,384,1024]{2,1,0:T(8,128)(2,1)}) %all-gather.17.cloned.1.call-update) | async-done | bytes 2359312 | tf_op jit(solution)/shard_map/all_gather | solution.py:59
  64.5 28.5 %all-gather.19.cloned.1.call-done = bf16[1024,1024]{1,0:T(8,128)(2,1)} async-done(((bf16[128,1024]{1,0:T(8,128)(2,1)}), bf16[1024,1024]{1,0:T(8,128)(2,1)}) %all-gather.19.cloned.1.call-update) | async-done | bytes 2097168 | tf_op jit(solution)/shard_map/all_gather | solution.py:494
  131.6 46.1 %reduce-scatter.23.cloned.1.call-done = bf16[3,96,1024]{2,1,0:T(8,128)(2,1)} async-done(((bf16[3,384,1024]{2,1,0:T(8,128)(2,1)}), bf16[3,96,1024]{2,1,0:T(8,128)(2,1)}) %reduce-scatter.23.cloned.1.call-update) | async-done | bytes 589840 | tf_op jit(solution)/shard_map/reduce_scatter | solution.py:63
  207.2 52.0 %all-gather.23.cloned.1.call-done = bf16[3,384,1024]{2,1,0:T(8,128)(2,1)} async-done(((bf16[3,96,1024]{2,1,0:T(8,128)(2,1)}), bf16[3,384,1024]{2,1,0:T(8,128)(2,1)}) %all-gather.23.cloned.1.call-update) | async-done | bytes 2359312 | tf_op jit(solution)/shard_map/all_gather | solution.py:59
  311.8 34.0 %attend.1 = (bf16[3,384,256]{2,1,0:T(8,128)(2,1)}, f32[3,384,256]{2,1,0:T(8,128)}) custom-call(s32[1]{0:T(128)} %bitcast.2.start_ref, bf16[3,384,256]{2,1,0:T(8,128)(2,1)} %fusion.45.query_ref, bf16[3,1536,256]{2,1,0:T(8,128)(2,1)} %all-gather.27.cloned.1.call-done.key_ref, bf16[3,1536,256]{2,1,0:T(8,128)(2,1)} %all-gather.29.cloned.1.call-done.value_ref, ...), custom_call_target="tpu_custom_call" | custom-call | flops 3623878656 | bytes 8388608 | tf_op jit(solution)/shard_map/attend/pallas_call | solution.py:231
  351.2 45.8 %reduce-scatter.25.cloned.1.call-done = bf16[3,96,1024]{2,1,0:T(8,128)(2,1)} async-done(((bf16[3,384,1024]{2,1,0:T(8,128)(2,1)}), bf16[3,96,1024]{2,1,0:T(8,128)(2,1)}) %reduce-scatter.25.cloned.1.call-update) | async-done | bytes 589840 | tf_op jit(solution)/shard_map/reduce_scatter | solution.py:63
  424.3 52.2 %all-gather.31.cloned.1.call-done = bf16[3,384,1024]{2,1,0:T(8,128)(2,1)} async-done(((bf16[3,96,1024]{2,1,0:T(8,128)(2,1)}), bf16[3,384,1024]{2,1,0:T(8,128)(2,1)}) %all-gather.31.cloned.1.call-update) | async-done | bytes 2359312 | tf_op jit(solution)/shard_map/all_gather | solution.py:59
  513.3 45.8 %reduce-scatter.27.cloned.1.call-done = bf16[3,96,1024]{2,1,0:T(8,128)(2,1)} async-done(((bf16[3,384,1024]{2,1,0:T(8,128)(2,1)}), bf16[3,96,1024]{2,1,0:T(8,128)(2,1)}) %reduce-scatter.27.cloned.1.call-update) | async-done | bytes 589840 | tf_op jit(solution)/shard_map/reduce_scatter | solution.py:63
  588.2 52.0 %all-gather.35.cloned.1.call-done = bf16[3,384,1024]{2,1,0:T(8,128)(2,1)} async-done(((bf16[3,96,1024]{2,1,0:T(8,128)(2,1)}), bf16[3,384,1024]{2,1,0:T(8,128)(2,1)}) %all-gather.35.cloned.1.call-update) | async-done | bytes 2359312 | tf_op jit(solution)/shard_map/all_gather | solution.py:59
  677.5 46.0 %reduce-scatter.29.cloned.1.call-done = bf16[3,96,1024]{2,1,0:T(8,128)(2,1)} async-done(((bf16[3,384,1024]{2,1,0:T(8,128)(2,1)}), bf16[3,96,1024]{2,1,0:T(8,128)(2,1)}) %reduce-scatter.29.cloned.1.call-update) | async-done | bytes 589840 | tf_op jit(solution)/shard_map/reduce_scatter | solution.py:63
  730.4 49.5 %all-gather.41.cloned.1.call-done = bf16[3,384,1024]{2,1,0:T(8,128)(2,1)} async-done(((bf16[3,96,1024]{2,1,0:T(8,128)(2,1)}), bf16[3,384,1024]{2,1,0:T(8,128)(2,1)}) %all-gather.41.cloned.1.call-update) | async-done | bytes 2359312 | tf_op jit(solution)/shard_map/all_gather | solution.py:69
  793.3 46.6 %reduce-scatter.31.cloned.1.call-done = bf16[3,96,1024]{2,1,0:T(8,128)(2,1)} async-done(((bf16[3,384,1024]{2,1,0:T(8,128)(2,1)}), bf16[3,96,1024]{2,1,0:T(8,128)(2,1)}) %reduce-scatter.31.cloned.1.call-update) | async-done | bytes 589840 | tf_op jit(solution)/shard_map/reduce_scatter | solution.py:73
  845.5 49.5 %all-gather.43.cloned.1.call-done = bf16[3,384,1024]{2,1,0:T(8,128)(2,1)} async-done(((bf16[3,96,1024]{2,1,0:T(8,128)(2,1)}), bf16[3,384,1024]{2,1,0:T(8,128)(2,1)}) %all-gather.43.cloned.1.call-update) | async-done | bytes 2359312 | tf_op jit(solution)/shard_map/all_gather | solution.py:69
  1130.7 46.6 %reduce-scatter.33.cloned.1.call-done = bf16[3,96,1024]{2,1,0:T(8,128)(2,1)} async-done(((bf16[3,384,1024]{2,1,0:T(8,128)(2,1)}), bf16[3,96,1024]{2,1,0:T(8,128)(2,1)}) %reduce-scatter.33.cloned.1.call-update) | async-done | bytes 589840 | tf_op jit(solution)/shard_map/reduce_scatter | solution.py:73
  1184.5 49.5 %all-gather.45.cloned.1.call-done = bf16[3,384,1024]{2,1,0:T(8,128)(2,1)} async-done(((bf16[3,96,1024]{2,1,0:T(8,128)(2,1)}), bf16[3,384,1024]{2,1,0:T(8,128)(2,1)}) %all-gather.45.cloned.1.call-update) | async-done | bytes 2359312 | tf_op jit(solution)/shard_map/all_gather | solution.py:69
  1237.3 69.8 %attend_back.1 = (bf16[3,384,256]{2,1,0:T(8,128)(2,1)}, bf16[3,1536,256]{2,1,0:T(8,128)(2,1)}, bf16[3,1536,256]{2,1,0:T(8,128)(2,1)}, f32[64,384]{1,0:T(8,128)}) custom-call(s32[1]{0:T(128)} %bitcast.2.start_ref, bf16[3,384,256]{2,1,0:T(8,128)(2,1)} %fusion.45.query_ref, bf16[3,1536,256]{2,1,0:T(8,128)(2,1)} %all-gather.27.cloned.1.call-done.key_ref, ...), custom_call_target="tpu_custom_call" | custom-call | flops 9059696640 | bytes 16777216 | tf_op jit(solution)/shard_map/attend_back/pallas_call | solution.py:252
  1311.9 27.0 %reduce-scatter.35.cloned.1.call-done = bf16[3,384,256]{2,1,0:T(8,128)(2,1)} async-done(((bf16[3,1536,256]{2,1,0:T(8,128)(2,1)}), bf16[3,384,256]{2,1,0:T(8,128)(2,1)}) %reduce-scatter.35.cloned.1.call-update) | async-done | bytes 589840 | tf_op jit(solution)/shard_map/reduce_scatter | solution.py:348
  1342.9 31.4 %reduce-scatter.37.cloned.1.call-done = bf16[3,384,256]{2,1,0:T(8,128)(2,1)} async-done(((bf16[3,1536,256]{2,1,0:T(8,128)(2,1)}), bf16[3,384,256]{2,1,0:T(8,128)(2,1)}) %reduce-scatter.37.cloned.1.call-update) | async-done | bytes 589840 | tf_op jit(solution)/shard_map/reduce_scatter | solution.py:349
  1380.7 47.7 %reduce-scatter.39.cloned.1.call-done = bf16[3,96,1024]{2,1,0:T(8,128)(2,1)} async-done(((bf16[3,384,1024]{2,1,0:T(8,128)(2,1)}), bf16[3,96,1024]{2,1,0:T(8,128)(2,1)}) %reduce-scatter.39.cloned.1.call-update) | async-done | bytes 589840 | tf_op jit(solution)/shard_map/reduce_scatter | solution.py:73
  1433.0 49.5 %all-gather.47.cloned.1.call-done = bf16[3,384,1024]{2,1,0:T(8,128)(2,1)} async-done(((bf16[3,96,1024]{2,1,0:T(8,128)(2,1)}), bf16[3,384,1024]{2,1,0:T(8,128)(2,1)}) %all-gather.47.cloned.1.call-update) | async-done | bytes 2359312 | tf_op jit(solution)/shard_map/all_gather | solution.py:69
  1601.3 36.7 %reduce-scatter.47.cloned.1.call-done = bf16[128,768]{1,0:T(8,128)(2,1)} async-done(((bf16[1024,768]{1,0:T(8,128)(2,1)}), bf16[128,768]{1,0:T(8,128)(2,1)}) %reduce-scatter.47.cloned.1.call-update) | async-done | bytes 196624
  1646.0 36.4 %reduce-scatter.45.cloned.1.call-done = bf16[128,1024]{1,0:T(8,128)(2,1)} async-done(((bf16[1024,1024]{1,0:T(8,128)(2,1)}), bf16[128,1024]{1,0:T(8,128)(2,1)}) %reduce-scatter.45.cloned.1.call-update) | async-done | bytes 262160
  1700.8 113.4 %all-reduce.7.cloned.1.call-done = f32[488,128]{1,0:T(8,128)} async-done(((f32[488,128]{1,0:T(8,128)}), f32[488,128]{1,0:T(8,128)}) %all-reduce.7.cloned.1.call-update) | async-done | bytes 249872 | tf_op jit(solution)/shard_map/psum | solution.py:517
  1823.9 44.6 %reduce-scatter.43.cloned.1.call-done = bf16[128,2048]{1,0:T(8,128)(2,1)} async-done(((bf16[1024,2048]{1,0:T(8,128)(2,1)}), bf16[128,2048]{1,0:T(8,128)(2,1)}) %reduce-scatter.43.cloned.1.call-update) | async-done | bytes 524304
  (539 shorter events, 710.4 us)
Async XLA Ops:
  12.4 110.3 %all-gather.21.cloned.1.call-start = ((), (), s32[]{:S(2)}) async-start(), calls=%async_computation.16 | async-start | bytes 2359296 | tf_op jit(solution)/shard_map/all_gather | solution.py:494
  13.1 164.6 %reduce-scatter.23.cloned.1.call-start = ((), (), s32[]{:S(2)}) async-start(), calls=%async_computation.17 | async-start | bytes 2949120 | tf_op jit(solution)/shard_map/reduce_scatter | solution.py:63
  131.5 127.7 %all-gather.23.cloned.1.call-start = ((), (), s32[]{:S(2)}) async-start(), calls=%async_computation.18 | async-start | bytes 2949120 | tf_op jit(solution)/shard_map/all_gather | solution.py:59
  180.9 104.7 %all-gather.29.cloned.1.call-start = ((), (), s32[]{:S(2)}) async-start(), calls=%async_computation.21 | async-start | bytes 2949120 | tf_op jit(solution)/shard_map/all_gather | solution.py:314
  266.0 131.1 %reduce-scatter.25.cloned.1.call-start = ((), (), s32[]{:S(2)}) async-start(), calls=%async_computation.22 | async-start | bytes 2949120 | tf_op jit(solution)/shard_map/reduce_scatter | solution.py:63
  350.7 125.8 %all-gather.31.cloned.1.call-start = ((), (), s32[]{:S(2)}) async-start(), calls=%async_computation.23 | async-start | bytes 2949120 | tf_op jit(solution)/shard_map/all_gather | solution.py:59
  401.3 157.8 %reduce-scatter.27.cloned.1.call-start = ((), (), s32[]{:S(2)}) async-start(), calls=%async_computation.25 | async-start | bytes 2949120 | tf_op jit(solution)/shard_map/reduce_scatter | solution.py:63
  513.2 127.0 %all-gather.35.cloned.1.call-start = ((), (), s32[]{:S(2)}) async-start(), calls=%async_computation.26 | async-start | bytes 2949120 | tf_op jit(solution)/shard_map/all_gather | solution.py:59
  562.6 105.9 %all-gather.39.cloned.1.call-start = ((), (), s32[]{:S(2)}) async-start(), calls=%async_computation.28 | async-start | bytes 2359296 | tf_op jit(solution)/shard_map/all_gather | solution.py:494
  563.2 160.3 %reduce-scatter.29.cloned.1.call-start = ((), (), s32[]{:S(2)}) async-start(), calls=%async_computation.29 | async-start | bytes 2949120 | tf_op jit(solution)/shard_map/reduce_scatter | solution.py:63
  675.6 104.2 %all-gather.41.cloned.1.call-start = ((), (), s32[]{:S(2)}) async-start(), calls=%async_computation.30 | async-start | bytes 2949120 | tf_op jit(solution)/shard_map/all_gather | solution.py:69
  730.4 109.6 %reduce-scatter.31.cloned.1.call-start = ((), (), s32[]{:S(2)}) async-start(), calls=%async_computation.31 | async-start | bytes 2949120 | tf_op jit(solution)/shard_map/reduce_scatter | solution.py:73
  793.3 101.7 %all-gather.43.cloned.1.call-start = ((), (), s32[]{:S(2)}) async-start(), calls=%async_computation.32 | async-start | bytes 2949120 | tf_op jit(solution)/shard_map/all_gather | solution.py:69
  845.5 331.8 %reduce-scatter.33.cloned.1.call-start = ((), (), s32[]{:S(2)}) async-start(), calls=%async_computation.33 | async-start | bytes 2949120 | tf_op jit(solution)/shard_map/reduce_scatter | solution.py:73
  1130.7 103.3 %all-gather.45.cloned.1.call-start = ((), (), s32[]{:S(2)}) async-start(), calls=%async_computation.34 | async-start | bytes 2949120 | tf_op jit(solution)/shard_map/all_gather | solution.py:69
  1184.4 154.4 %reduce-scatter.35.cloned.1.call-start = ((), (), s32[]{:S(2)}) async-start(), calls=%async_computation.35 | async-start | bytes 2949120 | tf_op jit(solution)/shard_map/reduce_scatter | solution.py:348
  1307.9 120.4 %reduce-scatter.39.cloned.1.call-start = ((), (), s32[]{:S(2)}) async-start(), calls=%async_computation.37 | async-start | bytes 2949120 | tf_op jit(solution)/shard_map/reduce_scatter | solution.py:73
  1380.4 102.0 %all-gather.47.cloned.1.call-start = ((), (), s32[]{:S(2)}) async-start(), calls=%async_computation.38 | async-start | bytes 2949120 | tf_op jit(solution)/shard_map/all_gather | solution.py:69
  1433.0 136.0 %reduce-scatter.41.cloned.1.call-start = ((), (), s32[]{:S(2)}) async-start(), calls=%async_computation.39 | async-start | bytes 2949120 | tf_op jit(solution)/shard_map/reduce_scatter | solution.py:73
  1496.0 100.4 %reduce-scatter.49.cloned.1.call-start = ((), (), s32[]{:S(2)}) async-start(), calls=%async_computation.44 | async-start | bytes 4718592
  1516.7 121.3 %reduce-scatter.47.cloned.1.call-start = ((), (), s32[]{:S(2)}) async-start(), calls=%async_computation.43 | async-start | bytes 1769472
  1526.7 155.7 %reduce-scatter.45.cloned.1.call-start = ((), (), s32[]{:S(2)}) async-start(), calls=%async_computation.42 | async-start | bytes 2359296
  1545.4 268.9 %all-reduce.7.cloned.1.call-start = ((), (), s32[]{:S(2)}) async-start(), calls=%async_computation.40 | async-start | bytes 499712 | tf_op jit(solution)/shard_map/psum | solution.py:517
  1574.9 293.6 %reduce-scatter.43.cloned.1.call-start = ((), (), s32[]{:S(2)}) async-start(), calls=%async_computation.41 | async-start | bytes 4718592
  (123 other events, 4707.2 us)
Sparse Core Ops, SparseCore 0:
  11.8 52.6 all-gather.16
  94.9 27.7 all-gather.20
  130.0 47.6 reduce-scatter.22
  209.2 49.9 all-gather.22
  349.3 47.7 reduce-scatter.24
  426.5 49.9 all-gather.30
  512.6 46.4 reduce-scatter.26
  590.2 49.9 all-gather.34
  675.8 47.6 reduce-scatter.28
  730.5 49.3 all-gather.40
  793.4 46.4 reduce-scatter.30
  845.6 49.3 all-gather.42
  1130.8 46.4 reduce-scatter.32
  1184.6 49.3 all-gather.44
  1307.3 31.5 reduce-scatter.34
  1341.4 32.7 reduce-scatter.36
  1380.6 47.7 reduce-scatter.38
  1433.1 49.3 all-gather.46
  1496.1 46.4 reduce-scatter.40
  1545.8 50.5 reduce-scatter.48
  1599.6 38.3 reduce-scatter.46
  1641.3 41.0 reduce-scatter.44
  1688.4 125.8 all-reduce.6
  1817.6 50.8 reduce-scatter.42
  (7 shorter events, 178.8 us)

commit v3 on v2

--- a/solution.py
+++ b/solution.py
@@ -53,6 +53,10 @@
 
 def weight_sum(left_reach, right_reach):
     return jnp.einsum("zbt,zbm->tm", left_reach, right_reach, preferred_element_type=jnp.float32)
+
+
+def together(*values):
+    return lax.optimization_barrier(values)
 
 
 def widen(normed):
@@ -294,6 +298,7 @@
     in_bias_grad = jnp.sum(grad_pre.astype(jnp.float32), axis=(0, 1))
     in_grad = weight_sum(wide_rows, grad_pre)
     grad_normed = narrow_grad(rows_out(grad_pre, weight_in))
+    grad_normed, in_grad, out_grad = together(grad_normed, in_grad, out_grad)
     grad_in, gain_grad, shift_grad = norm_backward(grad_normed, standard, inverse, norm_gain)
     return (
         grad_stream + grad_in,
@@ -301,7 +306,7 @@
     )
 
 
-def attn_forward(stream, norm_gain, norm_shift, weights, biases, rel_table, ctx_rank):
+def attn_forward(stream, norm_gain, norm_shift, weights, biases, rel_table, ctx_rank, late_shard):
     query_w, key_w, value_w, out_w = weights
     query_b, value_b, out_b = biases
     normed, standard, inverse = norm_forward(stream, norm_gain, norm_shift)
@@ -313,24 +318,29 @@
         lax.all_gather(keys_local, "ctx", axis=1, tiled=True),
         lax.all_gather(values_local, "ctx", axis=1, tiled=True),
     )
+    keys_all, values_all, late_shard = together(keys_all, values_all, late_shard)
+    late = gather_rows(late_shard)
     reach = rel_table.shape[0] - 1 - LEFT
     mixed_token_rows, log_total = attend(
         queries, keys_all, values_all, wide_table(rel_table), reach, ctx_rank * queries.shape[1]
     )
+    mixed_token_rows, late = together(mixed_token_rows, late)
     branch = narrow(rows_out(mixed_token_rows, out_w)) + out_b
     return (
         stream + branch,
         (standard, inverse, wide_rows, queries, keys_all, values_all, mixed_token_rows, log_total),
-    )
-
-
-def attn_backward(grad_stream, saved, norm_gain, weights, rel_table, ctx_rank):
+        late,
+    )
+
+
+def attn_backward(grad_stream, saved, norm_gain, weights, rel_table, ctx_rank, inner_grads):
     query_w, key_w, value_w, out_w = weights
     standard, inverse, wide_rows, queries, keys_all, values_all, mixed_token_rows, log_total = saved
     grad_branch = grad_stream.astype(jnp.bfloat16)
     out_bias_grad = jnp.sum(grad_branch.astype(jnp.float32), axis=(0, 1))
-    wide_grad = widen_grad(grad_branch)
-    out_grad = weight_sum(wide_grad, mixed_token_rows)
+    inner = jnp.concatenate([grad.astype(jnp.bfloat16) for grad in inner_grads], axis=1)
+    wide_grad, inner = together(widen_grad(grad_branch), inner)
+    inner = lax.psum_scatter(inner, ("fsdp", "ctx"), scatter_dimension=0, tiled=True)
     grad_mixed = rows_in(wide_grad, out_w).astype(jnp.bfloat16)
     reach = rel_table.shape[0] - 1 - LEFT
     query_low, key_terms, value_terms, table_turned = attend_back(
@@ -343,6 +353,9 @@
         reach,
         ctx_rank * queries.shape[1],
     )
+    query_low, key_terms, value_terms, inner = together(query_low, key_terms, value_terms, inner)
+    out_grad = weight_sum(wide_grad, mixed_token_rows)
+    inner_parts = split_columns(inner, inner_grads)
     table_grad = table_turned[:, LEFT : LEFT + rel_table.shape[0]].T
     key_grad, value_grad = (
         lax.psum_scatter(key_terms, "ctx", scatter_dimension=1, tiled=True),
@@ -357,6 +370,9 @@
     value_w_grad = weight_sum(wide_rows, value_low)
     grad_normed = narrow_grad(
         rows_out(query_low, query_w) + rows_out(key_low, key_w) + rows_out(value_low, value_w)
+    )
+    grad_normed, out_grad, query_w_grad, key_w_grad, value_w_grad = together(
+        grad_normed, out_grad, query_w_grad, key_w_grad, value_w_grad
     )
     grad_in, gain_grad, shift_grad = norm_backward(grad_normed, standard, inverse, norm_gain)
     return (
@@ -373,6 +389,7 @@
             out_bias_grad,
             table_grad,
         ),
+        inner_parts,
     )
 
 
@@ -418,6 +435,62 @@
             inner_pre,
         ),
     )
+
+
+def taps_back_kernel(depth_ref, grad_ref, padded_ref, gated_ref, depth_grad_ref, wide):
+    taps = depth_ref.shape[0]
+    rows, width = gated_ref.shape[1:]
+    step = 64
+
+    @pl.when(pl.program_id(0) == 0)
+    def _():
+        depth_grad_ref[...] = jnp.zeros_like(depth_grad_ref)
+
+    wide[: padded_ref.shape[1], :] = padded_ref[0].astype(jnp.float32)
+    for lane in range(0, width, 128):
+        lanes = slice(lane, lane + 128)
+        for start in range(0, rows, step):
+            own = grad_ref[0, start : start + step, lanes]
+            total = jnp.zeros((step, 128), jnp.float32)
+            for tap in range(taps):
+                first = start + taps - 1 - tap
+                total += depth_ref[tap : tap + 1, lanes] * grad_ref[0, first : first + step, lanes]
+                product = own * wide[start + tap : start + tap + step, lanes]
+                depth_grad_ref[8 * tap : 8 * tap + 8, lanes] += jnp.sum(
+                    product.reshape(step // 8, 8, 128), axis=0
+                )
+            gated_ref[0, start : start + step, lanes] = total
+
+
+def taps_back(grad_conv, ahead, padded, depth_local):
+    slots, rows, width = grad_conv.shape
+    taps = depth_local.shape[0]
+    spare = -(rows + taps - 1) % 8
+    reach = jnp.concatenate(
+        [grad_conv, ahead, jnp.zeros((slots, spare, width), jnp.float32)], axis=1
+    )
+    held = jnp.pad(padded, ((0, 0), (0, spare), (0, 0)))
+    by_slot = lambda count: pl.BlockSpec((1, count, width), lambda s: (s, 0, 0))
+    gated, depth_sums = pl.pallas_call(
+        taps_back_kernel,
+        out_shape=(
+            jax.ShapeDtypeStruct((slots, rows, width), jnp.float32),
+            jax.ShapeDtypeStruct((8 * taps, width), jnp.float32),
+        ),
+        grid=(slots,),
+        in_specs=[
+            pl.BlockSpec((taps, width), lambda s: (0, 0)),
+            by_slot(reach.shape[1]),
+            by_slot(held.shape[1]),
+        ],
+        out_specs=(by_slot(rows), pl.BlockSpec((8 * taps, width), lambda s: (0, 0))),
+        scratch_shapes=[pltpu.VMEM((held.shape[1], width), jnp.float32)],
+        cost_estimate=pl.CostEstimate(
+            flops=4 * taps * slots * rows * width, bytes_accessed=4 << 20, transcendentals=0
+        ),
+        name="taps_back",
+    )(depth_local, reach, held)
+    return gated, jnp.sum(depth_sums.reshape(taps, 8, width), axis=1)
 
 
 def conv_backward(grad_stream, saved, norm_gain, weights, depth_local, inner_gain):
@@ -450,30 +523,17 @@
     row_count = grad_conv.shape[1]
     tap_count = depth_local.shape[0]
     reach_rows = tap_count - 1
-    padded_float = padded.astype(jnp.float32)
-    depth_grad = jnp.stack(
-        [
-            jnp.sum(grad_conv * padded_float[:, tap_index : tap_index + row_count, :], axis=(0, 1))
-            for tap_index in range(tap_count)
-        ]
-    )
-    grad_padded = jnp.zeros(padded.shape, jnp.float32)
-    for tap_index in range(tap_count):
-        grad_padded = grad_padded.at[:, tap_index : tap_index + row_count, :].add(
-            depth_local[tap_index] * grad_conv
-        )
-    back_halo = from_behind(grad_padded[:, :reach_rows, :].astype(jnp.bfloat16), "ctx", -1).astype(
-        jnp.float32
-    )
-    grad_gated = grad_padded[:, reach_rows:, :] + jnp.pad(
-        back_halo, ((0, 0), (row_count - reach_rows, 0), (0, 0))
-    )
+    ahead = from_behind(grad_conv[:, :reach_rows, :].astype(jnp.bfloat16), "ctx", -1)
+    grad_gated, depth_grad = taps_back(grad_conv, ahead.astype(jnp.float32), padded, depth_local)
     gate_sig = jax.nn.sigmoid(part_gate)
     grad_value = (grad_gated * gate_sig).astype(jnp.bfloat16)
     grad_gate = (grad_gated * part_value * gate_sig * (1.0 - gate_sig)).astype(jnp.bfloat16)
     value_w_grad = weight_sum(wide_rows, grad_value)
     gate_w_grad = weight_sum(wide_rows, grad_gate)
     grad_normed = narrow_grad(rows_out(grad_value, value_w) + rows_out(grad_gate, gate_w))
+    grad_normed, out_grad, value_w_grad, gate_w_grad = together(
+        grad_normed, out_grad, value_w_grad, gate_w_grad
+    )
     grad_in, gain_grad, shift_grad = norm_backward(grad_normed, standard, inverse, norm_gain)
     return (
         grad_stream + grad_in,
@@ -497,6 +557,10 @@
 def scatter_sum(*grads):
     joined = jnp.concatenate([grad.astype(jnp.bfloat16) for grad in grads], axis=1)
     part = lax.psum_scatter(joined, ("fsdp", "ctx"), scatter_dimension=0, tiled=True)
+    return split_columns(part, grads)
+
+
+def split_columns(part, grads):
     pieces = []
     start = 0
     for grad in grads:
@@ -505,24 +569,28 @@
     return tuple(pieces)
 
 
-def sum_small(whole_parts, split_parts, tp_rank):
+def scatter_sum_all(grads, whole_parts, split_parts, own_sum):
+    rows = grads[0].shape[0]
+    flat = jnp.concatenate([part.reshape(-1) for part in whole_parts + split_parts])
+    columns = -(-flat.shape[0] // rows)
+    flat = jnp.pad(flat, (0, rows * columns - flat.shape[0])).reshape(rows, columns)
+    parts = scatter_sum(*grads, jnp.pad(flat, ((0, 0), (0, -columns % 128))))
+    small = parts[-1][:, :columns].reshape(-1)
+    held = small.shape[0]
+    sent = jnp.concatenate([small, own_sum.reshape(1)])
+    sent = jnp.pad(sent, (0, -sent.shape[0] % 128)).reshape(1, -1, 128)
     tp_count = lax.axis_size("tp")
-    split = jnp.concatenate([part.reshape(-1) for part in split_parts])
-    spread = lax.dynamic_update_slice(
-        jnp.zeros((tp_count, split.shape[0]), jnp.float32), split[None], (tp_rank, 0)
-    )
-    flat = jnp.concatenate([part.reshape(-1) for part in whole_parts] + [spread.reshape(-1)])
-    count = flat.shape[0]
-    flat = jnp.pad(flat, (0, -count % 1024)).reshape(-1, 128)
-    total = lax.psum(flat, ("fsdp", "ctx", "tp")).reshape(-1)
+    every = lax.all_gather(sent, ("fsdp", "ctx", "tp"), axis=0, tiled=True)
+    every = every.reshape(-1, tp_count, sent.size)
+    by_tp = every[:, :, :held].transpose(1, 0, 2).reshape(tp_count, -1)
+    total = jnp.sum(by_tp, axis=0)
+    spread = by_tp
     whole = []
     start = 0
     for part in whole_parts:
         whole.append(total[start : start + part.size].reshape(part.shape))
         start += part.size
-    spread = total[start : start + tp_count * split.shape[0]].reshape(tp_count, -1)
     pieces = []
-    start = 0
     for part in split_parts:
         piece = spread[:, start : start + part.size]
         if part.ndim == 1:
@@ -531,8 +599,8 @@
             piece = piece.reshape((tp_count,) + part.shape)
             pieces.append(piece.transpose(1, 0, 2).reshape(part.shape[0], -1))
         start += part.size
-    w, p = whole, pieces
-    return (
+    w, p = whole + [jnp.sum(every[:, :, held])], pieces
+    return parts[:-1], (
         w[0], w[1], p[0], w[2], w[3], w[4], p[1], p[2], w[5], w[6], w[7], w[8],
         p[3], p[4], p[5], w[9], w[10], p[6], w[11], w[12], w[13], w[14],
     )
@@ -576,33 +644,27 @@
     final_shift,
 ):
     ffn1_in_all = gather_rows(ffn1_in)
-    ffn1_out_all = gather_rows(ffn1_out)
-    attn_all = gather_rows(
-        jnp.concatenate([query_weight, key_weight, value_weight, attn_out_weight], axis=1)
-    )
-    conv_all = gather_rows(
-        jnp.concatenate([conv_value_weight, conv_gate_weight, conv_out_weight], axis=1)
-    )
-    ffn2_in_all = gather_rows(ffn2_in)
-    ffn2_out_all = gather_rows(ffn2_out)
     width = query_weight.shape[1]
-    gathered = (
-        ffn1_in_all,
-        ffn1_out_all,
+    early = gather_rows(
+        jnp.concatenate(
+            [ffn1_out, query_weight, key_weight, value_weight, attn_out_weight], axis=1
+        )
+    )
+    ffn1_out_all = early[:, : ffn1_out.shape[1]]
+    attn_all = early[:, ffn1_out.shape[1] :]
+    late_shard = jnp.concatenate(
+        [ffn2_in, ffn2_out, conv_value_weight, conv_gate_weight, conv_out_weight], axis=1
+    )
+    attn_weights = (
         attn_all[:, :width],
         attn_all[:, width : 2 * width],
         attn_all[:, 2 * width : 3 * width],
         attn_all[:, 3 * width :],
-        conv_all[:, :width],
-        conv_all[:, width : 2 * width],
-        conv_all[:, 2 * width :],
-        ffn2_in_all,
-        ffn2_out_all,
     )
     tp_rank = lax.axis_index("tp")
     ctx_rank = lax.axis_index("ctx")
-    hidden_local = gathered[0].shape[1]
-    width_local = gathered[2].shape[1]
+    hidden_local = ffn1_in.shape[1]
+    width_local = width
     ffn1_bias_local = local_cut(ffn1_in_bias, tp_rank, hidden_local)
     ffn2_bias_local = local_cut(ffn2_in_bias, tp_rank, hidden_local)
     query_bias_local = local_cut(query_bias, tp_rank, width_local)
@@ -612,22 +674,31 @@
     inner_shift_local = local_cut(conv_inner_shift, tp_rank, width_local)
     stream_zero = inputs.astype(jnp.float32)
     stream_one, saved_one = ffn_forward(
-        stream_zero, ffn1_gain, ffn1_shift, gathered[0], ffn1_bias_local, gathered[1], ffn1_out_bias
-    )
-    stream_two, saved_two = attn_forward(
+        stream_zero, ffn1_gain, ffn1_shift, ffn1_in_all, ffn1_bias_local, ffn1_out_all, ffn1_out_bias
+    )
+    stream_two, saved_two, late = attn_forward(
         stream_one,
         attn_gain,
         attn_shift,
-        (gathered[2], gathered[3], gathered[4], gathered[5]),
+        attn_weights,
         (query_bias_local, value_bias_local, attn_out_bias),
         rel_table,
         ctx_rank,
+        late_shard,
+    )
+    ffn2_in_all = late[:, :hidden_local]
+    ffn2_out_all = late[:, hidden_local : 2 * hidden_local]
+    conv_all = late[:, 2 * hidden_local :]
+    conv_weights = (
+        conv_all[:, :width],
+        conv_all[:, width : 2 * width],
+        conv_all[:, 2 * width :],
     )
     stream_three, saved_three = conv_forward(
         stream_two,
         conv_gain,
         conv_shift,
-        (gathered[6], gathered[7], gathered[8]),
+        conv_weights,
         depth_local,
         inner_gain_local,
         inner_shift_local,
@@ -636,9 +707,9 @@
         stream_three,
         ffn2_gain,
         ffn2_shift,
-        gathered[9],
+        ffn2_in_all,
         ffn2_bias_local,
-        gathered[10],
+        ffn2_out_all,
         ffn2_out_bias,
     )
     final_out, final_standard, final_inverse = norm_forward(stream_four, final_gain, final_shift)
@@ -650,35 +721,32 @@
     gradient_fourth, final_gain_grad, final_shift_grad = norm_backward(
         2.0 * misfit, final_standard, final_inverse, final_gain
     )
-    back_weights = gathered
     grad_three, ffn2_grads = ffn_backward(
-        gradient_fourth, saved_four, ffn2_gain, back_weights[9], back_weights[10]
+        gradient_fourth, saved_four, ffn2_gain, ffn2_in_all, ffn2_out_all
     )
     grad_two, conv_grads = conv_backward(
         grad_three,
         saved_three,
         conv_gain,
-        (back_weights[6], back_weights[7], back_weights[8]),
+        conv_weights,
         depth_local,
         inner_gain_local,
     )
-    grad_one, attn_grads = attn_backward(
+    grad_one, attn_grads, inner_parts = attn_backward(
         grad_two,
         saved_two,
         attn_gain,
-        (back_weights[2], back_weights[3], back_weights[4], back_weights[5]),
+        attn_weights,
         rel_table,
         ctx_rank,
+        (ffn2_grads[2], ffn2_grads[4], conv_grads[2], conv_grads[3], conv_grads[7]),
     )
     grad_zero, ffn1_grads = ffn_backward(
-        grad_one, saved_one, ffn1_gain, back_weights[0], back_weights[1]
-    )
-    ffn2_parts = scatter_sum(ffn2_grads[2], ffn2_grads[4])
-    conv_parts = scatter_sum(conv_grads[2], conv_grads[3], conv_grads[7])
+        grad_one, saved_one, ffn1_gain, ffn1_in_all, ffn1_out_all
+    )
     attn_parts = scatter_sum(attn_grads[2], attn_grads[4], attn_grads[5], attn_grads[7])
-    ffn1_parts = scatter_sum(ffn1_grads[2], ffn1_grads[4])
-    weight_parts = ffn1_parts + attn_parts + conv_parts + ffn2_parts
-    shared = sum_small(
+    ffn1_parts, shared = scatter_sum_all(
+        (ffn1_grads[2], ffn1_grads[4]),
         (
             ffn1_grads[0],
             ffn1_grads[1],
@@ -694,7 +762,6 @@
             ffn2_grads[5],
             final_gain_grad,
             final_shift_grad,
-            sse_local,
         ),
         (
             ffn1_grads[3],
@@ -705,8 +772,9 @@
             conv_grads[6],
             ffn2_grads[3],
         ),
-        tp_rank,
-    )
+        sse_local,
+    )
+    weight_parts = ffn1_parts + attn_parts + inner_parts[2:] + inner_parts[:2]
     token_count = (jnp.sum(clips_dev) * SEQ).astype(jnp.float32)
     loss = shared[21] / token_count
     return (

time: 1900 us -> 1480 us (0.78)
  waiting for transfers between devices: 1220 us -> 930 us
  local copies, waits for them, and re-layouts: 223 us -> 64.8 us
  blocking collectives: 34 us -> 107 us
  other arithmetic: 142 us -> 77.5 us
    unnamed x35 -> x26, waiting for transfers between devices: 130 us -> 1.77 us
    scatter-add x27 -> x0, local copies, waits for them, and re-layouts: 126 us -> none  [conv_backward(): grad_padded.at[:, tap_index:tap_index + row_count, :]]
    psum x1 -> x0, waiting for transfers between devices: 113 us -> none  [sum_small(): total = lax.psum(flat, ('fsdp', 'ctx', 'tp')).reshape(-1)]
    all_gather x6 -> x3, waiting for transfers between devices: 144 us -> 66.3 us  [gather_rows(): return lax.all_gather(shard, ('fsdp', 'ctx'), axis=0, tiled=True)]
    all_gather x0 -> x1, blocking collectives: none -> 71.1 us  [scatter_sum_all(): every = lax.all_gather(sent, ('fsdp', 'ctx', 'tp'), axis=0, tiled=True)]
    reduce_scatter x0 -> x3, waiting for transfers between devices: none -> 61.4 us  [the longest x2 61.4 us: scatter_sum(): lax.psum_scatter(joined, ('fsdp', 'ctx'), scatter_dimension=0, tiled=True)]
    add x25 -> x0, other arithmetic: 60.8 us -> none  [conv_backward(): grad_padded.at[:, tap_index:tap_index + row_count, :]]
    unnamed x272 -> x258, local copies, waits for them, and re-layouts: 62.6 us -> 25.6 us
  transfers between devices with their start and end apart: 33 -> 28, of which waited for: 31 -> 25; matrix products, arithmetic and copies ran while one was open for 9% -> 10% of each run, Pallas kernels for 0% -> 7%
where the time goes in v3:
time: 1480 us; the launch traced here: 1460 us
  waiting for transfers between devices  930 us (63%)
  matrix products  145 us (10%)
  Pallas kernels  115 us (8%)
  blocking collectives  107 us (7%)
  other arithmetic  77.5 us (5%)
  local copies, waits for them, and re-layouts  64.8 us (4%)
  between operations  18.2 us (1%)
    all_gather x4, waiting for transfers between devices, widen(): return lax.all_gather(normed.astype(jnp.bfloat16), 'tp', axis=1, tiled=True)  195 us
    all_gather x4, waiting for transfers between devices, widen_grad(): return lax.all_gather(grad_branch, 'tp', axis=1, tiled=True)  190 us
    reduce_scatter x4, waiting for transfers between devices, narrow(): lax.psum_scatter(partial_rows.astype(jnp.bfloat16), 'tp', scatter_dimensi...  184 us
    reduce_scatter x4, waiting for transfers between devices, narrow_grad(): lax.psum_scatter(partial_rows.astype(jnp.bfloat16), 'tp', scatter_dimensi...  129 us
    all_gather x1, blocking collectives, scatter_sum_all(): every = lax.all_gather(sent, ('fsdp', 'ctx', 'tp'), axis=0, tiled=True)  71.1 us
    pallas_call x1, Pallas kernels, attend_back(): pl.pallas_call(functools.partial(attend_back_kernel, reach), out_shape=(j...  69.8 us
    all_gather x3, waiting for transfers between devices, gather_rows(): return lax.all_gather(shard, ('fsdp', 'ctx'), axis=0, tiled=True)  66.3 us
    reduce_scatter x2, waiting for transfers between devices, scatter_sum(): lax.psum_scatter(joined, ('fsdp', 'ctx'), scatter_dimension=0, tiled=True)  61.4 us
  transfers between devices with their start and end apart: 28, of which 25 were waited for; matrix products, arithmetic and copies ran while one was open for 10% of the time, Pallas kernels for 7%

profile of v3, /device:TPU:0, one launch (start us, length us, event | category | flops | bytes accessed | tf_op | source)
XLA Modules:
  0.0 1464.0 jit_solution(11948685390191527212)
XLA Ops:
  13.8 50.3 %all-gather.14.cloned.1.call-done = bf16[3,384,1024]{2,1,0:T(8,128)(2,1)} async-done(((bf16[3,96,1024]{2,1,0:T(8,128)(2,1)}), bf16[3,384,1024]{2,1,0:T(8,128)(2,1)}) %all-gather.14.cloned.1.call-update) | async-done | bytes 2359312 | tf_op jit(solution)/shard_map/all_gather | solution.py:63
  64.1 28.5 %all-gather.16.cloned.1.call-done = bf16[1024,1024]{1,0:T(8,128)(2,1)} async-done(((bf16[128,1024]{1,0:T(8,128)(2,1)}), bf16[1024,1024]{1,0:T(8,128)(2,1)}) %all-gather.16.cloned.1.call-update) | async-done | bytes 2097168 | tf_op jit(solution)/shard_map/all_gather | solution.py:554
  99.7 31.9 %all-gather.18.cloned.1.call-done = bf16[1024,2048]{1,0:T(8,128)(2,1)} async-done(((bf16[128,2048]{1,0:T(8,128)(2,1)}), bf16[1024,2048]{1,0:T(8,128)(2,1)}) %all-gather.18.cloned.1.call-update) | async-done | bytes 4194320 | tf_op jit(solution)/shard_map/all_gather | solution.py:554
  138.9 47.8 %reduce-scatter.14.cloned.1.call-done = bf16[3,96,1024]{2,1,0:T(8,128)(2,1)} async-done(((bf16[3,384,1024]{2,1,0:T(8,128)(2,1)}), bf16[3,96,1024]{2,1,0:T(8,128)(2,1)}) %reduce-scatter.14.cloned.1.call-update) | async-done | bytes 589840 | tf_op jit(solution)/shard_map/reduce_scatter | solution.py:67
  191.2 48.7 %all-gather.20.cloned.1.call-done = bf16[3,384,1024]{2,1,0:T(8,128)(2,1)} async-done(((bf16[3,96,1024]{2,1,0:T(8,128)(2,1)}), bf16[3,384,1024]{2,1,0:T(8,128)(2,1)}) %all-gather.20.cloned.1.call-update) | async-done | bytes 2359312 | tf_op jit(solution)/shard_map/all_gather | solution.py:63
  266.2 26.2 %all-gather.22.cloned.1.call-done.key_ref = bf16[3,1536,256]{2,1,0:T(8,128)(2,1)} async-done(((bf16[3,384,256]{2,1,0:T(8,128)(2,1)}), bf16[3,1536,256]{2,1,0:T(8,128)(2,1)}) %all-gather.22.cloned.1.call-update) | async-done | bytes 2359312 | tf_op jit(solution)/shard_map/all_gather | solution.py:318
  297.7 34.0 %attend.1 = (bf16[3,384,256]{2,1,0:T(8,128)(2,1)}, f32[3,384,256]{2,1,0:T(8,128)}) custom-call(s32[1]{0:T(128)} %bitcast.2.start_ref, bf16[3,384,256]{2,1,0:T(8,128)(2,1)} %fusion.35.query_ref, bf16[3,1536,256]{2,1,0:T(8,128)(2,1)} %all-gather.22.cloned.1.call-done.key_ref, bf16[3,1536,256]{2,1,0:T(8,128)(2,1)} %all-gather.24.cloned.1.call-done.value_ref, ...), custom_call_target="tpu_custom_call" | custom-call | flops 3623878656 | bytes 8388608 | tf_op jit(solution)/shard_map/attend/pallas_call | solution.py:235
  341.4 47.7 %reduce-scatter.16.cloned.1.call-done = bf16[3,96,1024]{2,1,0:T(8,128)(2,1)} async-done(((bf16[3,384,1024]{2,1,0:T(8,128)(2,1)}), bf16[3,96,1024]{2,1,0:T(8,128)(2,1)}) %reduce-scatter.16.cloned.1.call-update) | async-done | bytes 589840 | tf_op jit(solution)/shard_map/reduce_scatter | solution.py:67
  394.4 47.5 %all-gather.28.cloned.1.call-done = bf16[3,384,1024]{2,1,0:T(8,128)(2,1)} async-done(((bf16[3,96,1024]{2,1,0:T(8,128)(2,1)}), bf16[3,384,1024]{2,1,0:T(8,128)(2,1)}) %all-gather.28.cloned.1.call-update) | async-done | bytes 2359312 | tf_op jit(solution)/shard_map/all_gather | solution.py:63
  483.7 45.7 %reduce-scatter.18.cloned.1.call-done = bf16[3,96,1024]{2,1,0:T(8,128)(2,1)} async-done(((bf16[3,384,1024]{2,1,0:T(8,128)(2,1)}), bf16[3,96,1024]{2,1,0:T(8,128)(2,1)}) %reduce-scatter.18.cloned.1.call-update) | async-done | bytes 589840 | tf_op jit(solution)/shard_map/reduce_scatter | solution.py:67
  533.7 48.8 %all-gather.30.cloned.1.call-done = bf16[3,384,1024]{2,1,0:T(8,128)(2,1)} async-done(((bf16[3,96,1024]{2,1,0:T(8,128)(2,1)}), bf16[3,384,1024]{2,1,0:T(8,128)(2,1)}) %all-gather.30.cloned.1.call-update) | async-done | bytes 2359312 | tf_op jit(solution)/shard_map/all_gather | solution.py:63
  598.7 43.2 %reduce-scatter.20.cloned.1.call-done = bf16[3,96,1024]{2,1,0:T(8,128)(2,1)} async-done(((bf16[3,384,1024]{2,1,0:T(8,128)(2,1)}), bf16[3,96,1024]{2,1,0:T(8,128)(2,1)}) %reduce-scatter.20.cloned.1.call-update) | async-done | bytes 589840 | tf_op jit(solution)/shard_map/reduce_scatter | solution.py:67
  648.7 49.5 %all-gather.32.cloned.1.call-done = bf16[3,384,1024]{2,1,0:T(8,128)(2,1)} async-done(((bf16[3,96,1024]{2,1,0:T(8,128)(2,1)}), bf16[3,384,1024]{2,1,0:T(8,128)(2,1)}) %all-gather.32.cloned.1.call-update) | async-done | bytes 2359312 | tf_op jit(solution)/shard_map/all_gather | solution.py:73
  726.8 32.8 %reduce-scatter.22.cloned.1.call-done = bf16[3,96,1024]{2,1,0:T(8,128)(2,1)} async-done(((bf16[3,384,1024]{2,1,0:T(8,128)(2,1)}), bf16[3,96,1024]{2,1,0:T(8,128)(2,1)}) %reduce-scatter.22.cloned.1.call-update) | async-done | bytes 589840 | tf_op jit(solution)/shard_map/reduce_scatter | solution.py:77
  764.8 49.4 %all-gather.34.cloned.1.call-done = bf16[3,384,1024]{2,1,0:T(8,128)(2,1)} async-done(((bf16[3,96,1024]{2,1,0:T(8,128)(2,1)}), bf16[3,384,1024]{2,1,0:T(8,128)(2,1)}) %all-gather.34.cloned.1.call-update) | async-done | bytes 2359312 | tf_op jit(solution)/shard_map/all_gather | solution.py:73
  872.4 39.1 %reduce-scatter.24.cloned.1.call-done = bf16[3,96,1024]{2,1,0:T(8,128)(2,1)} async-done(((bf16[3,384,1024]{2,1,0:T(8,128)(2,1)}), bf16[3,96,1024]{2,1,0:T(8,128)(2,1)}) %reduce-scatter.24.cloned.1.call-update) | async-done | bytes 589840 | tf_op jit(solution)/shard_map/reduce_scatter | solution.py:77
  924.0 41.5 %all-gather.36.cloned.1.call-done = bf16[3,384,1024]{2,1,0:T(8,128)(2,1)} async-done(((bf16[3,96,1024]{2,1,0:T(8,128)(2,1)}), bf16[3,384,1024]{2,1,0:T(8,128)(2,1)}) %all-gather.36.cloned.1.call-update) | async-done | bytes 2359312 | tf_op jit(solution)/shard_map/all_gather | solution.py:73
  969.3 69.8 %attend_back.1 = (bf16[3,384,256]{2,1,0:T(8,128)(2,1)}, bf16[3,1536,256]{2,1,0:T(8,128)(2,1)}, bf16[3,1536,256]{2,1,0:T(8,128)(2,1)}, f32[64,384]{1,0:T(8,128)}) custom-call(s32[1]{0:T(128)} %bitcast.2.start_ref, bf16[3,384,256]{2,1,0:T(8,128)(2,1)} %fusion.35.query_ref, bf16[3,1536,256]{2,1,0:T(8,128)(2,1)} %all-gather.22.cloned.1.call-done.key_ref, ...), custom_call_target="tpu_custom_call" | custom-call | flops 9059696640 | bytes 16777216 | tf_op jit(solution)/shard_map/attend_back/pallas_call | solution.py:256
  1044.3 26.6 %reduce-scatter.28.cloned.1.call-done = bf16[3,384,256]{2,1,0:T(8,128)(2,1)} async-done(((bf16[3,1536,256]{2,1,0:T(8,128)(2,1)}), bf16[3,384,256]{2,1,0:T(8,128)(2,1)}) %reduce-scatter.28.cloned.1.call-update) | async-done | bytes 589840 | tf_op jit(solution)/shard_map/reduce_scatter | solution.py:361
  1075.1 31.1 %reduce-scatter.30.cloned.1.call-done = bf16[3,384,256]{2,1,0:T(8,128)(2,1)} async-done(((bf16[3,1536,256]{2,1,0:T(8,128)(2,1)}), bf16[3,384,256]{2,1,0:T(8,128)(2,1)}) %reduce-scatter.30.cloned.1.call-update) | async-done | bytes 589840 | tf_op jit(solution)/shard_map/reduce_scatter | solution.py:362
  1122.3 38.3 %reduce-scatter.32.cloned.1.call-done = bf16[3,96,1024]{2,1,0:T(8,128)(2,1)} async-done(((bf16[3,384,1024]{2,1,0:T(8,128)(2,1)}), bf16[3,96,1024]{2,1,0:T(8,128)(2,1)}) %reduce-scatter.32.cloned.1.call-update) | async-done | bytes 589840 | tf_op jit(solution)/shard_map/reduce_scatter | solution.py:77
  1165.2 49.3 %all-gather.38.cloned.1.call-done = bf16[3,384,1024]{2,1,0:T(8,128)(2,1)} async-done(((bf16[3,96,1024]{2,1,0:T(8,128)(2,1)}), bf16[3,384,1024]{2,1,0:T(8,128)(2,1)}) %all-gather.38.cloned.1.call-update) | async-done | bytes 2359312 | tf_op jit(solution)/shard_map/all_gather | solution.py:73
  1324.8 49.6 %reduce-scatter.36.cloned.1.call-done = bf16[128,2176]{1,0:T(8,128)(2,1)} async-done(((bf16[1024,2176]{1,0:T(8,128)(2,1)}), bf16[128,2176]{1,0:T(8,128)(2,1)}) %reduce-scatter.36.cloned.1.call-update) | async-done | bytes 557072 | tf_op jit(solution)/shard_map/reduce_scatter | solution.py:559
  1376.0 71.1 %all_gather.55 = f32[32,30,128]{2,1,0:T(8,128)S(1)} all-gather(f32[1,30,128]{2,1,0:T(8,128)S(1)} %fusion.93), channel_id=1, replica_groups=mesh['fsdp'=2,'ctx'=4,'tp'=4] {'fsdp','ctx','tp'}, dimensions={0}, use_global_device_ids=true | all-gather | bytes 506880 | tf_op jit(solution)/shard_map/all_gather | solution.py:583
  (464 shorter events, 397.4 us)
Async XLA Ops:
  11.2 81.3 %all-gather.16.cloned.1.call-start = ((), (), s32[]{:S(2)}) async-start(), calls=%async_computation.14 | async-start | bytes 2359296 | tf_op jit(solution)/shard_map/all_gather | solution.py:554
  12.0 119.6 %all-gather.18.cloned.1.call-start = ((), (), s32[]{:S(2)}) async-start(), calls=%async_computation.15 | async-start | bytes 4718592 | tf_op jit(solution)/shard_map/all_gather | solution.py:554
  13.0 173.7 %reduce-scatter.14.cloned.1.call-start = ((), (), s32[]{:S(2)}) async-start(), calls=%async_computation.16 | async-start | bytes 2949120 | tf_op jit(solution)/shard_map/reduce_scatter | solution.py:67
  138.9 101.0 %all-gather.20.cloned.1.call-start = ((), (), s32[]{:S(2)}) async-start(), calls=%async_computation.17 | async-start | bytes 2949120 | tf_op jit(solution)/shard_map/all_gather | solution.py:63
  190.4 75.8 %all-gather.24.cloned.1.call-start = ((), (), s32[]{:S(2)}) async-start(), calls=%async_computation.19 | async-start | bytes 2949120 | tf_op jit(solution)/shard_map/all_gather | solution.py:319
  246.8 90.8 %all-gather.26.cloned.1.call-start = ((), (), s32[]{:S(2)}) async-start(), calls=%async_computation.20 | async-start | bytes 6488064 | tf_op jit(solution)/shard_map/all_gather | solution.py:554
  292.5 96.6 %reduce-scatter.16.cloned.1.call-start = ((), (), s32[]{:S(2)}) async-start(), calls=%async_computation.21 | async-start | bytes 2949120 | tf_op jit(solution)/shard_map/reduce_scatter | solution.py:67
  341.1 100.8 %all-gather.28.cloned.1.call-start = ((), (), s32[]{:S(2)}) async-start(), calls=%async_computation.22 | async-start | bytes 2949120 | tf_op jit(solution)/shard_map/all_gather | solution.py:63
  392.4 137.0 %reduce-scatter.18.cloned.1.call-start = ((), (), s32[]{:S(2)}) async-start(), calls=%async_computation.23 | async-start | bytes 2949120 | tf_op jit(solution)/shard_map/reduce_scatter | solution.py:67
  483.6 98.9 %all-gather.30.cloned.1.call-start = ((), (), s32[]{:S(2)}) async-start(), calls=%async_computation.24 | async-start | bytes 2949120 | tf_op jit(solution)/shard_map/all_gather | solution.py:63
  533.0 108.9 %reduce-scatter.20.cloned.1.call-start = ((), (), s32[]{:S(2)}) async-start(), calls=%async_computation.25 | async-start | bytes 2949120 | tf_op jit(solution)/shard_map/reduce_scatter | solution.py:67
  595.2 103.0 %all-gather.32.cloned.1.call-start = ((), (), s32[]{:S(2)}) async-start(), calls=%async_computation.26 | async-start | bytes 2949120 | tf_op jit(solution)/shard_map/all_gather | solution.py:73
  648.7 111.0 %reduce-scatter.22.cloned.1.call-start = ((), (), s32[]{:S(2)}) async-start(), calls=%async_computation.27 | async-start | bytes 2949120 | tf_op jit(solution)/shard_map/reduce_scatter | solution.py:77
  713.0 101.3 %all-gather.34.cloned.1.call-start = ((), (), s32[]{:S(2)}) async-start(), calls=%async_computation.28 | async-start | bytes 2949120 | tf_op jit(solution)/shard_map/all_gather | solution.py:73
  764.8 146.8 %reduce-scatter.24.cloned.1.call-start = ((), (), s32[]{:S(2)}) async-start(), calls=%async_computation.29 | async-start | bytes 2949120 | tf_op jit(solution)/shard_map/reduce_scatter | solution.py:77
  865.0 100.5 %all-gather.36.cloned.1.call-start = ((), (), s32[]{:S(2)}) async-start(), calls=%async_computation.30 | async-start | bytes 2949120 | tf_op jit(solution)/shard_map/all_gather | solution.py:73
  915.9 123.2 %reduce-scatter.26.cloned.1.call-start = ((), (), s32[]{:S(2)}) async-start(), calls=%async_computation.31 | async-start | bytes 6488064 | tf_op jit(solution)/shard_map/reduce_scatter | solution.py:343
  965.5 105.4 %reduce-scatter.28.cloned.1.call-start = ((), (), s32[]{:S(2)}) async-start(), calls=%async_computation.32 | async-start | bytes 2949120 | tf_op jit(solution)/shard_map/reduce_scatter | solution.py:361
  1039.2 67.0 %reduce-scatter.30.cloned.1.call-start = ((), (), s32[]{:S(2)}) async-start(), calls=%async_computation.33 | async-start | bytes 2949120 | tf_op jit(solution)/shard_map/reduce_scatter | solution.py:362
  1039.9 120.6 %reduce-scatter.32.cloned.1.call-start = ((), (), s32[]{:S(2)}) async-start(), calls=%async_computation.34 | async-start | bytes 2949120 | tf_op jit(solution)/shard_map/reduce_scatter | solution.py:77
  1112.6 101.9 %all-gather.38.cloned.1.call-start = ((), (), s32[]{:S(2)}) async-start(), calls=%async_computation.35 | async-start | bytes 2949120 | tf_op jit(solution)/shard_map/all_gather | solution.py:73
  1165.0 109.7 %reduce-scatter.34.cloned.1.call-start = ((), (), s32[]{:S(2)}) async-start(), calls=%async_computation.36 | async-start | bytes 2949120 | tf_op jit(solution)/shard_map/reduce_scatter | solution.py:77
  1228.1 90.4 %reduce-scatter.38.cloned.1.call-start = ((), (), s32[]{:S(2)}) async-start(), calls=%async_computation.38 | async-start | bytes 2359296 | tf_op jit(solution)/shard_map/reduce_scatter | solution.py:559
  1231.3 143.1 %reduce-scatter.36.cloned.1.call-start = ((), (), s32[]{:S(2)}) async-start(), calls=%async_computation.37 | async-start | bytes 5013504 | tf_op jit(solution)/shard_map/reduce_scatter | solution.py:559
  (121 other events, 1115.4 us)
Sparse Core Ops, SparseCore 0:
  11.3 52.6 all-gather.13
  66.0 26.5 all-gather.15
  95.0 36.5 all-gather.17
  139.0 47.6 reduce-scatter.13
  190.5 49.3 all-gather.19
  294.3 43.1 all-gather.25
  341.2 47.8 reduce-scatter.15
  392.5 49.3 all-gather.27
  483.7 45.6 reduce-scatter.17
  533.1 49.3 all-gather.29
  595.3 46.4 reduce-scatter.19
  648.8 49.3 all-gather.31
  713.1 46.4 reduce-scatter.21
  764.9 49.3 all-gather.33
  865.1 46.3 reduce-scatter.23
  916.1 49.3 all-gather.35
  968.9 57.7 reduce-scatter.25
  1039.3 31.5 reduce-scatter.27
  1073.4 32.7 reduce-scatter.29
  1112.8 47.7 reduce-scatter.31
  1165.1 49.3 all-gather.37
  1228.2 46.4 reduce-scatter.33
  1278.0 40.4 reduce-scatter.37
  1321.8 52.5 reduce-scatter.35
  (2 shorter events, 46.7 us)

commit v4 on v3

--- a/solution.py
+++ b/solution.py
@@ -153,8 +153,8 @@
 
 
 def attend_back_kernel(
-    reach, start_ref, query_ref, key_ref, value_ref, table_ref, total_ref, grad_ref,
-    query_grad_ref, key_grad_ref, value_grad_ref, table_grad_ref, place, key_sum, value_sum,
+    reach, start_ref, query_ref, key_ref, value_ref, table_ref, total_ref, grad_ref, groups_ref,
+    query_grad_ref, pair_grad_ref, table_grad_ref, place, key_sum, value_sum,
 ):
     rows = query_ref.shape[1]
     key_count = key_ref.shape[1]
@@ -186,17 +186,17 @@
         key_sum[lanes, :] += dot_n(query_block.T, grad_scores)
         wide = grad_scores.astype(jnp.float32)
         place[:, 128 : 128 + key_count] = wide
-        apart_all = (
-            lax.broadcasted_iota(jnp.int32, wide.shape, 1)
-            - lax.broadcasted_iota(jnp.int32, wide.shape, 0)
-            - rows_at
-        )
-        far_left = jnp.sum(jnp.where(apart_all <= -LEFT, wide, 0.0), axis=-1, keepdims=True)
-        far_right = jnp.sum(jnp.where(apart_all >= reach, wide, 0.0), axis=-1, keepdims=True)
         window = place[:, pl.ds(pl.multiple_of(rows_at, 128), BAND)]
         window_col = lax.broadcasted_iota(jnp.int32, window.shape, 1) + rows_at - 128
+        window = jnp.where((window_col >= 0) & (window_col < key_count), window, 0.0)
         apart = band_distance(rows)
-        inside = (apart > -LEFT) & (apart < reach) & (window_col >= 0) & (window_col < key_count)
+        by_group = dot_n(grad_scores, groups_ref[...])
+        past = lax.broadcasted_iota(jnp.int32, by_group.shape, 1) * 128 - rows_at
+        far_left = jnp.sum(jnp.where(past < -128, by_group, 0.0), axis=-1, keepdims=True)
+        far_left += jnp.sum(jnp.where(apart <= -LEFT, window, 0.0), axis=-1, keepdims=True)
+        far_right = jnp.sum(jnp.where(past >= BAND - 128, by_group, 0.0), axis=-1, keepdims=True)
+        far_right += jnp.sum(jnp.where(apart >= reach, window, 0.0), axis=-1, keepdims=True)
+        inside = (apart > -LEFT) & (apart < reach)
         turned = jnp.where(inside, window, 0.0)
         row = lax.broadcasted_iota(jnp.int32, turned.shape, 0)
         for bit in range((rows - 1).bit_length()):
@@ -213,8 +213,8 @@
 
     @pl.when(block == pl.num_programs(2) - 1)
     def _():
-        key_grad_ref[0] = key_sum[...].T.astype(jnp.bfloat16)
-        value_grad_ref[0] = value_sum[...].T.astype(jnp.bfloat16)
+        pair_grad_ref[0, 0] = key_sum[...].T.astype(jnp.bfloat16)
+        pair_grad_ref[1, 0] = value_sum[...].T.astype(jnp.bfloat16)
 
 
 def attend_specs(queries, keys):
@@ -224,14 +224,17 @@
     grid = (slots, width // lanes, rows // block)
     by_query = pl.BlockSpec((1, block, lanes), lambda s, p, b, *_: (s, b, p))
     by_key = pl.BlockSpec((1, keys.shape[1], lanes), lambda s, p, b, *_: (s, 0, p))
+    by_value = pl.BlockSpec(
+        (1, keys.shape[1], lanes), lambda s, p, b, *_: (s, 0, p + width // lanes)
+    )
     table = pl.BlockSpec((BAND, HEAD), lambda s, p, b, *_: (0, 0))
     place = pltpu.VMEM((block, keys.shape[1] + 256), jnp.float32)
     flops = slots * rows * keys.shape[1] * width * 4
-    return grid, by_query, by_key, table, place, flops
-
-
-def attend(queries, keys, values, table, reach, query_start):
-    grid, by_query, by_key, by_table, place, flops = attend_specs(queries, keys)
+    return grid, by_query, by_key, by_value, table, place, flops
+
+
+def attend(queries, pairs, table, reach, query_start):
+    grid, by_query, by_key, by_value, by_table, place, flops = attend_specs(queries, pairs)
     return pl.pallas_call(
         functools.partial(attend_kernel, reach),
         out_shape=(
@@ -241,41 +244,50 @@
         grid_spec=pltpu.PrefetchScalarGridSpec(
             num_scalar_prefetch=1,
             grid=grid,
-            in_specs=[by_query, by_key, by_key, by_table],
+            in_specs=[by_query, by_key, by_value, by_table],
             out_specs=(by_query, by_query),
             scratch_shapes=[place],
         ),
         cost_estimate=pl.CostEstimate(flops=2 * flops, bytes_accessed=8 << 20, transcendentals=flops >> 8),
         name="attend",
-    )(query_start.reshape(1), queries, keys, values, table)
-
-
-def attend_back(queries, keys, values, table, totals, grad_mixed, reach, query_start):
-    grid, by_query, by_key, by_table, place, flops = attend_specs(queries, keys)
-    turned = pltpu.VMEM((2 * HEAD, keys.shape[1]), jnp.float32)
+    )(query_start.reshape(1), queries, pairs, pairs, table)
+
+
+def attend_back(queries, pairs, table, totals, grad_mixed, reach, query_start):
+    grid, by_query, by_key, by_value, by_table, place, flops = attend_specs(queries, pairs)
+    slots, key_count = pairs.shape[:2]
+    turned = pltpu.VMEM((2 * HEAD, key_count), jnp.float32)
+    group = jnp.arange(key_count, dtype=jnp.int32)[:, None] // 128
+    groups = (group == jnp.arange(128, dtype=jnp.int32)[None, :]).astype(jnp.bfloat16)
     return pl.pallas_call(
         functools.partial(attend_back_kernel, reach),
         out_shape=(
             jax.ShapeDtypeStruct(queries.shape, jnp.bfloat16),
-            jax.ShapeDtypeStruct(keys.shape, jnp.bfloat16),
-            jax.ShapeDtypeStruct(keys.shape, jnp.bfloat16),
+            jax.ShapeDtypeStruct((2, slots, key_count, queries.shape[2]), jnp.bfloat16),
             jax.ShapeDtypeStruct((HEAD, BAND), jnp.float32),
         ),
         grid_spec=pltpu.PrefetchScalarGridSpec(
             num_scalar_prefetch=1,
             grid=grid,
-            in_specs=[by_query, by_key, by_key, by_table, by_query, by_query],
+            in_specs=[
+                by_query,
+                by_key,
+                by_value,
+                by_table,
+                by_query,
+                by_query,
+                pl.BlockSpec((key_count, 128), lambda s, p, b, *_: (0, 0)),
+            ],
             out_specs=(
                 by_query,
-                by_key,
-                by_key,
+                pl.BlockSpec((2, 1, key_count, 2 * HEAD), lambda s, p, b, *_: (0, s, 0, p)),
                 pl.BlockSpec((HEAD, BAND), lambda s, p, b, *_: (0, 0)),
             ),
             scratch_shapes=[place, turned, turned],
         ),
         cost_estimate=pl.CostEstimate(flops=5 * flops, bytes_accessed=16 << 20, transcendentals=flops >> 8),
         name="attend_back",
-    )(query_start.reshape(1), queries, keys, values, table, totals, grad_mixed)
+    )(query_start.reshape(1), queries, pairs, pairs, table, totals, grad_mixed, groups)
 
 
 def ffn_forward(stream, norm_gain, norm_shift, weight_in, bias_in, weight_out, bias_out):
@@ -285,6 +297,30 @@
     active = jax.nn.silu(hidden_pre).astype(jnp.bfloat16)
     branch = narrow(rows_out(active, weight_out)) + bias_out
     return (stream + 0.5 * branch, (standard, inverse, wide_rows, hidden_pre))
+
+
+def ffn_forward_first(
+    stream, norm_gain, norm_shift, shard_in, bias_in, shard_out, bias_out, later_shards
+):
+    normed, standard, inverse = norm_forward(stream, norm_gain, norm_shift)
+    normed, shard_in = together(normed.astype(jnp.bfloat16), shard_in)
+    wide_rows = widen(normed)
+    pieces = [
+        gather_rows(shard_in[:, start : start + 256]) for start in range(0, shard_in.shape[1], 256)
+    ]
+    wide_rows, shard_out, *pieces = together(wide_rows, shard_out, *pieces)
+    weight_out = gather_rows(shard_out)
+    weight_in = jnp.concatenate(pieces, axis=1)
+    hidden_pre = rows_in(wide_rows, weight_in) + bias_in
+    active = jax.nn.silu(hidden_pre).astype(jnp.bfloat16)
+    partial_rows = rows_out(active, weight_out).astype(jnp.bfloat16)
+    partial_rows, *later_shards = together(partial_rows, *later_shards)
+    later = [gather_rows(shard) for shard in later_shards]
+    summed = lax.psum_scatter(partial_rows, "tp", scatter_dimension=1, tiled=True)
+    summed, *later = together(summed, *later)
+    branch = summed.astype(jnp.float32) + bias_out
+    saved = (standard, inverse, wide_rows, hidden_pre)
+    return (stream + 0.5 * branch, saved, weight_in, weight_out, later)
 
 
 def ffn_backward(grad_stream, saved, norm_gain, weight_in, weight_out):
@@ -312,30 +348,28 @@
     normed, standard, inverse = norm_forward(stream, norm_gain, norm_shift)
     wide_rows = widen(normed)
     queries = (rows_in(wide_rows, query_w) + query_b).astype(jnp.bfloat16)
-    keys_local = rows_in(wide_rows, key_w).astype(jnp.bfloat16)
-    values_local = (rows_in(wide_rows, value_w) + value_b).astype(jnp.bfloat16)
-    keys_all, values_all = (
-        lax.all_gather(keys_local, "ctx", axis=1, tiled=True),
-        lax.all_gather(values_local, "ctx", axis=1, tiled=True),
-    )
-    keys_all, values_all, late_shard = together(keys_all, values_all, late_shard)
+    pair_b = jnp.concatenate([jnp.zeros_like(value_b), value_b])
+    pair_w = jnp.concatenate([key_w, value_w], axis=1)
+    pairs = (rows_in(wide_rows, pair_w) + pair_b).astype(jnp.bfloat16)
+    pairs_all = lax.all_gather(pairs, "ctx", axis=1, tiled=True)
+    pairs_all, late_shard = together(pairs_all, late_shard)
     late = gather_rows(late_shard)
     reach = rel_table.shape[0] - 1 - LEFT
     mixed_token_rows, log_total = attend(
-        queries, keys_all, values_all, wide_table(rel_table), reach, ctx_rank * queries.shape[1]
+        queries, pairs_all, wide_table(rel_table), reach, ctx_rank * queries.shape[1]
     )
     mixed_token_rows, late = together(mixed_token_rows, late)
     branch = narrow(rows_out(mixed_token_rows, out_w)) + out_b
     return (
         stream + branch,
-        (standard, inverse, wide_rows, queries, keys_all, values_all, mixed_token_rows, log_total),
+        (standard, inverse, wide_rows, queries, pairs_all, mixed_token_rows, log_total),
         late,
     )
 
 
 def attn_backward(grad_stream, saved, norm_gain, weights, rel_table, ctx_rank, inner_grads):
     query_w, key_w, value_w, out_w = weights
-    standard, inverse, wide_rows, queries, keys_all, values_all, mixed_token_rows, log_total = saved
+    standard, inverse, wide_rows, queries, pairs_all, mixed_token_rows, log_total = saved
     grad_branch = grad_stream.astype(jnp.bfloat16)
     out_bias_grad = jnp.sum(grad_branch.astype(jnp.float32), axis=(0, 1))
     inner = jnp.concatenate([grad.astype(jnp.bfloat16) for grad in inner_grads], axis=1)
@@ -343,26 +377,21 @@
     inner = lax.psum_scatter(inner, ("fsdp", "ctx"), scatter_dimension=0, tiled=True)
     grad_mixed = rows_in(wide_grad, out_w).astype(jnp.bfloat16)
     reach = rel_table.shape[0] - 1 - LEFT
-    query_low, key_terms, value_terms, table_turned = attend_back(
+    query_low, pair_terms, table_turned = attend_back(
         queries,
-        keys_all,
-        values_all,
+        pairs_all,
         wide_table(rel_table),
         log_total,
         grad_mixed,
         reach,
         ctx_rank * queries.shape[1],
     )
-    query_low, key_terms, value_terms, inner = together(query_low, key_terms, value_terms, inner)
+    query_low, pair_terms, inner = together(query_low, pair_terms, inner)
     out_grad = weight_sum(wide_grad, mixed_token_rows)
     inner_parts = split_columns(inner, inner_grads)
     table_grad = table_turned[:, LEFT : LEFT + rel_table.shape[0]].T
-    key_grad, value_grad = (
-        lax.psum_scatter(key_terms, "ctx", scatter_dimension=1, tiled=True),
-        lax.psum_scatter(value_terms, "ctx", scatter_dimension=1, tiled=True),
-    )
-    key_low = key_grad.astype(jnp.bfloat16)
-    value_low = value_grad.astype(jnp.bfloat16)
+    pair_low = lax.psum_scatter(pair_terms, "ctx", scatter_dimension=2, tiled=True)
+    key_low, value_low = pair_low[0], pair_low[1]
     query_bias_grad = jnp.sum(query_low.astype(jnp.float32), axis=(0, 1))
     value_bias_grad = jnp.sum(value_low.astype(jnp.float32), axis=(0, 1))
     query_w_grad = weight_sum(wide_rows, query_low)
@@ -569,7 +598,7 @@
     return tuple(pieces)
 
 
-def scatter_sum_all(grads, whole_parts, split_parts, own_sum):
+def scatter_sum_all(grads, whole_parts, split_parts, own_parts):
     rows = grads[0].shape[0]
     flat = jnp.concatenate([part.reshape(-1) for part in whole_parts + split_parts])
     columns = -(-flat.shape[0] // rows)
@@ -577,10 +606,11 @@
     parts = scatter_sum(*grads, jnp.pad(flat, ((0, 0), (0, -columns % 128))))
     small = parts[-1][:, :columns].reshape(-1)
     held = small.shape[0]
-    sent = jnp.concatenate([small, own_sum.reshape(1)])
+    sent = jnp.concatenate([small] + [part.reshape(-1) for part in own_parts])
     sent = jnp.pad(sent, (0, -sent.shape[0] % 128)).reshape(1, -1, 128)
     tp_count = lax.axis_size("tp")
-    every = lax.all_gather(sent, ("fsdp", "ctx", "tp"), axis=0, tiled=True)
+    every = lax.all_gather(sent, "tp", axis=0, tiled=True)
+    every = lax.all_gather(every, ("fsdp", "ctx"), axis=0, tiled=True)
     every = every.reshape(-1, tp_count, sent.size)
     by_tp = every[:, :, :held].transpose(1, 0, 2).reshape(tp_count, -1)
     total = jnp.sum(by_tp, axis=0)
@@ -599,7 +629,13 @@
             piece = piece.reshape((tp_count,) + part.shape)
             pieces.append(piece.transpose(1, 0, 2).reshape(part.shape[0], -1))
         start += part.size
-    w, p = whole + [jnp.sum(every[:, :, held])], pieces
+    own = jnp.sum(every[:, :, held:], axis=(0, 1))
+    start = 0
+    owned = []
+    for part in own_parts:
+        owned.append(own[start : start + part.size].reshape(part.shape))
+        start += part.size
+    w, p = owned[:2] + whole + owned[2:], pieces
     return parts[:-1], (
         w[0], w[1], p[0], w[2], w[3], w[4], p[1], p[2], w[5], w[6], w[7], w[8],
         p[3], p[4], p[5], w[9], w[10], p[6], w[11], w[12], w[13], w[14],
@@ -643,23 +679,9 @@
     final_gain,
     final_shift,
 ):
-    ffn1_in_all = gather_rows(ffn1_in)
     width = query_weight.shape[1]
-    early = gather_rows(
-        jnp.concatenate(
-            [ffn1_out, query_weight, key_weight, value_weight, attn_out_weight], axis=1
-        )
-    )
-    ffn1_out_all = early[:, : ffn1_out.shape[1]]
-    attn_all = early[:, ffn1_out.shape[1] :]
     late_shard = jnp.concatenate(
         [ffn2_in, ffn2_out, conv_value_weight, conv_gate_weight, conv_out_weight], axis=1
-    )
-    attn_weights = (
-        attn_all[:, :width],
-        attn_all[:, width : 2 * width],
-        attn_all[:, 2 * width : 3 * width],
-        attn_all[:, 3 * width :],
     )
     tp_rank = lax.axis_index("tp")
     ctx_rank = lax.axis_index("ctx")
@@ -673,8 +695,15 @@
     inner_gain_local = local_cut(conv_inner_gain, tp_rank, width_local)
     inner_shift_local = local_cut(conv_inner_shift, tp_rank, width_local)
     stream_zero = inputs.astype(jnp.float32)
-    stream_one, saved_one = ffn_forward(
-        stream_zero, ffn1_gain, ffn1_shift, ffn1_in_all, ffn1_bias_local, ffn1_out_all, ffn1_out_bias
+    stream_one, saved_one, ffn1_in_all, ffn1_out_all, attn_weights = ffn_forward_first(
+        stream_zero,
+        ffn1_gain,
+        ffn1_shift,
+        ffn1_in,
+        ffn1_bias_local,
+        ffn1_out,
+        ffn1_out_bias,
+        (query_weight, key_weight, value_weight, attn_out_weight),
     )
     stream_two, saved_two, late = attn_forward(
         stream_one,
@@ -748,8 +777,6 @@
     ffn1_parts, shared = scatter_sum_all(
         (ffn1_grads[2], ffn1_grads[4]),
         (
-            ffn1_grads[0],
-            ffn1_grads[1],
             ffn1_grads[5],
             attn_grads[0],
             attn_grads[1],
@@ -772,7 +799,7 @@
             conv_grads[6],
             ffn2_grads[3],
         ),
-        sse_local,
+        (ffn1_grads[0], ffn1_grads[1], sse_local),
     )
     weight_parts = ffn1_parts + attn_parts + inner_parts[2:] + inner_parts[:2]
     token_count = (jnp.sum(clips_dev) * SEQ).astype(jnp.float32)

time: 1480 us -> 1360 us (0.919)
  waiting for transfers between devices: 930 us -> 791 us
  blocking collectives: 107 us -> 137 us
    reduce_scatter x4 -> x3, waiting for transfers between devices: 184 us -> 137 us  [narrow(): lax.psum_scatter(partial_rows.astype(jnp.bfloat16), 'tp', scatter_dimensi...]
    all_gather x3 -> x2, waiting for transfers between devices: 66.3 us -> 27.2 us  [gather_rows(): return lax.all_gather(shard, ('fsdp', 'ctx'), axis=0, tiled=True)]
    all_gather x4, waiting for transfers between devices: 195 us -> 158 us  [widen(): return lax.all_gather(normed.astype(jnp.bfloat16), 'tp', axis=1, tiled=True)]
    all_gather x1 -> x10, blocking collectives: 71.1 us -> 101 us  [the longest x8 77.1 us: gather_rows(): return lax.all_gather(shard, ('fsdp', 'ctx'), axis=0, tiled=True)]
    reduce_scatter x2, waiting for transfers between devices: 61.4 us -> 81.7 us  [scatter_sum(): lax.psum_scatter(joined, ('fsdp', 'ctx'), scatter_dimension=0, tiled=True)]
    reduce_scatter x4, waiting for transfers between devices: 129 us -> 112 us  [narrow_grad(): lax.psum_scatter(partial_rows.astype(jnp.bfloat16), 'tp', scatter_dimensi...]
    all_gather x2 -> x1, waiting for transfers between devices: 44.7 us -> 32.8 us  [attn_forward(): pairs_all = lax.all_gather(pairs, 'ctx', axis=1, tiled=True)]
    dot_general x11 -> x10, matrix products: 52.5 us -> 48.8 us  [rows_in(): jnp.einsum('zub,bx->zux', left_reach, right_reach, preferred_element_type...]
  transfers between devices with their start and end apart: 28 -> 25, of which waited for: 25 -> 22; matrix products, arithmetic and copies ran while one was open for 10% -> 10% of each run, Pallas kernels for 7% -> 8%
where the time goes in v4:
time: 1360 us; the launch traced here: 1340 us
  waiting for transfers between devices  791 us (58%)
  blocking collectives  137 us (10%)
  matrix products  135 us (10%)
  Pallas kernels  114 us (8%)
  other arithmetic  77.9 us (6%)
  local copies, waits for them, and re-layouts  66.4 us (5%)
  between operations  18.1 us (1%)
    all_gather x4, waiting for transfers between devices, widen_grad(): return lax.all_gather(grad_branch, 'tp', axis=1, tiled=True)  190 us
    all_gather x4, waiting for transfers between devices, widen(): return lax.all_gather(normed.astype(jnp.bfloat16), 'tp', axis=1, tiled=True)  158 us
    reduce_scatter x3, waiting for transfers between devices, narrow(): lax.psum_scatter(partial_rows.astype(jnp.bfloat16), 'tp', scatter_dimensi...  137 us
    reduce_scatter x4, waiting for transfers between devices, narrow_grad(): lax.psum_scatter(partial_rows.astype(jnp.bfloat16), 'tp', scatter_dimensi...  112 us
    reduce_scatter x2, waiting for transfers between devices, scatter_sum(): lax.psum_scatter(joined, ('fsdp', 'ctx'), scatter_dimension=0, tiled=True)  81.7 us
    all_gather x8, blocking collectives, gather_rows(): return lax.all_gather(shard, ('fsdp', 'ctx'), axis=0, tiled=True)  77.1 us
    pallas_call x1, Pallas kernels, attend_back(): pl.pallas_call(functools.partial(attend_back_kernel, reach), out_shape=(j...  68.7 us
    dot_general x10, matrix products, rows_in(): jnp.einsum('zub,bx->zux', left_reach, right_reach, preferred_element_type...  48.8 us
  transfers between devices with their start and end apart: 25, of which 22 were waited for; matrix products, arithmetic and copies ran while one was open for 10% of the time, Pallas kernels for 8%

profile of v4, /device:TPU:0, one launch (start us, length us, event | category | flops | bytes accessed | tf_op | source)
XLA Modules:
  0.0 1344.5 jit_solution(7674109354205631694)
XLA Ops:
  71.1 21.4 %all-gather.14.cloned.1.call-done = bf16[1024,1024]{1,0:T(8,128)(2,1)} async-done(((bf16[128,1024]{1,0:T(8,128)(2,1)}), bf16[1024,1024]{1,0:T(8,128)(2,1)}) %all-gather.14.cloned.1.call-update) | async-done | bytes 2097168 | tf_op jit(solution)/shard_map/all_gather | solution.py:583
  151.7 48.5 %all-gather.16.cloned.1.call-done = bf16[3,384,1024]{2,1,0:T(8,128)(2,1)} async-done(((bf16[3,96,1024]{2,1,0:T(8,128)(2,1)}), bf16[3,384,1024]{2,1,0:T(8,128)(2,1)}) %all-gather.16.cloned.1.call-update) | async-done | bytes 2359312 | tf_op jit(solution)/shard_map/all_gather | solution.py:63
  207.8 32.8 %all-gather.18.cloned.1.call-done.key_ref.value_ref = bf16[3,1536,512]{2,1,0:T(8,128)(2,1)} async-done(((bf16[3,384,512]{2,1,0:T(8,128)(2,1)}), bf16[3,1536,512]{2,1,0:T(8,128)(2,1)}) %all-gather.18.cloned.1.call-update) | async-done | bytes 4718608 | tf_op jit(solution)/shard_map/all_gather | solution.py:354
  245.8 34.1 %attend.1 = (bf16[3,384,256]{2,1,0:T(8,128)(2,1)}, f32[3,384,256]{2,1,0:T(8,128)}) custom-call(s32[1]{0:T(128)} %bitcast.2.start_ref, bf16[3,384,256]{2,1,0:T(8,128)(2,1)} %fusion.34.query_ref, bf16[3,1536,512]{2,1,0:T(8,128)(2,1)} %all-gather.18.cloned.1.call-done.key_ref.value_ref, bf16[3,1536,512]{2,1,0:T(8,128)(2,1)} %all-gather.18.cloned.1.call-done.key_ref.value_ref, ...), custom_call_target="tpu_custom_call" | custom-call | flops 3623878656 | bytes 8388608 | tf_op jit(solution)/shard_map/attend/pallas_call | solution.py:238
  288.9 47.8 %reduce-scatter.15.cloned.1.call-done = bf16[3,96,1024]{2,1,0:T(8,128)(2,1)} async-done(((bf16[3,384,1024]{2,1,0:T(8,128)(2,1)}), bf16[3,96,1024]{2,1,0:T(8,128)(2,1)}) %reduce-scatter.15.cloned.1.call-update) | async-done | bytes 589840 | tf_op jit(solution)/shard_map/reduce_scatter | solution.py:67
  341.9 47.6 %all-gather.22.cloned.1.call-done = bf16[3,384,1024]{2,1,0:T(8,128)(2,1)} async-done(((bf16[3,96,1024]{2,1,0:T(8,128)(2,1)}), bf16[3,384,1024]{2,1,0:T(8,128)(2,1)}) %all-gather.22.cloned.1.call-update) | async-done | bytes 2359312 | tf_op jit(solution)/shard_map/all_gather | solution.py:63
  408.0 18.3 %all-reduce.6 = (f32[3,384]{1,0:T(4,128)}, f32[3,384]{1,0:T(4,128)}) all-reduce(f32[3,384]{1,0:T(4,128)} %get-tuple-element.231, f32[3,384]{1,0:T(4,128)} %get-tuple-element.230), channel_id=1, replica_groups=mesh['fsdp'=2,'ctx'=4,'tp'=4] {'tp'}, use_global_device_ids=true, to_apply=%region_11.12 | all-reduce | flops 2304 | bytes 18432 | tf_op jit(solution)/shard_map/psum | solution.py:443
  431.1 45.7 %reduce-scatter.17.cloned.1.call-done = bf16[3,96,1024]{2,1,0:T(8,128)(2,1)} async-done(((bf16[3,384,1024]{2,1,0:T(8,128)(2,1)}), bf16[3,96,1024]{2,1,0:T(8,128)(2,1)}) %reduce-scatter.17.cloned.1.call-update) | async-done | bytes 589840 | tf_op jit(solution)/shard_map/reduce_scatter | solution.py:67
  481.4 48.5 %all-gather.24.cloned.1.call-done = bf16[3,384,1024]{2,1,0:T(8,128)(2,1)} async-done(((bf16[3,96,1024]{2,1,0:T(8,128)(2,1)}), bf16[3,384,1024]{2,1,0:T(8,128)(2,1)}) %all-gather.24.cloned.1.call-update) | async-done | bytes 2359312 | tf_op jit(solution)/shard_map/all_gather | solution.py:63
  545.6 43.6 %reduce-scatter.19.cloned.1.call-done = bf16[3,96,1024]{2,1,0:T(8,128)(2,1)} async-done(((bf16[3,384,1024]{2,1,0:T(8,128)(2,1)}), bf16[3,96,1024]{2,1,0:T(8,128)(2,1)}) %reduce-scatter.19.cloned.1.call-update) | async-done | bytes 589840 | tf_op jit(solution)/shard_map/reduce_scatter | solution.py:67
  596.0 49.5 %all-gather.26.cloned.1.call-done = bf16[3,384,1024]{2,1,0:T(8,128)(2,1)} async-done(((bf16[3,96,1024]{2,1,0:T(8,128)(2,1)}), bf16[3,384,1024]{2,1,0:T(8,128)(2,1)}) %all-gather.26.cloned.1.call-update) | async-done | bytes 2359312 | tf_op jit(solution)/shard_map/all_gather | solution.py:73
  674.3 32.6 %reduce-scatter.21.cloned.1.call-done = bf16[3,96,1024]{2,1,0:T(8,128)(2,1)} async-done(((bf16[3,384,1024]{2,1,0:T(8,128)(2,1)}), bf16[3,96,1024]{2,1,0:T(8,128)(2,1)}) %reduce-scatter.21.cloned.1.call-update) | async-done | bytes 589840 | tf_op jit(solution)/shard_map/reduce_scatter | solution.py:77
  712.1 49.4 %all-gather.28.cloned.1.call-done = bf16[3,384,1024]{2,1,0:T(8,128)(2,1)} async-done(((bf16[3,96,1024]{2,1,0:T(8,128)(2,1)}), bf16[3,384,1024]{2,1,0:T(8,128)(2,1)}) %all-gather.28.cloned.1.call-update) | async-done | bytes 2359312 | tf_op jit(solution)/shard_map/all_gather | solution.py:73
  766.6 18.0 %all-reduce.5 = (f32[3,384]{1,0:T(4,128)}, f32[3,384]{1,0:T(4,128)}) all-reduce(f32[3,384]{1,0:T(4,128)} %get-tuple-element.204, f32[3,384]{1,0:T(4,128)} %get-tuple-element.224), channel_id=1, replica_groups=mesh['fsdp'=2,'ctx'=4,'tp'=4] {'tp'}, use_global_device_ids=true, to_apply=%region_26.27 | all-reduce | flops 2304 | bytes 18432 | tf_op jit(solution)/shard_map/psum | solution.py:546
  819.7 39.1 %reduce-scatter.23.cloned.1.call-done = bf16[3,96,1024]{2,1,0:T(8,128)(2,1)} async-done(((bf16[3,384,1024]{2,1,0:T(8,128)(2,1)}), bf16[3,96,1024]{2,1,0:T(8,128)(2,1)}) %reduce-scatter.23.cloned.1.call-update) | async-done | bytes 589840 | tf_op jit(solution)/shard_map/reduce_scatter | solution.py:77
  871.2 41.6 %all-gather.30.cloned.1.call-done = bf16[3,384,1024]{2,1,0:T(8,128)(2,1)} async-done(((bf16[3,96,1024]{2,1,0:T(8,128)(2,1)}), bf16[3,384,1024]{2,1,0:T(8,128)(2,1)}) %all-gather.30.cloned.1.call-update) | async-done | bytes 2359312 | tf_op jit(solution)/shard_map/all_gather | solution.py:73
  917.5 68.7 %attend_back.1 = (bf16[3,384,256]{2,1,0:T(8,128)(2,1)}, bf16[2,3,1536,256]{3,2,1,0:T(8,128)(2,1)}, f32[64,384]{1,0:T(8,128)}) custom-call(s32[1]{0:T(128)} %bitcast.2.start_ref, bf16[3,384,256]{2,1,0:T(8,128)(2,1)} %fusion.34.query_ref, bf16[3,1536,512]{2,1,0:T(8,128)(2,1)} %all-gather.18.cloned.1.call-done.key_ref.value_ref, ...), custom_call_target="tpu_custom_call" | custom-call | flops 9059696640 | bytes 16777216 | tf_op jit(solution)/shard_map/attend_back/pallas_call | solution.py:262
  990.5 42.6 %reduce-scatter.27.cloned.1.call-done = bf16[2,3,384,256]{3,2,1,0:T(8,128)(2,1)} async-done(((bf16[2,3,1536,256]{3,2,1,0:T(8,128)(2,1)}), bf16[2,3,384,256]{3,2,1,0:T(8,128)(2,1)}) %reduce-scatter.27.cloned.1.call-update) | async-done | bytes 1179664 | tf_op jit(solution)/shard_map/reduce_scatter | solution.py:393
  1048.8 38.2 %reduce-scatter.29.cloned.1.call-done = bf16[3,96,1024]{2,1,0:T(8,128)(2,1)} async-done(((bf16[3,384,1024]{2,1,0:T(8,128)(2,1)}), bf16[3,96,1024]{2,1,0:T(8,128)(2,1)}) %reduce-scatter.29.cloned.1.call-update) | async-done | bytes 589840 | tf_op jit(solution)/shard_map/reduce_scatter | solution.py:77
  1091.8 49.3 %all-gather.32.cloned.1.call-done = bf16[3,384,1024]{2,1,0:T(8,128)(2,1)} async-done(((bf16[3,96,1024]{2,1,0:T(8,128)(2,1)}), bf16[3,384,1024]{2,1,0:T(8,128)(2,1)}) %all-gather.32.cloned.1.call-update) | async-done | bytes 2359312 | tf_op jit(solution)/shard_map/all_gather | solution.py:73
  1168.6 13.7 %concatenate.46 = bf16[26944]{0:T(1024)(128)(2,1)} concatenate(bf16[1024]{0:T(1024)(128)(2,1)} %get-tuple-element.243, bf16[1024]{0:T(1024)(128)(2,1)} %get-tuple-element.205, bf16[1024]{0:T(1024)(128)(2,1)} %get-tuple-element.229, bf16[1024]{0:T(1024)(128)(2,1)} %get-tuple-element.240, bf16[4672]{0:T(1024)(128)(2,1)} %reshape.341, bf16[1024]{0:T(1024)(128)(2,1)} %get-tuple-element.209, ...), dimensions={0} | concatenate | bytes 107776 | tf_op jit(solution)/shard_map/concatenate | solution.py:603
  1213.1 32.0 %reduce-scatter.35.cloned.1.call-done = bf16[128,1024]{1,0:T(8,128)(2,1)} async-done(((bf16[1024,1024]{1,0:T(8,128)(2,1)}), bf16[128,1024]{1,0:T(8,128)(2,1)}) %reduce-scatter.35.cloned.1.call-update) | async-done | bytes 262160 | tf_op jit(solution)/shard_map/reduce_scatter | solution.py:588
  1251.4 49.7 %reduce-scatter.33.cloned.1.call-done = bf16[128,2176]{1,0:T(8,128)(2,1)} async-done(((bf16[1024,2176]{1,0:T(8,128)(2,1)}), bf16[128,2176]{1,0:T(8,128)(2,1)}) %reduce-scatter.33.cloned.1.call-update) | async-done | bytes 557072 | tf_op jit(solution)/shard_map/reduce_scatter | solution.py:588
  1303.3 13.4 all_gather.82
  (490 shorter events, 400.3 us)
Async XLA Ops:
  7.2 56.8 %all-gather.12.cloned.1.call-start = ((), (), s32[]{:S(2)}) async-start(), calls=%async_computation.12 | async-start | bytes 2949120 | tf_op jit(solution)/shard_map/all_gather | solution.py:63
  11.2 81.3 %all-gather.14.cloned.1.call-start = ((), (), s32[]{:S(2)}) async-start(), calls=%async_computation.13 | async-start | bytes 2359296 | tf_op jit(solution)/shard_map/all_gather | solution.py:583
  64.1 83.4 %reduce-scatter.13.cloned.1.call-start = ((), (), s32[]{:S(2)}) async-start(), calls=%async_computation.14 | async-start | bytes 2949120 | tf_op jit(solution)/shard_map/reduce_scatter | solution.py:319
  99.7 100.5 %all-gather.16.cloned.1.call-start = ((), (), s32[]{:S(2)}) async-start(), calls=%async_computation.15 | async-start | bytes 2949120 | tf_op jit(solution)/shard_map/all_gather | solution.py:63
  150.7 90.0 %all-gather.18.cloned.1.call-start = ((), (), s32[]{:S(2)}) async-start(), calls=%async_computation.16 | async-start | bytes 5898240 | tf_op jit(solution)/shard_map/all_gather | solution.py:354
  204.3 81.3 %all-gather.20.cloned.1.call-start = ((), (), s32[]{:S(2)}) async-start(), calls=%async_computation.17 | async-start | bytes 6488064 | tf_op jit(solution)/shard_map/all_gather | solution.py:583
  240.6 96.1 %reduce-scatter.15.cloned.1.call-start = ((), (), s32[]{:S(2)}) async-start(), calls=%async_computation.18 | async-start | bytes 2949120 | tf_op jit(solution)/shard_map/reduce_scatter | solution.py:67
  288.9 100.7 %all-gather.22.cloned.1.call-start = ((), (), s32[]{:S(2)}) async-start(), calls=%async_computation.19 | async-start | bytes 2949120 | tf_op jit(solution)/shard_map/all_gather | solution.py:63
  340.1 136.8 %reduce-scatter.17.cloned.1.call-start = ((), (), s32[]{:S(2)}) async-start(), calls=%async_computation.20 | async-start | bytes 2949120 | tf_op jit(solution)/shard_map/reduce_scatter | solution.py:67
  395.6 5.5 collective-permute-start
  431.1 98.9 %all-gather.24.cloned.1.call-start = ((), (), s32[]{:S(2)}) async-start(), calls=%async_computation.21 | async-start | bytes 2949120 | tf_op jit(solution)/shard_map/all_gather | solution.py:63
  480.4 108.8 %reduce-scatter.19.cloned.1.call-start = ((), (), s32[]{:S(2)}) async-start(), calls=%async_computation.22 | async-start | bytes 2949120 | tf_op jit(solution)/shard_map/reduce_scatter | solution.py:67
  542.6 102.9 %all-gather.26.cloned.1.call-start = ((), (), s32[]{:S(2)}) async-start(), calls=%async_computation.23 | async-start | bytes 2949120 | tf_op jit(solution)/shard_map/all_gather | solution.py:73
  596.0 111.0 %reduce-scatter.21.cloned.1.call-start = ((), (), s32[]{:S(2)}) async-start(), calls=%async_computation.24 | async-start | bytes 2949120 | tf_op jit(solution)/shard_map/reduce_scatter | solution.py:77
  660.3 101.3 %all-gather.28.cloned.1.call-start = ((), (), s32[]{:S(2)}) async-start(), calls=%async_computation.25 | async-start | bytes 2949120 | tf_op jit(solution)/shard_map/all_gather | solution.py:73
  712.1 146.7 %reduce-scatter.23.cloned.1.call-start = ((), (), s32[]{:S(2)}) async-start(), calls=%async_computation.26 | async-start | bytes 2949120 | tf_op jit(solution)/shard_map/reduce_scatter | solution.py:77
  812.3 100.5 %all-gather.30.cloned.1.call-start = ((), (), s32[]{:S(2)}) async-start(), calls=%async_computation.27 | async-start | bytes 2949120 | tf_op jit(solution)/shard_map/all_gather | solution.py:73
  863.2 123.0 %reduce-scatter.25.cloned.1.call-start = ((), (), s32[]{:S(2)}) async-start(), calls=%async_computation.28 | async-start | bytes 6488064 | tf_op jit(solution)/shard_map/reduce_scatter | solution.py:377
  912.8 120.4 %reduce-scatter.27.cloned.1.call-start = ((), (), s32[]{:S(2)}) async-start(), calls=%async_computation.29 | async-start | bytes 5898240 | tf_op jit(solution)/shard_map/reduce_scatter | solution.py:393
  986.3 100.8 %reduce-scatter.29.cloned.1.call-start = ((), (), s32[]{:S(2)}) async-start(), calls=%async_computation.30 | async-start | bytes 2949120 | tf_op jit(solution)/shard_map/reduce_scatter | solution.py:77
  1039.2 101.9 %all-gather.32.cloned.1.call-start = ((), (), s32[]{:S(2)}) async-start(), calls=%async_computation.31 | async-start | bytes 2949120 | tf_op jit(solution)/shard_map/all_gather | solution.py:73
  1091.6 109.7 %reduce-scatter.31.cloned.1.call-start = ((), (), s32[]{:S(2)}) async-start(), calls=%async_computation.32 | async-start | bytes 2949120 | tf_op jit(solution)/shard_map/reduce_scatter | solution.py:77
  1154.6 90.4 %reduce-scatter.35.cloned.1.call-start = ((), (), s32[]{:S(2)}) async-start(), calls=%async_computation.34 | async-start | bytes 2359296 | tf_op jit(solution)/shard_map/reduce_scatter | solution.py:588
  1157.8 143.3 %reduce-scatter.33.cloned.1.call-start = ((), (), s32[]{:S(2)}) async-start(), calls=%async_computation.33 | async-start | bytes 5013504 | tf_op jit(solution)/shard_map/reduce_scatter | solution.py:588
  (131 other events, 1567.9 us)
Sparse Core Ops, SparseCore 0:
  11.3 52.6 all-gather.11
  65.9 26.5 all-gather.13
  99.8 47.6 reduce-scatter.12
  150.8 49.3 all-gather.15
  204.4 36.1 all-gather.17
  242.4 43.1 all-gather.19
  289.0 47.6 reduce-scatter.14
  340.2 49.3 all-gather.21
  431.2 45.6 reduce-scatter.16
  480.5 49.3 all-gather.23
  542.7 46.4 reduce-scatter.18
  596.1 49.3 all-gather.25
  660.4 46.4 reduce-scatter.20
  712.2 49.3 all-gather.27
  812.4 46.3 reduce-scatter.22
  863.4 49.3 all-gather.29
  916.0 57.7 reduce-scatter.24
  986.4 46.6 reduce-scatter.26
  1039.3 47.6 reduce-scatter.28
  1091.7 49.3 all-gather.31
  1154.7 46.4 reduce-scatter.30
  1204.5 40.4 reduce-scatter.34
  1248.5 52.5 reduce-scatter.32

commit v5 on v4

--- a/solution.py
+++ b/solution.py
@@ -61,6 +61,16 @@
 
 def widen(normed):
     return lax.all_gather(normed.astype(jnp.bfloat16), "tp", axis=1, tiled=True)
+
+
+def widen_ctx(normed):
+    return lax.all_gather(normed.astype(jnp.bfloat16), "ctx", axis=1, tiled=True)
+
+
+def narrow_ctx(partial_rows):
+    return lax.psum_scatter(
+        partial_rows.astype(jnp.bfloat16), "ctx", scatter_dimension=1, tiled=True
+    )
 
 
 def narrow(partial_rows):
@@ -292,10 +302,10 @@
 
 def ffn_forward(stream, norm_gain, norm_shift, weight_in, bias_in, weight_out, bias_out):
     normed, standard, inverse = norm_forward(stream, norm_gain, norm_shift)
-    wide_rows = widen(normed)
+    wide_rows = widen_ctx(normed)
     hidden_pre = rows_in(wide_rows, weight_in) + bias_in
     active = jax.nn.silu(hidden_pre).astype(jnp.bfloat16)
-    branch = narrow(rows_out(active, weight_out)) + bias_out
+    branch = narrow_ctx(rows_out(active, weight_out)).astype(jnp.float32) + bias_out
     return (stream + 0.5 * branch, (standard, inverse, wide_rows, hidden_pre))
 
 
@@ -303,62 +313,76 @@
     stream, norm_gain, norm_shift, shard_in, bias_in, shard_out, bias_out, later_shards
 ):
     normed, standard, inverse = norm_forward(stream, norm_gain, norm_shift)
-    normed, shard_in = together(normed.astype(jnp.bfloat16), shard_in)
-    wide_rows = widen(normed)
+    normed, shard_in, shard_out = together(normed.astype(jnp.bfloat16), shard_in, shard_out)
+    wide_rows = widen_ctx(normed)
+    mine_in, mine_out = across(shard_in), across(shard_out)
+    piece = -(-mine_in.shape[0] // 4)
     pieces = [
-        gather_rows(shard_in[:, start : start + 256]) for start in range(0, shard_in.shape[1], 256)
+        gather_panels(mine_in[start : start + piece])
+        for start in range(0, mine_in.shape[0], piece)
     ]
-    wide_rows, shard_out, *pieces = together(wide_rows, shard_out, *pieces)
-    weight_out = gather_rows(shard_out)
-    weight_in = jnp.concatenate(pieces, axis=1)
+    weight_out = gather_panels(mine_out)
+    weight_in = join_panels(jnp.concatenate(pieces, axis=1))
+    wide_rows, weight_in, weight_out = together(wide_rows, weight_in, weight_out)
+    weight_out = join_panels(weight_out)
     hidden_pre = rows_in(wide_rows, weight_in) + bias_in
     active = jax.nn.silu(hidden_pre).astype(jnp.bfloat16)
     partial_rows = rows_out(active, weight_out).astype(jnp.bfloat16)
     partial_rows, *later_shards = together(partial_rows, *later_shards)
     later = [gather_rows(shard) for shard in later_shards]
-    summed = lax.psum_scatter(partial_rows, "tp", scatter_dimension=1, tiled=True)
+    summed = narrow_ctx(partial_rows)
     summed, *later = together(summed, *later)
     branch = summed.astype(jnp.float32) + bias_out
     saved = (standard, inverse, wide_rows, hidden_pre)
     return (stream + 0.5 * branch, saved, weight_in, weight_out, later)
 
 
-def ffn_backward(grad_stream, saved, norm_gain, weight_in, weight_out):
+def ffn_backward(grad_stream, saved, norm_gain, weight_in, weight_out, beside=None):
     standard, inverse, wide_rows, hidden_pre = saved
     grad_branch = (0.5 * grad_stream).astype(jnp.bfloat16)
     out_bias_grad = jnp.sum(grad_branch.astype(jnp.float32), axis=(0, 1))
-    wide_grad = widen_grad(grad_branch)
+    wide_grad = widen_ctx(grad_branch)
+    if beside is not None:
+        wide_grad, beside = together(wide_grad, beside)
+        beside = lax.psum_scatter(beside, ("fsdp", "ctx"), scatter_dimension=0, tiled=True)
     active = jax.nn.silu(hidden_pre).astype(jnp.bfloat16)
     out_grad = weight_sum(wide_grad, active)
     grad_pre = (rows_in(wide_grad, weight_out) * silu_slope(hidden_pre)).astype(jnp.bfloat16)
     in_bias_grad = jnp.sum(grad_pre.astype(jnp.float32), axis=(0, 1))
     in_grad = weight_sum(wide_rows, grad_pre)
-    grad_normed = narrow_grad(rows_out(grad_pre, weight_in))
+    partial_rows = rows_out(grad_pre, weight_in).astype(jnp.bfloat16)
+    if beside is not None:
+        partial_rows, beside = together(partial_rows, beside)
+    grad_normed = narrow_ctx(partial_rows)
     grad_normed, in_grad, out_grad = together(grad_normed, in_grad, out_grad)
+    grad_normed = grad_normed.astype(jnp.float32)
     grad_in, gain_grad, shift_grad = norm_backward(grad_normed, standard, inverse, norm_gain)
     return (
         grad_stream + grad_in,
         (gain_grad, shift_grad, in_grad, in_bias_grad, out_grad, out_bias_grad),
-    )
-
-
-def attn_forward(stream, norm_gain, norm_shift, weights, biases, rel_table, ctx_rank, late_shard):
+        beside,
+    )
+
+
+def attn_forward(stream, norm_gain, norm_shift, weights, biases, rel_table, ctx_rank, late_shard, panel_shards):
     query_w, key_w, value_w, out_w = weights
     query_b, value_b, out_b = biases
     normed, standard, inverse = norm_forward(stream, norm_gain, norm_shift)
-    wide_rows = widen(normed)
+    normed, *panel_shards = together(normed.astype(jnp.bfloat16), *panel_shards)
+    mine = jnp.concatenate([across(shard) for shard in panel_shards], axis=1)
+    wide_rows, mine = together(widen(normed), mine)
     queries = (rows_in(wide_rows, query_w) + query_b).astype(jnp.bfloat16)
     pair_b = jnp.concatenate([jnp.zeros_like(value_b), value_b])
     pair_w = jnp.concatenate([key_w, value_w], axis=1)
     pairs = (rows_in(wide_rows, pair_w) + pair_b).astype(jnp.bfloat16)
     pairs_all = lax.all_gather(pairs, "ctx", axis=1, tiled=True)
-    pairs_all, late_shard = together(pairs_all, late_shard)
-    late = gather_rows(late_shard)
+    pairs_all, late_shard, mine = together(pairs_all, late_shard, mine)
+    late = (gather_panels(mine), gather_rows(late_shard))
     reach = rel_table.shape[0] - 1 - LEFT
     mixed_token_rows, log_total = attend(
         queries, pairs_all, wide_table(rel_table), reach, ctx_rank * queries.shape[1]
     )
-    mixed_token_rows, late = together(mixed_token_rows, late)
+    mixed_token_rows, *late = together(mixed_token_rows, *late)
     branch = narrow(rows_out(mixed_token_rows, out_w)) + out_b
     return (
         stream + branch,
@@ -372,9 +396,11 @@
     standard, inverse, wide_rows, queries, pairs_all, mixed_token_rows, log_total = saved
     grad_branch = grad_stream.astype(jnp.bfloat16)
     out_bias_grad = jnp.sum(grad_branch.astype(jnp.float32), axis=(0, 1))
-    inner = jnp.concatenate([grad.astype(jnp.bfloat16) for grad in inner_grads], axis=1)
-    wide_grad, inner = together(widen_grad(grad_branch), inner)
+    inner = jnp.concatenate([grad.astype(jnp.bfloat16) for grad in inner_grads[2:]], axis=1)
+    panels = split_panels(*inner_grads[:2])
+    wide_grad, inner, panels = together(widen_grad(grad_branch), inner, panels)
     inner = lax.psum_scatter(inner, ("fsdp", "ctx"), scatter_dimension=0, tiled=True)
+    panels = scatter_panels(panels)
     grad_mixed = rows_in(wide_grad, out_w).astype(jnp.bfloat16)
     reach = rel_table.shape[0] - 1 - LEFT
     query_low, pair_terms, table_turned = attend_back(
@@ -386,11 +412,19 @@
         reach,
         ctx_rank * queries.shape[1],
     )
-    query_low, pair_terms, inner = together(query_low, pair_terms, inner)
+    query_low, pair_terms, inner, panels = together(query_low, pair_terms, inner, panels)
     out_grad = weight_sum(wide_grad, mixed_token_rows)
-    inner_parts = split_columns(inner, inner_grads)
+    inner_parts = split_columns(inner, inner_grads[2:])
     table_grad = table_turned[:, LEFT : LEFT + rel_table.shape[0]].T
     pair_low = lax.psum_scatter(pair_terms, "ctx", scatter_dimension=2, tiled=True)
+    half = panels.shape[1] // 2
+    pair_low, first_part, second_part = together(
+        pair_low, across_back(panels[:, :half]), across_back(panels[:, half:])
+    )
+    inner_parts = (
+        first_part.astype(jnp.float32),
+        second_part.astype(jnp.float32),
+    ) + inner_parts
     key_low, value_low = pair_low[0], pair_low[1]
     query_bias_grad = jnp.sum(query_low.astype(jnp.float32), axis=(0, 1))
     value_bias_grad = jnp.sum(value_low.astype(jnp.float32), axis=(0, 1))
@@ -579,6 +613,38 @@
     )
 
 
+def across(shard):
+    return lax.all_to_all(shard, "ctx", split_axis=1, concat_axis=0, tiled=True)
+
+
+def across_back(shard):
+    return lax.all_to_all(shard, "ctx", split_axis=0, concat_axis=1, tiled=True)
+
+
+def gather_panels(mine):
+    return lax.all_gather(mine, ("tp", "fsdp"), axis=0, tiled=False)
+
+
+def join_panels(panels):
+    count, rows, columns = panels.shape
+    tp_count = lax.axis_size("tp")
+    panels = panels.reshape(tp_count, count // tp_count * rows, columns)
+    return panels.transpose(1, 0, 2).reshape(panels.shape[1], tp_count * columns)
+
+
+def split_panels(*grads):
+    tp_count = lax.axis_size("tp")
+    parts = []
+    for grad in grads:
+        part = grad.astype(jnp.bfloat16).reshape(grad.shape[0], tp_count, -1)
+        parts.append(part.transpose(1, 0, 2).reshape(tp_count * grad.shape[0], -1))
+    return jnp.concatenate(parts, axis=1)
+
+
+def scatter_panels(joined):
+    return lax.psum_scatter(joined, ("tp", "fsdp"), scatter_dimension=0, tiled=True)
+
+
 def gather_rows(shard):
     return lax.all_gather(shard, ("fsdp", "ctx"), axis=0, tiled=True)
 
@@ -598,17 +664,24 @@
     return tuple(pieces)
 
 
-def scatter_sum_all(grads, whole_parts, split_parts, own_parts):
-    rows = grads[0].shape[0]
+def small_columns(whole_parts, split_parts, rows):
     flat = jnp.concatenate([part.reshape(-1) for part in whole_parts + split_parts])
     columns = -(-flat.shape[0] // rows)
     flat = jnp.pad(flat, (0, rows * columns - flat.shape[0])).reshape(rows, columns)
-    parts = scatter_sum(*grads, jnp.pad(flat, ((0, 0), (0, -columns % 128))))
-    small = parts[-1][:, :columns].reshape(-1)
+    return jnp.pad(flat, ((0, 0), (0, -columns % 128)))
+
+
+def finish_small(small, whole_parts, split_parts, own_parts, hidden_part):
+    rows = small.shape[0] * lax.axis_size(("fsdp", "ctx"))
+    count = sum(part.size for part in whole_parts + split_parts)
+    small = small[:, : -(-count // rows)].astype(jnp.float32).reshape(-1)
     held = small.shape[0]
-    sent = jnp.concatenate([small] + [part.reshape(-1) for part in own_parts])
+    sent = jnp.concatenate(
+        [small] + [part.reshape(-1) for part in own_parts] + [hidden_part.reshape(-1)]
+    )
     sent = jnp.pad(sent, (0, -sent.shape[0] % 128)).reshape(1, -1, 128)
     tp_count = lax.axis_size("tp")
+    ctx_count = lax.axis_size("ctx")
     every = lax.all_gather(sent, "tp", axis=0, tiled=True)
     every = lax.all_gather(every, ("fsdp", "ctx"), axis=0, tiled=True)
     every = every.reshape(-1, tp_count, sent.size)
@@ -635,11 +708,32 @@
     for part in own_parts:
         owned.append(own[start : start + part.size].reshape(part.shape))
         start += part.size
-    w, p = owned[:2] + whole + owned[2:], pieces
-    return parts[:-1], (
-        w[0], w[1], p[0], w[2], w[3], w[4], p[1], p[2], w[5], w[6], w[7], w[8],
-        p[3], p[4], p[5], w[9], w[10], p[6], w[11], w[12], w[13], w[14],
-    )
+    first = held + start
+    hidden = every[:, :, first : first + hidden_part.size]
+    hidden = hidden.reshape(-1, ctx_count, tp_count, hidden_part.size).sum(axis=(0, 2))
+    hidden = hidden_order(hidden)
+    w, p = whole, pieces
+    return (
+        owned[0], owned[1], hidden, owned[2], w[0], w[1], p[0], p[1], w[2], w[3], w[4], w[5],
+        p[2], p[3], p[4], w[6], w[7], w[8], w[9], w[10], w[11], owned[3],
+    )
+
+
+def hidden_order(by_ctx):
+    ctx_count = by_ctx.shape[0]
+    parts = by_ctx.reshape(ctx_count, lax.axis_size("tp"), -1)
+    return parts.transpose(1, 0, 2).reshape(-1)
+
+
+def hidden_local(full, ctx_rank):
+    parts = full.reshape(lax.axis_size("tp"), lax.axis_size("ctx"), -1)
+    return lax.dynamic_slice_in_dim(parts, ctx_rank, 1, 1).reshape(-1)
+
+
+def hidden_put(local, ctx_rank):
+    parts = local.reshape(lax.axis_size("tp"), 1, -1)
+    full = jnp.zeros((parts.shape[0], lax.axis_size("ctx"), parts.shape[2]), jnp.float32)
+    return lax.dynamic_update_slice_in_dim(full, parts, ctx_rank, 1).reshape(-1)
 
 
 def body(
@@ -681,14 +775,13 @@
 ):
     width = query_weight.shape[1]
     late_shard = jnp.concatenate(
-        [ffn2_in, ffn2_out, conv_value_weight, conv_gate_weight, conv_out_weight], axis=1
+        [conv_value_weight, conv_gate_weight, conv_out_weight], axis=1
     )
     tp_rank = lax.axis_index("tp")
     ctx_rank = lax.axis_index("ctx")
-    hidden_local = ffn1_in.shape[1]
     width_local = width
-    ffn1_bias_local = local_cut(ffn1_in_bias, tp_rank, hidden_local)
-    ffn2_bias_local = local_cut(ffn2_in_bias, tp_rank, hidden_local)
+    ffn1_bias_local = hidden_local(ffn1_in_bias, ctx_rank)
+    ffn2_bias_local = hidden_local(ffn2_in_bias, ctx_rank)
     query_bias_local = local_cut(query_bias, tp_rank, width_local)
     value_bias_local = local_cut(value_bias, tp_rank, width_local)
     depth_local = local_cut(conv_depth, tp_rank, width_local)
@@ -714,10 +807,12 @@
         rel_table,
         ctx_rank,
         late_shard,
-    )
-    ffn2_in_all = late[:, :hidden_local]
-    ffn2_out_all = late[:, hidden_local : 2 * hidden_local]
-    conv_all = late[:, 2 * hidden_local :]
+        (ffn2_in, ffn2_out),
+    )
+    half = late[0].shape[2] // 2
+    ffn2_in_all = join_panels(late[0][:, :, :half])
+    ffn2_out_all = join_panels(late[0][:, :, half:])
+    conv_all = late[1]
     conv_weights = (
         conv_all[:, :width],
         conv_all[:, width : 2 * width],
@@ -750,7 +845,7 @@
     gradient_fourth, final_gain_grad, final_shift_grad = norm_backward(
         2.0 * misfit, final_standard, final_inverse, final_gain
     )
-    grad_three, ffn2_grads = ffn_backward(
+    grad_three, ffn2_grads, _ = ffn_backward(
         gradient_fourth, saved_four, ffn2_gain, ffn2_in_all, ffn2_out_all
     )
     grad_two, conv_grads = conv_backward(
@@ -770,37 +865,49 @@
         ctx_rank,
         (ffn2_grads[2], ffn2_grads[4], conv_grads[2], conv_grads[3], conv_grads[7]),
     )
-    grad_zero, ffn1_grads = ffn_backward(
-        grad_one, saved_one, ffn1_gain, ffn1_in_all, ffn1_out_all
-    )
-    attn_parts = scatter_sum(attn_grads[2], attn_grads[4], attn_grads[5], attn_grads[7])
-    ffn1_parts, shared = scatter_sum_all(
-        (ffn1_grads[2], ffn1_grads[4]),
-        (
-            ffn1_grads[5],
-            attn_grads[0],
-            attn_grads[1],
-            attn_grads[8],
-            attn_grads[9],
-            conv_grads[0],
-            conv_grads[1],
-            ffn2_grads[0],
-            ffn2_grads[1],
-            ffn2_grads[5],
-            final_gain_grad,
-            final_shift_grad,
-        ),
-        (
-            ffn1_grads[3],
-            attn_grads[3],
-            attn_grads[6],
-            conv_grads[4],
-            conv_grads[5],
-            conv_grads[6],
-            ffn2_grads[3],
-        ),
-        (ffn1_grads[0], ffn1_grads[1], sse_local),
-    )
+    attn_mats = (attn_grads[2], attn_grads[4], attn_grads[5], attn_grads[7])
+    whole_parts = (
+        attn_grads[0],
+        attn_grads[1],
+        attn_grads[8],
+        attn_grads[9],
+        conv_grads[0],
+        conv_grads[1],
+        ffn2_grads[0],
+        ffn2_grads[1],
+        hidden_put(ffn2_grads[3], ctx_rank),
+        ffn2_grads[5],
+        final_gain_grad,
+        final_shift_grad,
+    )
+    split_parts = (
+        attn_grads[3],
+        attn_grads[6],
+        conv_grads[4],
+        conv_grads[5],
+        conv_grads[6],
+    )
+    columns = small_columns(whole_parts, split_parts, attn_mats[0].shape[0])
+    beside_mats = attn_mats + (columns,)
+    beside = jnp.concatenate([part.astype(jnp.bfloat16) for part in beside_mats], axis=1)
+    grad_zero, ffn1_grads, beside = ffn_backward(
+        grad_one, saved_one, ffn1_gain, ffn1_in_all, ffn1_out_all, beside
+    )
+    attn_parts = split_columns(beside, beside_mats)
+    panels = scatter_panels(split_panels(ffn1_grads[2], ffn1_grads[4]))
+    half = panels.shape[1] // 2
+    ffn1_parts = (
+        across_back(panels[:, :half]).astype(jnp.float32),
+        across_back(panels[:, half:]).astype(jnp.float32),
+    )
+    shared = finish_small(
+        attn_parts[-1],
+        whole_parts,
+        split_parts,
+        (ffn1_grads[0], ffn1_grads[1], ffn1_grads[5], sse_local),
+        ffn1_grads[3],
+    )
+    attn_parts = attn_parts[:-1]
     weight_parts = ffn1_parts + attn_parts + inner_parts[2:] + inner_parts[:2]
     token_count = (jnp.sum(clips_dev) * SEQ).astype(jnp.float32)
     loss = shared[21] / token_count

time: 1360 us -> 1460 us (1.074)
  blocking collectives: 137 us -> 251 us
  waiting for transfers between devices: 791 us -> 689 us
  local copies, waits for them, and re-layouts: 66.4 us -> 137 us
  starting transfers between devices: 5.35 us -> 26.4 us
    all_gather x2 -> x6, blocking collectives: 23.7 us -> 156 us  [the longest x4 129 us: gather_panels(): return lax.all_gather(mine, ('tp', 'fsdp'), axis=0, tiled=False)]
    all_gather x4 -> x2, waiting for transfers between devices: 190 us -> 93.6 us  [widen_grad(): return lax.all_gather(grad_branch, 'tp', axis=1, tiled=True)]
    all_gather x0 -> x6, waiting for transfers between devices: none -> 90.4 us  [the longest x2 63.6 us: gather_panels(): return lax.all_gather(mine, ('tp', 'fsdp'), axis=0, tiled=False)]
    all_gather x4 -> x2, waiting for transfers between devices: 158 us -> 73.5 us  [widen(): return lax.all_gather(normed.astype(jnp.bfloat16), 'tp', axis=1, tiled=True)]
    reduce_scatter x3 -> x7, waiting for transfers between devices: 91.4 us -> 167 us  [the longest x4 70.5 us: narrow_ctx(): lax.psum_scatter(partial_rows.astype(jnp.bfloat16), 'ctx', scatter_dimens...]
    reduce_scatter x3 -> x2, waiting for transfers between devices: 137 us -> 92.1 us  [narrow(): lax.psum_scatter(partial_rows.astype(jnp.bfloat16), 'tp', scatter_dimensi...]
    all_gather x8 -> x4, blocking collectives: 77.1 us -> 40.9 us  [gather_rows(): return lax.all_gather(shard, ('fsdp', 'ctx'), axis=0, tiled=True)]
    reduce_scatter x4 -> x2, waiting for transfers between devices: 112 us -> 77 us  [narrow_grad(): lax.psum_scatter(partial_rows.astype(jnp.bfloat16), 'tp', scatter_dimensi...]
  transfers between devices with their start and end apart: 25 -> 33, of which waited for: 22 -> 25; matrix products, arithmetic and copies ran while one was open for 10% -> 14% of each run, Pallas kernels for 8% -> 7%
where the time goes in v5:
time: 1460 us; the launch traced here: 1440 us
  waiting for transfers between devices  689 us (47%)
  blocking collectives  251 us (17%)
  local copies, waits for them, and re-layouts  137 us (9%)
  matrix products  125 us (9%)
  Pallas kernels  114 us (8%)
  other arithmetic  83.1 us (6%)
  starting transfers between devices  26.4 us (2%)
  between operations  18.6 us (1%)
    all_gather x4, blocking collectives, gather_panels(): return lax.all_gather(mine, ('tp', 'fsdp'), axis=0, tiled=False)  129 us
    all_gather x2, waiting for transfers between devices, widen_grad(): return lax.all_gather(grad_branch, 'tp', axis=1, tiled=True)  93.6 us
    reduce_scatter x2, waiting for transfers between devices, narrow(): lax.psum_scatter(partial_rows.astype(jnp.bfloat16), 'tp', scatter_dimensi...  92.1 us
    reduce_scatter x2, waiting for transfers between devices, narrow_grad(): lax.psum_scatter(partial_rows.astype(jnp.bfloat16), 'tp', scatter_dimensi...  77 us
    all_gather x2, waiting for transfers between devices, widen(): return lax.all_gather(normed.astype(jnp.bfloat16), 'tp', axis=1, tiled=True)  73.5 us
    reduce_scatter x4, waiting for transfers between devices, narrow_ctx(): lax.psum_scatter(partial_rows.astype(jnp.bfloat16), 'ctx', scatter_dimens...  70.5 us
    pallas_call x1, Pallas kernels, attend_back(): pl.pallas_call(functools.partial(attend_back_kernel, reach), out_shape=(j...  68.7 us
    reduce_scatter x2, waiting for transfers between devices, scatter_panels(): lax.psum_scatter(joined, ('tp', 'fsdp'), scatter_dimension=0, tiled=True)  68.5 us
  transfers between devices with their start and end apart: 33, of which 25 were waited for; matrix products, arithmetic and copies ran while one was open for 14% of the time, Pallas kernels for 7%

profile of v5, /device:TPU:0, one launch (start us, length us, event | category | flops | bytes accessed | tf_op | source)
XLA Modules:
  0.0 1444.6 jit_solution(1281703933603700565)
XLA Ops:
  36.3 32.9 %all_gather.80 = bf16[8,128,256]{2,1,0:T(8,128)(2,1)S(1)} all-gather(bf16[1,128,256]{2,1,0:T(8,128)(2,1)S(1)} %copy.173), channel_id=1, replica_groups=mesh['fsdp'=2,'ctx'=4,'tp'=4] {'tp','fsdp'}, dimensions={0}, use_global_device_ids=true | all-gather | bytes 589824 | tf_op jit(solution)/shard_map/all_gather | solution.py:625
  69.2 33.5 %all_gather.79 = bf16[8,128,256]{2,1,0:T(8,128)(2,1)S(1)} all-gather(bf16[1,128,256]{2,1,0:T(8,128)(2,1)S(1)} %copy.172), channel_id=1, replica_groups=mesh['fsdp'=2,'ctx'=4,'tp'=4] {'tp','fsdp'}, dimensions={0}, use_global_device_ids=true | all-gather | bytes 589824 | tf_op jit(solution)/shard_map/all_gather | solution.py:625
  102.7 31.5 %all_gather.78 = bf16[8,128,256]{2,1,0:T(8,128)(2,1)S(1)} all-gather(bf16[1,128,256]{2,1,0:T(8,128)(2,1)S(1)} %copy.171), channel_id=1, replica_groups=mesh['fsdp'=2,'ctx'=4,'tp'=4] {'tp','fsdp'}, dimensions={0}, use_global_device_ids=true | all-gather | bytes 589824 | tf_op jit(solution)/shard_map/all_gather | solution.py:625
  134.2 31.2 %all_gather.77 = bf16[8,128,256]{2,1,0:T(8,128)(2,1)S(1)} all-gather(bf16[1,128,256]{2,1,0:T(8,128)(2,1)S(1)} %copy.170), channel_id=1, replica_groups=mesh['fsdp'=2,'ctx'=4,'tp'=4] {'tp','fsdp'}, dimensions={0}, use_global_device_ids=true | all-gather | bytes 589824 | tf_op jit(solution)/shard_map/all_gather | solution.py:625
  251.7 26.0 %all-gather.18.cloned.1.call-done = bf16[3,384,1024]{2,1,0:T(8,128)(2,1)} async-done(((bf16[3,96,1024]{2,1,0:T(8,128)(2,1)}), bf16[3,384,1024]{2,1,0:T(8,128)(2,1)}) %all-gather.18.cloned.1.call-update) | async-done | bytes 2359312 | tf_op jit(solution)/shard_map/all_gather | solution.py:63
  283.4 34.8 %all-gather.20.cloned.1.call-done.key_ref.value_ref = bf16[3,1536,512]{2,1,0:T(8,128)(2,1)} async-done(((bf16[3,384,512]{2,1,0:T(8,128)(2,1)}), bf16[3,1536,512]{2,1,0:T(8,128)(2,1)}) %all-gather.20.cloned.1.call-update) | async-done | bytes 4718608 | tf_op jit(solution)/shard_map/all_gather | solution.py:378
  324.0 34.1 %attend.1 = (bf16[3,384,256]{2,1,0:T(8,128)(2,1)}, f32[3,384,256]{2,1,0:T(8,128)}) custom-call(s32[1]{0:T(128)} %bitcast.14.start_ref, bf16[3,384,256]{2,1,0:T(8,128)(2,1)} %fusion.20.query_ref, bf16[3,1536,512]{2,1,0:T(8,128)(2,1)} %all-gather.20.cloned.1.call-done.key_ref.value_ref, bf16[3,1536,512]{2,1,0:T(8,128)(2,1)} %all-gather.20.cloned.1.call-done.key_ref.value_ref, ...), custom_call_target="tpu_custom_call" | custom-call | flops 3623878656 | bytes 8388608 | tf_op jit(solution)/shard_map/attend/pallas_call | solution.py:248
  358.1 63.6 %all-gather.36.cloned.1.call-done = bf16[4096,512]{1,0:T(8,128)(2,1)} async-done(((bf16[512,512]{1,0:T(8,128)(2,1)}), bf16[4096,512]{1,0:T(8,128)(2,1)}) %all-gather.36.cloned.1.call-update) | async-done | bytes 4194320 | tf_op jit(solution)/shard_map/all_gather | solution.py:625
  425.0 46.4 %reduce-scatter.16.cloned.1.call-done = bf16[3,96,1024]{2,1,0:T(8,128)(2,1)} async-done(((bf16[3,384,1024]{2,1,0:T(8,128)(2,1)}), bf16[3,96,1024]{2,1,0:T(8,128)(2,1)}) %reduce-scatter.16.cloned.1.call-update) | async-done | bytes 589840 | tf_op jit(solution)/shard_map/reduce_scatter | solution.py:77
  477.2 47.5 %all-gather.24.cloned.1.call-done = bf16[3,384,1024]{2,1,0:T(8,128)(2,1)} async-done(((bf16[3,96,1024]{2,1,0:T(8,128)(2,1)}), bf16[3,384,1024]{2,1,0:T(8,128)(2,1)}) %all-gather.24.cloned.1.call-update) | async-done | bytes 2359312 | tf_op jit(solution)/shard_map/all_gather | solution.py:63
  565.6 45.8 %reduce-scatter.18.cloned.1.call-done = bf16[3,96,1024]{2,1,0:T(8,128)(2,1)} async-done(((bf16[3,384,1024]{2,1,0:T(8,128)(2,1)}), bf16[3,96,1024]{2,1,0:T(8,128)(2,1)}) %reduce-scatter.18.cloned.1.call-update) | async-done | bytes 589840 | tf_op jit(solution)/shard_map/reduce_scatter | solution.py:77
  651.8 30.5 %reduce-scatter.20.cloned.1.call-done = bf16[3,96,1024]{2,1,0:T(8,128)(2,1)} async-done(((bf16[3,384,1024]{2,1,0:T(8,128)(2,1)}), bf16[3,96,1024]{2,1,0:T(8,128)(2,1)}) %reduce-scatter.20.cloned.1.call-update) | async-done | bytes 589840 | tf_op jit(solution)/shard_map/reduce_scatter | solution.py:71
  689.0 23.9 %all-gather.28.cloned.1.call-done = bf16[3,384,1024]{2,1,0:T(8,128)(2,1)} async-done(((bf16[3,96,1024]{2,1,0:T(8,128)(2,1)}), bf16[3,384,1024]{2,1,0:T(8,128)(2,1)}) %all-gather.28.cloned.1.call-update) | async-done | bytes 2359312 | tf_op jit(solution)/shard_map/all_gather | solution.py:67
  740.5 18.8 %reduce-scatter.22.cloned.1.call-done = bf16[3,96,1024]{2,1,0:T(8,128)(2,1)} async-done(((bf16[3,384,1024]{2,1,0:T(8,128)(2,1)}), bf16[3,96,1024]{2,1,0:T(8,128)(2,1)}) %reduce-scatter.22.cloned.1.call-update) | async-done | bytes 589840 | tf_op jit(solution)/shard_map/reduce_scatter | solution.py:71
  763.9 50.1 %all-gather.30.cloned.1.call-done = bf16[3,384,1024]{2,1,0:T(8,128)(2,1)} async-done(((bf16[3,96,1024]{2,1,0:T(8,128)(2,1)}), bf16[3,384,1024]{2,1,0:T(8,128)(2,1)}) %all-gather.30.cloned.1.call-update) | async-done | bytes 2359312 | tf_op jit(solution)/shard_map/all_gather | solution.py:83
  819.1 18.4 %all-reduce.5 = (f32[3,384]{1,0:T(4,128)}, f32[3,384]{1,0:T(4,128)}) all-reduce(f32[3,384]{1,0:T(4,128)} %get-tuple-element.302, f32[3,384]{1,0:T(4,128)} %get-tuple-element.320), channel_id=1, replica_groups=mesh['fsdp'=2,'ctx'=4,'tp'=4] {'tp'}, use_global_device_ids=true, to_apply=%region_26.27 | all-reduce | flops 2304 | bytes 18432 | tf_op jit(solution)/shard_map/psum | solution.py:580
  870.8 38.8 %reduce-scatter.24.cloned.1.call-done = bf16[3,96,1024]{2,1,0:T(8,128)(2,1)} async-done(((bf16[3,384,1024]{2,1,0:T(8,128)(2,1)}), bf16[3,96,1024]{2,1,0:T(8,128)(2,1)}) %reduce-scatter.24.cloned.1.call-update) | async-done | bytes 589840 | tf_op jit(solution)/shard_map/reduce_scatter | solution.py:87
  921.5 43.5 %all-gather.32.cloned.1.call-done = bf16[3,384,1024]{2,1,0:T(8,128)(2,1)} async-done(((bf16[3,96,1024]{2,1,0:T(8,128)(2,1)}), bf16[3,384,1024]{2,1,0:T(8,128)(2,1)}) %all-gather.32.cloned.1.call-update) | async-done | bytes 2359312 | tf_op jit(solution)/shard_map/all_gather | solution.py:83
  970.3 68.7 %attend_back.1 = (bf16[3,384,256]{2,1,0:T(8,128)(2,1)}, bf16[2,3,1536,256]{3,2,1,0:T(8,128)(2,1)}, f32[64,384]{1,0:T(8,128)}) custom-call(s32[1]{0:T(128)} %bitcast.14.start_ref, bf16[3,384,256]{2,1,0:T(8,128)(2,1)} %fusion.20.query_ref, bf16[3,1536,512]{2,1,0:T(8,128)(2,1)} %all-gather.20.cloned.1.call-done.key_ref.value_ref, ...), custom_call_target="tpu_custom_call" | custom-call | flops 9059696640 | bytes 16777216 | tf_op jit(solution)/shard_map/attend_back/pallas_call | solution.py:272
  1039.0 58.2 %reduce-scatter.28.cloned.1.call-done = bf16[512,512]{1,0:T(8,128)(2,1)} async-done(((bf16[4096,512]{1,0:T(8,128)(2,1)}), bf16[512,512]{1,0:T(8,128)(2,1)}) %reduce-scatter.28.cloned.1.call-update) | async-done | bytes 524304 | tf_op jit(solution)/shard_map/reduce_scatter | solution.py:645
  1117.8 29.4 %reduce-scatter.30.cloned.1.call-done = bf16[2,3,384,256]{3,2,1,0:T(8,128)(2,1)} async-done(((bf16[2,3,1536,256]{3,2,1,0:T(8,128)(2,1)}), bf16[2,3,384,256]{3,2,1,0:T(8,128)(2,1)}) %reduce-scatter.30.cloned.1.call-update) | async-done | bytes 1179664 | tf_op jit(solution)/shard_map/reduce_scatter | solution.py:419
  1162.8 38.2 %reduce-scatter.32.cloned.1.call-done = bf16[3,96,1024]{2,1,0:T(8,128)(2,1)} async-done(((bf16[3,384,1024]{2,1,0:T(8,128)(2,1)}), bf16[3,96,1024]{2,1,0:T(8,128)(2,1)}) %reduce-scatter.32.cloned.1.call-update) | async-done | bytes 589840 | tf_op jit(solution)/shard_map/reduce_scatter | solution.py:87
  1256.4 27.8 %reduce-scatter.34.cloned.1.call-done = bf16[128,1152]{1,0:T(8,128)(2,1)} async-done(((bf16[1024,1152]{1,0:T(8,128)(2,1)}), bf16[128,1152]{1,0:T(8,128)(2,1)}) %reduce-scatter.34.cloned.1.call-update) | async-done | bytes 294928 | tf_op jit(solution)/shard_map/reduce_scatter | solution.py:347
  1298.2 21.1 %reduce-scatter.36.cloned.1.call-done = bf16[3,96,1024]{2,1,0:T(8,128)(2,1)} async-done(((bf16[3,384,1024]{2,1,0:T(8,128)(2,1)}), bf16[3,96,1024]{2,1,0:T(8,128)(2,1)}) %reduce-scatter.36.cloned.1.call-update) | async-done | bytes 589840 | tf_op jit(solution)/shard_map/reduce_scatter | solution.py:71
  (588 shorter events, 531.4 us)
Async XLA Ops:
  7.2 160.7 %all-gather.14.cloned.1.call-start = ((), (), s32[]{:S(2)}) async-start(), calls=%async_computation.21 | async-start | bytes 2949120 | tf_op jit(solution)/shard_map/all_gather | solution.py:67
  11.2 156.8 %all-gather.16.cloned.1.call-start = ((), (), s32[]{:S(2)}) async-start(), calls=%async_computation.22 | async-start | bytes 2359296 | tf_op jit(solution)/shard_map/all_gather | solution.py:625
  26.6 197.8 %reduce-scatter.14.cloned.1.call-start = ((), (), s32[]{:S(2)}) async-start(), calls=%async_computation.23 | async-start | bytes 2949120 | tf_op jit(solution)/shard_map/reduce_scatter | solution.py:71
  182.7 95.0 %all-gather.18.cloned.1.call-start = ((), (), s32[]{:S(2)}) async-start(), calls=%async_computation.24 | async-start | bytes 2949120 | tf_op jit(solution)/shard_map/all_gather | solution.py:63
  242.8 75.4 %all-gather.20.cloned.1.call-start = ((), (), s32[]{:S(2)}) async-start(), calls=%async_computation.25 | async-start | bytes 5898240 | tf_op jit(solution)/shard_map/all_gather | solution.py:378
  281.8 76.3 %all-gather.22.cloned.1.call-start = ((), (), s32[]{:S(2)}) async-start(), calls=%async_computation.26 | async-start | bytes 1769472 | tf_op jit(solution)/shard_map/all_gather | solution.py:649
  318.2 103.5 %all-gather.36.cloned.1.call-start = ((), (), s32[]{:S(2)}) async-start(), calls=%async_computation.45 | async-start | bytes 4718592 | tf_op jit(solution)/shard_map/all_gather | solution.py:625
  318.9 152.4 %reduce-scatter.16.cloned.1.call-start = ((), (), s32[]{:S(2)}) async-start(), calls=%async_computation.27 | async-start | bytes 2949120 | tf_op jit(solution)/shard_map/reduce_scatter | solution.py:77
  425.0 99.7 %all-gather.24.cloned.1.call-start = ((), (), s32[]{:S(2)}) async-start(), calls=%async_computation.28 | async-start | bytes 2949120 | tf_op jit(solution)/shard_map/all_gather | solution.py:63
  475.2 136.3 %reduce-scatter.18.cloned.1.call-start = ((), (), s32[]{:S(2)}) async-start(), calls=%async_computation.29 | async-start | bytes 2949120 | tf_op jit(solution)/shard_map/reduce_scatter | solution.py:77
  565.6 72.5 %all-gather.26.cloned.1.call-start = ((), (), s32[]{:S(2)}) async-start(), calls=%async_computation.30 | async-start | bytes 2949120 | tf_op jit(solution)/shard_map/all_gather | solution.py:67
  614.5 67.8 %reduce-scatter.20.cloned.1.call-start = ((), (), s32[]{:S(2)}) async-start(), calls=%async_computation.31 | async-start | bytes 2949120 | tf_op jit(solution)/shard_map/reduce_scatter | solution.py:71
  688.7 70.6 %reduce-scatter.22.cloned.1.call-start = ((), (), s32[]{:S(2)}) async-start(), calls=%async_computation.33 | async-start | bytes 2949120 | tf_op jit(solution)/shard_map/reduce_scatter | solution.py:71
  726.4 87.6 %all-gather.30.cloned.1.call-start = ((), (), s32[]{:S(2)}) async-start(), calls=%async_computation.34 | async-start | bytes 2949120 | tf_op jit(solution)/shard_map/all_gather | solution.py:83
  763.9 145.7 %reduce-scatter.24.cloned.1.call-start = ((), (), s32[]{:S(2)}) async-start(), calls=%async_computation.35 | async-start | bytes 2949120 | tf_op jit(solution)/shard_map/reduce_scatter | solution.py:87
  863.0 102.0 %all-gather.32.cloned.1.call-start = ((), (), s32[]{:S(2)}) async-start(), calls=%async_computation.36 | async-start | bytes 2949120 | tf_op jit(solution)/shard_map/all_gather | solution.py:83
  915.5 123.5 %reduce-scatter.26.cloned.1.call-start = ((), (), s32[]{:S(2)}) async-start(), calls=%async_computation.37 | async-start | bytes 1769472 | tf_op jit(solution)/shard_map/reduce_scatter | solution.py:402
  965.0 132.2 %reduce-scatter.28.cloned.1.call-start = ((), (), s32[]{:S(2)}) async-start(), calls=%async_computation.38 | async-start | bytes 4718592 | tf_op jit(solution)/shard_map/reduce_scatter | solution.py:645
  965.8 181.4 %reduce-scatter.30.cloned.1.call-start = ((), (), s32[]{:S(2)}) async-start(), calls=%async_computation.39 | async-start | bytes 5898240 | tf_op jit(solution)/shard_map/reduce_scatter | solution.py:419
  1111.0 90.1 %reduce-scatter.32.cloned.1.call-start = ((), (), s32[]{:S(2)}) async-start(), calls=%async_computation.40 | async-start | bytes 2949120 | tf_op jit(solution)/shard_map/reduce_scatter | solution.py:87
  1153.2 89.1 %all-gather.34.cloned.1.call-start = ((), (), s32[]{:S(2)}) async-start(), calls=%async_computation.41 | async-start | bytes 2949120 | tf_op jit(solution)/shard_map/all_gather | solution.py:67
  1205.6 78.5 %reduce-scatter.34.cloned.1.call-start = ((), (), s32[]{:S(2)}) async-start(), calls=%async_computation.42 | async-start | bytes 2654208 | tf_op jit(solution)/shard_map/reduce_scatter | solution.py:347
  1242.3 77.1 %reduce-scatter.36.cloned.1.call-start = ((), (), s32[]{:S(2)}) async-start(), calls=%async_computation.43 | async-start | bytes 2949120 | tf_op jit(solution)/shard_map/reduce_scatter | solution.py:71
  1284.2 130.5 %reduce-scatter.38.cloned.1.call-start = ((), (), s32[]{:S(2)}) async-start(), calls=%async_computation.44 | async-start | bytes 4718592 | tf_op jit(solution)/shard_map/reduce_scatter | solution.py:645
  (159 other events, 1655.6 us)
Sparse Core Ops, SparseCore 0:
  11.3 29.5 all-gather.13
  43.6 57.0 all-gather.15
  182.8 34.4 reduce-scatter.13
  228.6 49.0 all-gather.17
  281.9 36.1 all-gather.19
  320.5 25.5 all-gather.21
  348.8 72.8 all-gather.35
  425.1 46.2 reduce-scatter.15
  475.3 49.3 all-gather.23
  565.7 45.6 reduce-scatter.17
  614.6 23.4 all-gather.25
  649.5 32.7 reduce-scatter.19
  688.8 24.0 all-gather.27
  726.5 32.7 reduce-scatter.21
  764.0 49.9 all-gather.29
  863.1 46.3 reduce-scatter.23
  915.6 49.3 all-gather.31
  968.1 37.1 reduce-scatter.25
  1008.9 88.2 reduce-scatter.27
  1099.6 47.4 reduce-scatter.29
  1153.3 47.7 reduce-scatter.31
  1242.4 41.7 reduce-scatter.33
  1286.6 32.7 reduce-scatter.35
  1324.2 90.3 reduce-scatter.37
  (1 shorter events, 23.4 us)

commit v6 on v4

--- a/solution.py
+++ b/solution.py
@@ -136,7 +136,7 @@
     return col - 128 - row
 
 
-def attend_kernel(reach, start_ref, query_ref, key_ref, value_ref, table_ref, mixed_ref, total_ref, place):
+def attend_kernel(reach, start_ref, query_ref, key_ref, value_ref, table_ref, mixed_ref, probs_ref, place):
     rows = query_ref.shape[1]
     rows_at = start_ref[0] + pl.program_id(2) * rows
     table = table_ref[...]
@@ -149,11 +149,11 @@
         row_sum = jnp.sum(powers, axis=-1, keepdims=True)
         probs = (powers * (1.0 / row_sum)).astype(jnp.bfloat16)
         mixed_ref[0, :, lanes] = dot_n(probs, value_ref[0, :, lanes]).astype(jnp.bfloat16)
-        total_ref[0, :, lanes] = jnp.broadcast_to(top + jnp.log(row_sum), (rows, HEAD))
+        probs_ref[0, half] = probs
 
 
 def attend_back_kernel(
-    reach, start_ref, query_ref, key_ref, value_ref, table_ref, total_ref, grad_ref, groups_ref,
+    reach, start_ref, query_ref, key_ref, value_ref, table_ref, probs_ref, grad_ref, groups_ref,
     query_grad_ref, pair_grad_ref, table_grad_ref, place, key_sum, value_sum,
 ):
     rows = query_ref.shape[1]
@@ -177,12 +177,12 @@
         query_block = query_ref[0, :, lanes] * scale
         keys = key_ref[0, :, lanes]
         grad_block = grad_ref[0, :, lanes]
-        scores = scaled_scores(query_block, keys, table, place, rows_at, reach)
-        probs = jnp.exp(scores - total_ref[0, :, half * HEAD : half * HEAD + 1])
+        probs_low = probs_ref[0, half]
+        probs = probs_low.astype(jnp.float32)
         grad_probs = dot_t(grad_block, value_ref[0, :, lanes])
         row_dot = jnp.sum(probs * grad_probs, axis=-1, keepdims=True)
         grad_scores = (probs * (grad_probs - row_dot)).astype(jnp.bfloat16)
-        value_sum[lanes, :] += dot_n(grad_block.T, probs.astype(jnp.bfloat16))
+        value_sum[lanes, :] += dot_n(grad_block.T, probs_low)
         key_sum[lanes, :] += dot_n(query_block.T, grad_scores)
         wide = grad_scores.astype(jnp.float32)
         place[:, 128 : 128 + key_count] = wide
@@ -230,22 +230,26 @@
     table = pl.BlockSpec((BAND, HEAD), lambda s, p, b, *_: (0, 0))
     place = pltpu.VMEM((block, keys.shape[1] + 256), jnp.float32)
     flops = slots * rows * keys.shape[1] * width * 4
-    return grid, by_query, by_key, by_value, table, place, flops
+    by_prob = pl.BlockSpec((1, 2, block, keys.shape[1]), lambda s, p, b, *_: (s, p, b, 0))
+    return grid, by_query, by_key, by_value, by_prob, table, place, flops
 
 
 def attend(queries, pairs, table, reach, query_start):
-    grid, by_query, by_key, by_value, by_table, place, flops = attend_specs(queries, pairs)
+    grid, by_query, by_key, by_value, by_prob, by_table, place, flops = attend_specs(queries, pairs)
     return pl.pallas_call(
         functools.partial(attend_kernel, reach),
         out_shape=(
             jax.ShapeDtypeStruct(queries.shape, jnp.bfloat16),
-            jax.ShapeDtypeStruct(queries.shape, jnp.float32),
+            jax.ShapeDtypeStruct(
+                queries.shape[:1] + (queries.shape[2] // HEAD, queries.shape[1], pairs.shape[1]),
+                jnp.bfloat16,
+            ),
         ),
         grid_spec=pltpu.PrefetchScalarGridSpec(
             num_scalar_prefetch=1,
             grid=grid,
             in_specs=[by_query, by_key, by_value, by_table],
-            out_specs=(by_query, by_query),
+            out_specs=(by_query, by_prob),
             scratch_shapes=[place],
         ),
         cost_estimate=pl.CostEstimate(flops=2 * flops, bytes_accessed=8 << 20, transcendentals=flops >> 8),
@@ -254,7 +258,7 @@
 
 
 def attend_back(queries, pairs, table, totals, grad_mixed, reach, query_start):
-    grid, by_query, by_key, by_value, by_table, place, flops = attend_specs(queries, pairs)
+    grid, by_query, by_key, by_value, by_prob, by_table, place, flops = attend_specs(queries, pairs)
     slots, key_count = pairs.shape[:2]
     turned = pltpu.VMEM((2 * HEAD, key_count), jnp.float32)
     group = jnp.arange(key_count, dtype=jnp.int32)[:, None] // 128
@@ -274,7 +278,7 @@
                 by_key,
                 by_value,
                 by_table,
-                by_query,
+                by_prob,
                 by_query,
                 pl.BlockSpec((key_count, 128), lambda s, p, b, *_: (0, 0)),
             ],
@@ -323,22 +327,29 @@
     return (stream + 0.5 * branch, saved, weight_in, weight_out, later)
 
 
-def ffn_backward(grad_stream, saved, norm_gain, weight_in, weight_out):
+def ffn_backward(grad_stream, saved, norm_gain, weight_in, weight_out, beside=None):
     standard, inverse, wide_rows, hidden_pre = saved
     grad_branch = (0.5 * grad_stream).astype(jnp.bfloat16)
     out_bias_grad = jnp.sum(grad_branch.astype(jnp.float32), axis=(0, 1))
     wide_grad = widen_grad(grad_branch)
+    if beside is not None:
+        wide_grad, beside = together(wide_grad, beside)
+        beside = lax.psum_scatter(beside, ("fsdp", "ctx"), scatter_dimension=0, tiled=True)
     active = jax.nn.silu(hidden_pre).astype(jnp.bfloat16)
     out_grad = weight_sum(wide_grad, active)
     grad_pre = (rows_in(wide_grad, weight_out) * silu_slope(hidden_pre)).astype(jnp.bfloat16)
     in_bias_grad = jnp.sum(grad_pre.astype(jnp.float32), axis=(0, 1))
     in_grad = weight_sum(wide_rows, grad_pre)
-    grad_normed = narrow_grad(rows_out(grad_pre, weight_in))
+    partial_rows = rows_out(grad_pre, weight_in).astype(jnp.bfloat16)
+    if beside is not None:
+        partial_rows, beside = together(partial_rows, beside)
+    grad_normed = narrow_grad(partial_rows)
     grad_normed, in_grad, out_grad = together(grad_normed, in_grad, out_grad)
     grad_in, gain_grad, shift_grad = norm_backward(grad_normed, standard, inverse, norm_gain)
     return (
         grad_stream + grad_in,
         (gain_grad, shift_grad, in_grad, in_bias_grad, out_grad, out_bias_grad),
+        beside,
     )
 
 
@@ -422,6 +433,11 @@
     )
 
 
+def sum_rows(first, second):
+    every = lax.all_gather(jnp.stack([first, second]), "tp", axis=0, tiled=False)
+    return jnp.sum(every, axis=0)
+
+
 def conv_forward(stream, norm_gain, norm_shift, weights, depth_local, inner_gain, inner_offset):
     value_w, gate_w, out_w = weights
     normed, standard, inverse = norm_forward(stream, norm_gain, norm_shift)
@@ -440,9 +456,7 @@
             convolved
             + depth_local[tap_index] * padded_float[:, tap_index : tap_index + row_count, :]
         )
-    row_sums = lax.psum(
-        (jnp.sum(convolved, axis=-1), jnp.sum(convolved * convolved, axis=-1)), "tp"
-    )
+    row_sums = sum_rows(jnp.sum(convolved, axis=-1), jnp.sum(convolved * convolved, axis=-1))
     row_mean = (row_sums[0] / D)[..., None]
     row_var = (row_sums[1] / D)[..., None] - row_mean * row_mean
     inner_inverse = lax.rsqrt(row_var + epsilon)
@@ -543,8 +557,8 @@
     inner_gain_grad = jnp.sum(grad_inner * inner_standard, axis=(0, 1))
     inner_shift_grad = jnp.sum(grad_inner, axis=(0, 1))
     grad_standard = grad_inner * inner_gain
-    row_sums = lax.psum(
-        (jnp.sum(grad_standard, axis=-1), jnp.sum(grad_standard * inner_standard, axis=-1)), "tp"
+    row_sums = sum_rows(
+        jnp.sum(grad_standard, axis=-1), jnp.sum(grad_standard * inner_standard, axis=-1)
     )
     grad_conv = inner_inverse * (
         grad_standard - (row_sums[0] / D)[..., None] - inner_standard * (row_sums[1] / D)[..., None]
@@ -598,15 +612,21 @@
     return tuple(pieces)
 
 
-def scatter_sum_all(grads, whole_parts, split_parts, own_parts):
-    rows = grads[0].shape[0]
+def small_columns(whole_parts, split_parts, rows):
     flat = jnp.concatenate([part.reshape(-1) for part in whole_parts + split_parts])
     columns = -(-flat.shape[0] // rows)
     flat = jnp.pad(flat, (0, rows * columns - flat.shape[0])).reshape(rows, columns)
-    parts = scatter_sum(*grads, jnp.pad(flat, ((0, 0), (0, -columns % 128))))
-    small = parts[-1][:, :columns].reshape(-1)
+    return jnp.pad(flat, ((0, 0), (0, -columns % 128)))
+
+
+def finish_small(small, whole_parts, split_parts, own_parts, hidden_part):
+    rows = small.shape[0] * lax.axis_size(("fsdp", "ctx"))
+    count = sum(part.size for part in whole_parts + split_parts)
+    small = small[:, : -(-count // rows)].astype(jnp.float32).reshape(-1)
     held = small.shape[0]
-    sent = jnp.concatenate([small] + [part.reshape(-1) for part in own_parts])
+    sent = jnp.concatenate(
+        [small] + [part.reshape(-1) for part in own_parts] + [hidden_part.reshape(-1)]
+    )
     sent = jnp.pad(sent, (0, -sent.shape[0] % 128)).reshape(1, -1, 128)
     tp_count = lax.axis_size("tp")
     every = lax.all_gather(sent, "tp", axis=0, tiled=True)
@@ -629,16 +649,17 @@
             piece = piece.reshape((tp_count,) + part.shape)
             pieces.append(piece.transpose(1, 0, 2).reshape(part.shape[0], -1))
         start += part.size
-    own = jnp.sum(every[:, :, held:], axis=(0, 1))
+    own = jnp.sum(every[:, :, held:], axis=0)
+    owned = []
     start = 0
-    owned = []
     for part in own_parts:
-        owned.append(own[start : start + part.size].reshape(part.shape))
+        owned.append(jnp.sum(own[:, start : start + part.size], axis=0).reshape(part.shape))
         start += part.size
-    w, p = owned[:2] + whole + owned[2:], pieces
-    return parts[:-1], (
-        w[0], w[1], p[0], w[2], w[3], w[4], p[1], p[2], w[5], w[6], w[7], w[8],
-        p[3], p[4], p[5], w[9], w[10], p[6], w[11], w[12], w[13], w[14],
+    hidden = own[:, start : start + hidden_part.size].reshape(-1)
+    w, p = whole, pieces
+    return (
+        owned[0], owned[1], hidden, owned[2], w[0], w[1], p[0], p[1], w[2], w[3], w[4], w[5],
+        p[2], p[3], p[4], w[6], w[7], p[5], w[8], w[9], w[10], owned[3],
     )
 
 
@@ -750,7 +771,7 @@
     gradient_fourth, final_gain_grad, final_shift_grad = norm_backward(
         2.0 * misfit, final_standard, final_inverse, final_gain
     )
-    grad_three, ffn2_grads = ffn_backward(
+    grad_three, ffn2_grads, _ = ffn_backward(
         gradient_fourth, saved_four, ffn2_gain, ffn2_in_all, ffn2_out_all
     )
     grad_two, conv_grads = conv_backward(
@@ -770,37 +791,44 @@
         ctx_rank,
         (ffn2_grads[2], ffn2_grads[4], conv_grads[2], conv_grads[3], conv_grads[7]),
     )
-    grad_zero, ffn1_grads = ffn_backward(
-        grad_one, saved_one, ffn1_gain, ffn1_in_all, ffn1_out_all
-    )
-    attn_parts = scatter_sum(attn_grads[2], attn_grads[4], attn_grads[5], attn_grads[7])
-    ffn1_parts, shared = scatter_sum_all(
-        (ffn1_grads[2], ffn1_grads[4]),
-        (
-            ffn1_grads[5],
-            attn_grads[0],
-            attn_grads[1],
-            attn_grads[8],
-            attn_grads[9],
-            conv_grads[0],
-            conv_grads[1],
-            ffn2_grads[0],
-            ffn2_grads[1],
-            ffn2_grads[5],
-            final_gain_grad,
-            final_shift_grad,
-        ),
-        (
-            ffn1_grads[3],
-            attn_grads[3],
-            attn_grads[6],
-            conv_grads[4],
-            conv_grads[5],
-            conv_grads[6],
-            ffn2_grads[3],
-        ),
-        (ffn1_grads[0], ffn1_grads[1], sse_local),
-    )
+    attn_mats = (attn_grads[2], attn_grads[4], attn_grads[5], attn_grads[7])
+    whole_parts = (
+        attn_grads[0],
+        attn_grads[1],
+        attn_grads[8],
+        attn_grads[9],
+        conv_grads[0],
+        conv_grads[1],
+        ffn2_grads[0],
+        ffn2_grads[1],
+        ffn2_grads[5],
+        final_gain_grad,
+        final_shift_grad,
+    )
+    split_parts = (
+        attn_grads[3],
+        attn_grads[6],
+        conv_grads[4],
+        conv_grads[5],
+        conv_grads[6],
+        ffn2_grads[3],
+    )
+    columns = small_columns(whole_parts, split_parts, attn_mats[0].shape[0])
+    beside_mats = attn_mats + (columns,)
+    beside = jnp.concatenate([part.astype(jnp.bfloat16) for part in beside_mats], axis=1)
+    grad_zero, ffn1_grads, beside = ffn_backward(
+        grad_one, saved_one, ffn1_gain, ffn1_in_all, ffn1_out_all, beside
+    )
+    attn_parts = split_columns(beside, beside_mats)
+    ffn1_parts = scatter_sum(ffn1_grads[2], ffn1_grads[4])
+    shared = finish_small(
+        attn_parts[-1],
+        whole_parts,
+        split_parts,
+        (ffn1_grads[0], ffn1_grads[1], ffn1_grads[5], sse_local),
+        ffn1_grads[3],
+    )
+    attn_parts = attn_parts[:-1]
     weight_parts = ffn1_parts + attn_parts + inner_parts[2:] + inner_parts[:2]
     token_count = (jnp.sum(clips_dev) * SEQ).astype(jnp.float32)
     loss = shared[21] / token_count

time: 1360 us -> 1320 us (0.971)
  waiting for transfers between devices: 791 us -> 747 us
  local copies, waits for them, and re-layouts: 66.4 us -> 86.6 us
    reduce_scatter x2 -> x1, waiting for transfers between devices: 81.7 us -> 0.01 us  [scatter_sum(): lax.psum_scatter(joined, ('fsdp', 'ctx'), scatter_dimension=0, tiled=True)]
    psum x2 -> x0, blocking collectives: 36.2 us -> none  [the longest x1 18.3 us: conv_forward(): lax.psum((jnp.sum(convolved, axis=-1), jnp.sum(convolved * convolved, axi...]
    reduce_scatter x4, waiting for transfers between devices: 112 us -> 146 us  [narrow_grad(): lax.psum_scatter(partial_rows.astype(jnp.bfloat16), 'tp', scatter_dimensi...]
    all_gather x4, waiting for transfers between devices: 190 us -> 158 us  [widen_grad(): return lax.all_gather(grad_branch, 'tp', axis=1, tiled=True)]
    all_gather x2 -> x4, blocking collectives: 23.7 us -> 54.7 us  [the longest x2 27.6 us: sum_rows(): lax.all_gather(jnp.stack([first, second]), 'tp', axis=0, tiled=False)]
    reduce_scatter x0 -> x1, waiting for transfers between devices: none -> 30.8 us  [ffn_backward(): lax.psum_scatter(beside, ('fsdp', 'ctx'), scatter_dimension=0, tiled=True)]
    unnamed x280 -> x278, local copies, waits for them, and re-layouts: 27 us -> 35.3 us
  transfers between devices with their start and end apart: 25 -> 25, of which waited for: 22 -> 21; matrix products, arithmetic and copies ran while one was open for 10% -> 13% of each run, Pallas kernels for 8% -> 7%
where the time goes in v6:
time: 1320 us; the launch traced here: 1310 us
  waiting for transfers between devices  747 us (57%)
  matrix products  135 us (10%)
  blocking collectives  132 us (10%)
  Pallas kernels  103 us (8%)
  local copies, waits for them, and re-layouts  86.6 us (7%)
  other arithmetic  81.3 us (6%)
  between operations  18.2 us (1%)
    all_gather x4, waiting for transfers between devices, widen_grad(): return lax.all_gather(grad_branch, 'tp', axis=1, tiled=True)  158 us
    all_gather x4, waiting for transfers between devices, widen(): return lax.all_gather(normed.astype(jnp.bfloat16), 'tp', axis=1, tiled=True)  157 us
    reduce_scatter x4, waiting for transfers between devices, narrow_grad(): lax.psum_scatter(partial_rows.astype(jnp.bfloat16), 'tp', scatter_dimensi...  146 us
    reduce_scatter x3, waiting for transfers between devices, narrow(): lax.psum_scatter(partial_rows.astype(jnp.bfloat16), 'tp', scatter_dimensi...  139 us
    all_gather x8, blocking collectives, gather_rows(): return lax.all_gather(shard, ('fsdp', 'ctx'), axis=0, tiled=True)  77.1 us
    pallas_call x1, Pallas kernels, attend_back(): pl.pallas_call(functools.partial(attend_back_kernel, reach), out_shape=(j...  56.6 us
    dot_general x10, matrix products, rows_in(): jnp.einsum('zub,bx->zux', left_reach, right_reach, preferred_element_type...  48.6 us
    reduce_scatter x1, waiting for transfers between devices, attn_backward(): lax.psum_scatter(pair_terms, 'ctx', scatter_dimension=2, tiled=True)  46 us
  transfers between devices with their start and end apart: 25, of which 21 were waited for; matrix products, arithmetic and copies ran while one was open for 13% of the time, Pallas kernels for 7%

profile of v6, /device:TPU:0, one launch (start us, length us, event | category | flops | bytes accessed | tf_op | source)
XLA Modules:
  0.0 1308.1 jit_solution(265675915206077819)
XLA Ops:
  71.0 21.5 %all-gather.16.cloned.1.call-done = bf16[1024,1024]{1,0:T(8,128)(2,1)} async-done(((bf16[128,1024]{1,0:T(8,128)(2,1)}), bf16[1024,1024]{1,0:T(8,128)(2,1)}) %all-gather.16.cloned.1.call-update) | async-done | bytes 2097168 | tf_op jit(solution)/shard_map/all_gather | solution.py:597
  152.0 48.2 %all-gather.18.cloned.1.call-done = bf16[3,384,1024]{2,1,0:T(8,128)(2,1)} async-done(((bf16[3,96,1024]{2,1,0:T(8,128)(2,1)}), bf16[3,384,1024]{2,1,0:T(8,128)(2,1)}) %all-gather.18.cloned.1.call-update) | async-done | bytes 2359312 | tf_op jit(solution)/shard_map/all_gather | solution.py:63
  207.9 32.8 %all-gather.20.cloned.1.call-done.key_ref.value_ref = bf16[3,1536,512]{2,1,0:T(8,128)(2,1)} async-done(((bf16[3,384,512]{2,1,0:T(8,128)(2,1)}), bf16[3,1536,512]{2,1,0:T(8,128)(2,1)}) %all-gather.20.cloned.1.call-update) | async-done | bytes 4718608 | tf_op jit(solution)/shard_map/all_gather | solution.py:365
  245.8 34.6 %attend.1 = (bf16[3,384,256]{2,1,0:T(8,128)(2,1)}, bf16[3,4,384,1536]{3,2,1,0:T(8,128)(2,1)}) custom-call(s32[1]{0:T(128)} %bitcast.2.start_ref, bf16[3,384,256]{2,1,0:T(8,128)(2,1)} %fusion.32.query_ref, bf16[3,1536,512]{2,1,0:T(8,128)(2,1)} %all-gather.20.cloned.1.call-done.key_ref.value_ref, ...), custom_call_target="tpu_custom_call" | custom-call | flops 3623878656 | bytes 8388608 | tf_op jit(solution)/shard_map/attend/pallas_call | solution.py:239
  289.0 47.8 %reduce-scatter.15.cloned.1.call-done = bf16[3,96,1024]{2,1,0:T(8,128)(2,1)} async-done(((bf16[3,384,1024]{2,1,0:T(8,128)(2,1)}), bf16[3,96,1024]{2,1,0:T(8,128)(2,1)}) %reduce-scatter.15.cloned.1.call-update) | async-done | bytes 589840 | tf_op jit(solution)/shard_map/reduce_scatter | solution.py:67
  342.1 47.5 %all-gather.24.cloned.1.call-done = bf16[3,384,1024]{2,1,0:T(8,128)(2,1)} async-done(((bf16[3,96,1024]{2,1,0:T(8,128)(2,1)}), bf16[3,384,1024]{2,1,0:T(8,128)(2,1)}) %all-gather.24.cloned.1.call-update) | async-done | bytes 2359312 | tf_op jit(solution)/shard_map/all_gather | solution.py:63
  407.5 13.8 %all-gather = f32[8,3,384]{2,1,0:T(4,128)} all-gather(f32[2,3,384]{2,1,0:T(4,128)S(1)} %pad_maximum_fusion.3), channel_id=2, replica_groups=mesh['fsdp'=2,'ctx'=4,'tp'=4] {'tp'}, dimensions={0}, use_global_device_ids=true | all-gather | bytes 46080 | tf_op jit(solution)/shard_map/all_gather | solution.py:437
  426.3 46.8 %reduce-scatter.17.cloned.1.call-done = bf16[3,96,1024]{2,1,0:T(8,128)(2,1)} async-done(((bf16[3,384,1024]{2,1,0:T(8,128)(2,1)}), bf16[3,96,1024]{2,1,0:T(8,128)(2,1)}) %reduce-scatter.17.cloned.1.call-update) | async-done | bytes 589840 | tf_op jit(solution)/shard_map/reduce_scatter | solution.py:67
  477.2 48.6 %all-gather.26.cloned.1.call-done = bf16[3,384,1024]{2,1,0:T(8,128)(2,1)} async-done(((bf16[3,96,1024]{2,1,0:T(8,128)(2,1)}), bf16[3,384,1024]{2,1,0:T(8,128)(2,1)}) %all-gather.26.cloned.1.call-update) | async-done | bytes 2359312 | tf_op jit(solution)/shard_map/all_gather | solution.py:63
  540.8 44.3 %reduce-scatter.19.cloned.1.call-done = bf16[3,96,1024]{2,1,0:T(8,128)(2,1)} async-done(((bf16[3,384,1024]{2,1,0:T(8,128)(2,1)}), bf16[3,96,1024]{2,1,0:T(8,128)(2,1)}) %reduce-scatter.19.cloned.1.call-update) | async-done | bytes 589840 | tf_op jit(solution)/shard_map/reduce_scatter | solution.py:67
  591.9 49.5 %all-gather.28.cloned.1.call-done = bf16[3,384,1024]{2,1,0:T(8,128)(2,1)} async-done(((bf16[3,96,1024]{2,1,0:T(8,128)(2,1)}), bf16[3,384,1024]{2,1,0:T(8,128)(2,1)}) %all-gather.28.cloned.1.call-update) | async-done | bytes 2359312 | tf_op jit(solution)/shard_map/all_gather | solution.py:73
  670.1 32.8 %reduce-scatter.21.cloned.1.call-done = bf16[3,96,1024]{2,1,0:T(8,128)(2,1)} async-done(((bf16[3,384,1024]{2,1,0:T(8,128)(2,1)}), bf16[3,96,1024]{2,1,0:T(8,128)(2,1)}) %reduce-scatter.21.cloned.1.call-update) | async-done | bytes 589840 | tf_op jit(solution)/shard_map/reduce_scatter | solution.py:77
  708.0 49.5 %all-gather.30.cloned.1.call-done = bf16[3,384,1024]{2,1,0:T(8,128)(2,1)} async-done(((bf16[3,96,1024]{2,1,0:T(8,128)(2,1)}), bf16[3,384,1024]{2,1,0:T(8,128)(2,1)}) %all-gather.30.cloned.1.call-update) | async-done | bytes 2359312 | tf_op jit(solution)/shard_map/all_gather | solution.py:73
  762.4 13.8 %all-gather.1 = f32[8,3,384]{2,1,0:T(4,128)} all-gather(f32[2,3,384]{2,1,0:T(4,128)S(1)} %pad_maximum_fusion.4), channel_id=3, replica_groups=mesh['fsdp'=2,'ctx'=4,'tp'=4] {'tp'}, dimensions={0}, use_global_device_ids=true | all-gather | bytes 46080 | tf_op jit(solution)/shard_map/all_gather | solution.py:437
  811.7 39.2 %reduce-scatter.23.cloned.1.call-done = bf16[3,96,1024]{2,1,0:T(8,128)(2,1)} async-done(((bf16[3,384,1024]{2,1,0:T(8,128)(2,1)}), bf16[3,96,1024]{2,1,0:T(8,128)(2,1)}) %reduce-scatter.23.cloned.1.call-update) | async-done | bytes 589840 | tf_op jit(solution)/shard_map/reduce_scatter | solution.py:77
  863.3 41.6 %all-gather.32.cloned.1.call-done = bf16[3,384,1024]{2,1,0:T(8,128)(2,1)} async-done(((bf16[3,96,1024]{2,1,0:T(8,128)(2,1)}), bf16[3,384,1024]{2,1,0:T(8,128)(2,1)}) %all-gather.32.cloned.1.call-update) | async-done | bytes 2359312 | tf_op jit(solution)/shard_map/all_gather | solution.py:73
  909.4 56.6 %attend_back.1 = (bf16[3,384,256]{2,1,0:T(8,128)(2,1)}, bf16[2,3,1536,256]{3,2,1,0:T(8,128)(2,1)}, f32[64,384]{1,0:T(8,128)}) custom-call(s32[1]{0:T(128)} %bitcast.2.start_ref, bf16[3,384,256]{2,1,0:T(8,128)(2,1)} %fusion.32.query_ref, bf16[3,1536,512]{2,1,0:T(8,128)(2,1)} %all-gather.20.cloned.1.call-done.key_ref.value_ref, ...), custom_call_target="tpu_custom_call" | custom-call | flops 9059696640 | bytes 16777216 | tf_op jit(solution)/shard_map/attend_back/pallas_call | solution.py:266
  970.2 46.0 %reduce-scatter.27.cloned.1.call-done = bf16[2,3,384,256]{3,2,1,0:T(8,128)(2,1)} async-done(((bf16[2,3,1536,256]{3,2,1,0:T(8,128)(2,1)}), bf16[2,3,384,256]{3,2,1,0:T(8,128)(2,1)}) %reduce-scatter.27.cloned.1.call-update) | async-done | bytes 1179664 | tf_op jit(solution)/shard_map/reduce_scatter | solution.py:404
  1032.0 38.2 %reduce-scatter.29.cloned.1.call-done = bf16[3,96,1024]{2,1,0:T(8,128)(2,1)} async-done(((bf16[3,384,1024]{2,1,0:T(8,128)(2,1)}), bf16[3,96,1024]{2,1,0:T(8,128)(2,1)}) %reduce-scatter.29.cloned.1.call-update) | async-done | bytes 589840 | tf_op jit(solution)/shard_map/reduce_scatter | solution.py:77
  1106.4 17.8 %all-gather.34.cloned.1.call-done = bf16[3,384,1024]{2,1,0:T(8,128)(2,1)} async-done(((bf16[3,96,1024]{2,1,0:T(8,128)(2,1)}), bf16[3,384,1024]{2,1,0:T(8,128)(2,1)}) %all-gather.34.cloned.1.call-update) | async-done | bytes 2359312 | tf_op jit(solution)/shard_map/all_gather | solution.py:73
  1137.9 30.8 %reduce-scatter.31.cloned.1.call-done = bf16[128,1152]{1,0:T(8,128)(2,1)} async-done(((bf16[1024,1152]{1,0:T(8,128)(2,1)}), bf16[128,1152]{1,0:T(8,128)(2,1)}) %reduce-scatter.31.cloned.1.call-update) | async-done | bytes 294928 | tf_op jit(solution)/shard_map/reduce_scatter | solution.py:337
  1182.7 36.1 %reduce-scatter.33.cloned.1.call-done = bf16[3,96,1024]{2,1,0:T(8,128)(2,1)} async-done(((bf16[3,384,1024]{2,1,0:T(8,128)(2,1)}), bf16[3,96,1024]{2,1,0:T(8,128)(2,1)}) %reduce-scatter.33.cloned.1.call-update) | async-done | bytes 589840 | tf_op jit(solution)/shard_map/reduce_scatter | solution.py:77
  1241.7 13.4 %all_gather.98 = f32[4,58,128]{2,1,0:T(8,128)S(1)} all-gather(f32[1,58,128]{2,1,0:T(8,128)S(1)} %pad_bitcast_fusion), channel_id=1, replica_groups=mesh['fsdp'=2,'ctx'=4,'tp'=4] {'tp'}, dimensions={0}, use_global_device_ids=true | all-gather | bytes 148480 | tf_op jit(solution)/shard_map/all_gather | solution.py:632
  1255.1 13.7 %all_gather.99 = f32[32,58,128]{2,1,0:T(8,128)} all-gather(f32[4,58,128]{2,1,0:T(8,128)S(1)} %all_gather.98), channel_id=1, replica_groups=mesh['fsdp'=2,'ctx'=4,'tp'=4] {'fsdp','ctx'}, dimensions={0}, use_global_device_ids=true | all-gather | bytes 1069056 | tf_op jit(solution)/shard_map/all_gather | solution.py:633
  (493 shorter events, 425.1 us)
Async XLA Ops:
  7.2 56.8 %all-gather.14.cloned.1.call-start = ((), (), s32[]{:S(2)}) async-start(), calls=%async_computation.12 | async-start | bytes 2949120 | tf_op jit(solution)/shard_map/all_gather | solution.py:63
  11.2 81.3 %all-gather.16.cloned.1.call-start = ((), (), s32[]{:S(2)}) async-start(), calls=%async_computation.13 | async-start | bytes 2359296 | tf_op jit(solution)/shard_map/all_gather | solution.py:597
  64.1 83.5 %reduce-scatter.13.cloned.1.call-start = ((), (), s32[]{:S(2)}) async-start(), calls=%async_computation.14 | async-start | bytes 2949120 | tf_op jit(solution)/shard_map/reduce_scatter | solution.py:323
  99.7 100.5 %all-gather.18.cloned.1.call-start = ((), (), s32[]{:S(2)}) async-start(), calls=%async_computation.15 | async-start | bytes 2949120 | tf_op jit(solution)/shard_map/all_gather | solution.py:63
  150.7 90.0 %all-gather.20.cloned.1.call-start = ((), (), s32[]{:S(2)}) async-start(), calls=%async_computation.16 | async-start | bytes 5898240 | tf_op jit(solution)/shard_map/all_gather | solution.py:365
  204.3 81.3 %all-gather.22.cloned.1.call-start = ((), (), s32[]{:S(2)}) async-start(), calls=%async_computation.17 | async-start | bytes 6488064 | tf_op jit(solution)/shard_map/all_gather | solution.py:597
  240.7 96.1 %reduce-scatter.15.cloned.1.call-start = ((), (), s32[]{:S(2)}) async-start(), calls=%async_computation.18 | async-start | bytes 2949120 | tf_op jit(solution)/shard_map/reduce_scatter | solution.py:67
  288.9 100.7 %all-gather.24.cloned.1.call-start = ((), (), s32[]{:S(2)}) async-start(), calls=%async_computation.19 | async-start | bytes 2949120 | tf_op jit(solution)/shard_map/all_gather | solution.py:63
  340.1 133.0 %reduce-scatter.17.cloned.1.call-start = ((), (), s32[]{:S(2)}) async-start(), calls=%async_computation.20 | async-start | bytes 2949120 | tf_op jit(solution)/shard_map/reduce_scatter | solution.py:67
  395.6 5.6 collective-permute-start
  426.3 99.5 %all-gather.26.cloned.1.call-start = ((), (), s32[]{:S(2)}) async-start(), calls=%async_computation.21 | async-start | bytes 2949120 | tf_op jit(solution)/shard_map/all_gather | solution.py:63
  476.2 108.8 %reduce-scatter.19.cloned.1.call-start = ((), (), s32[]{:S(2)}) async-start(), calls=%async_computation.22 | async-start | bytes 2949120 | tf_op jit(solution)/shard_map/reduce_scatter | solution.py:67
  538.4 103.0 %all-gather.28.cloned.1.call-start = ((), (), s32[]{:S(2)}) async-start(), calls=%async_computation.23 | async-start | bytes 2949120 | tf_op jit(solution)/shard_map/all_gather | solution.py:73
  591.9 111.0 %reduce-scatter.21.cloned.1.call-start = ((), (), s32[]{:S(2)}) async-start(), calls=%async_computation.24 | async-start | bytes 2949120 | tf_op jit(solution)/shard_map/reduce_scatter | solution.py:77
  656.3 101.2 %all-gather.30.cloned.1.call-start = ((), (), s32[]{:S(2)}) async-start(), calls=%async_computation.25 | async-start | bytes 2949120 | tf_op jit(solution)/shard_map/all_gather | solution.py:73
  708.0 143.0 %reduce-scatter.23.cloned.1.call-start = ((), (), s32[]{:S(2)}) async-start(), calls=%async_computation.26 | async-start | bytes 2949120 | tf_op jit(solution)/shard_map/reduce_scatter | solution.py:77
  803.6 101.2 %all-gather.32.cloned.1.call-start = ((), (), s32[]{:S(2)}) async-start(), calls=%async_computation.27 | async-start | bytes 2949120 | tf_op jit(solution)/shard_map/all_gather | solution.py:73
  855.3 110.6 %reduce-scatter.25.cloned.1.call-start = ((), (), s32[]{:S(2)}) async-start(), calls=%async_computation.28 | async-start | bytes 6488064 | tf_op jit(solution)/shard_map/reduce_scatter | solution.py:388
  904.9 111.3 %reduce-scatter.27.cloned.1.call-start = ((), (), s32[]{:S(2)}) async-start(), calls=%async_computation.29 | async-start | bytes 5898240 | tf_op jit(solution)/shard_map/reduce_scatter | solution.py:404
  966.1 104.1 %reduce-scatter.29.cloned.1.call-start = ((), (), s32[]{:S(2)}) async-start(), calls=%async_computation.30 | async-start | bytes 2949120 | tf_op jit(solution)/shard_map/reduce_scatter | solution.py:77
  1022.3 101.9 %all-gather.34.cloned.1.call-start = ((), (), s32[]{:S(2)}) async-start(), calls=%async_computation.31 | async-start | bytes 2949120 | tf_op jit(solution)/shard_map/all_gather | solution.py:73
  1074.7 94.0 %reduce-scatter.31.cloned.1.call-start = ((), (), s32[]{:S(2)}) async-start(), calls=%async_computation.32 | async-start | bytes 2654208 | tf_op jit(solution)/shard_map/reduce_scatter | solution.py:337
  1124.3 94.5 %reduce-scatter.33.cloned.1.call-start = ((), (), s32[]{:S(2)}) async-start(), calls=%async_computation.33 | async-start | bytes 2949120 | tf_op jit(solution)/shard_map/reduce_scatter | solution.py:77
  1168.7 129.1 %reduce-scatter.35.cloned.1.call-start = ((), (), s32[]{:S(2)}) async-start(), calls=%async_computation.34 | async-start | bytes 4718592 | tf_op jit(solution)/shard_map/reduce_scatter | solution.py:602
  (128 other events, 1572.5 us)
Sparse Core Ops, SparseCore 0:
  11.3 52.6 all-gather.13
  65.9 26.5 all-gather.15
  99.8 47.6 reduce-scatter.12
  150.8 49.3 all-gather.17
  204.4 36.1 all-gather.19
  242.4 43.1 all-gather.21
  289.0 47.6 reduce-scatter.14
  340.2 49.3 all-gather.23
  426.4 46.7 reduce-scatter.16
  476.3 49.3 all-gather.25
  538.5 46.4 reduce-scatter.18
  592.0 49.3 all-gather.27
  656.4 46.4 reduce-scatter.20
  708.1 49.3 all-gather.29
  803.8 47.1 reduce-scatter.22
  855.5 49.3 all-gather.31
  908.1 57.7 reduce-scatter.24
  968.3 47.8 reduce-scatter.26
  1022.5 47.6 reduce-scatter.28
  1074.8 49.3 all-gather.33
  1127.6 41.0 reduce-scatter.30
  1171.0 47.7 reduce-scatter.32
  1225.8 51.9 reduce-scatter.34

commit v7 on v6

--- a/solution.py
+++ b/solution.py
@@ -333,18 +333,21 @@
     out_bias_grad = jnp.sum(grad_branch.astype(jnp.float32), axis=(0, 1))
     wide_grad = widen_grad(grad_branch)
     if beside is not None:
-        wide_grad, beside = together(wide_grad, beside)
-        beside = lax.psum_scatter(beside, ("fsdp", "ctx"), scatter_dimension=0, tiled=True)
+        wide_grad, beside = together(wide_grad, exchange(beside, ("fsdp", "ctx")))
+        beside = add_up(beside)
     active = jax.nn.silu(hidden_pre).astype(jnp.bfloat16)
     out_grad = weight_sum(wide_grad, active)
     grad_pre = (rows_in(wide_grad, weight_out) * silu_slope(hidden_pre)).astype(jnp.bfloat16)
     in_bias_grad = jnp.sum(grad_pre.astype(jnp.float32), axis=(0, 1))
     in_grad = weight_sum(wide_rows, grad_pre)
     partial_rows = rows_out(grad_pre, weight_in).astype(jnp.bfloat16)
+    grad_normed = narrow_grad(partial_rows)
     if beside is not None:
-        partial_rows, beside = together(partial_rows, beside)
-    grad_normed = narrow_grad(partial_rows)
+        in_grad = exchange(in_grad.astype(jnp.bfloat16), ("fsdp", "ctx"))
+        out_grad = exchange(out_grad.astype(jnp.bfloat16), ("fsdp", "ctx"))
     grad_normed, in_grad, out_grad = together(grad_normed, in_grad, out_grad)
+    if beside is not None:
+        in_grad, out_grad = add_up(in_grad), add_up(out_grad)
     grad_in, gain_grad, shift_grad = norm_backward(grad_normed, standard, inverse, norm_gain)
     return (
         grad_stream + grad_in,
@@ -401,7 +404,7 @@
     out_grad = weight_sum(wide_grad, mixed_token_rows)
     inner_parts = split_columns(inner, inner_grads)
     table_grad = table_turned[:, LEFT : LEFT + rel_table.shape[0]].T
-    pair_low = lax.psum_scatter(pair_terms, "ctx", scatter_dimension=2, tiled=True)
+    pair_low = add_up(exchange(pair_terms, "ctx", 2)).astype(jnp.bfloat16)
     key_low, value_low = pair_low[0], pair_low[1]
     query_bias_grad = jnp.sum(query_low.astype(jnp.float32), axis=(0, 1))
     value_bias_grad = jnp.sum(value_low.astype(jnp.float32), axis=(0, 1))
@@ -597,10 +600,16 @@
     return lax.all_gather(shard, ("fsdp", "ctx"), axis=0, tiled=True)
 
 
-def scatter_sum(*grads):
-    joined = jnp.concatenate([grad.astype(jnp.bfloat16) for grad in grads], axis=1)
-    part = lax.psum_scatter(joined, ("fsdp", "ctx"), scatter_dimension=0, tiled=True)
-    return split_columns(part, grads)
+def exchange(joined, axes, dim=0):
+    count = lax.axis_size(axes)
+    shape = joined.shape
+    parts = joined.reshape(shape[:dim] + (count, shape[dim] // count) + shape[dim + 1 :])
+    parts = jnp.moveaxis(parts, dim, 0)
+    return lax.all_to_all(parts, axes, split_axis=0, concat_axis=0, tiled=True)
+
+
+def add_up(received):
+    return jnp.sum(received.astype(jnp.float32), axis=0)
 
 
 def split_columns(part, grads):
@@ -820,7 +829,7 @@
         grad_one, saved_one, ffn1_gain, ffn1_in_all, ffn1_out_all, beside
     )
     attn_parts = split_columns(beside, beside_mats)
-    ffn1_parts = scatter_sum(ffn1_grads[2], ffn1_grads[4])
+    ffn1_parts = (ffn1_grads[2], ffn1_grads[4])
     shared = finish_small(
         attn_parts[-1],
         whole_parts,

time: 1320 us -> 1320 us (level)
  waiting for transfers between devices: 747 us -> 700 us
  blocking collectives: 132 us -> 162 us
  starting transfers between devices: 5.44 us -> 19.6 us
    all_to_all x0 -> x3, waiting for transfers between devices: none -> 83.1 us  [exchange(): return lax.all_to_all(parts, axes, split_axis=0, concat_axis=0, tiled=True)]
    reduce_scatter x3 -> x0, waiting for transfers between devices: 76.9 us -> none  [the longest x1 46 us: attn_backward(): lax.psum_scatter(pair_terms, 'ctx', scatter_dimension=2, tiled=True)]
    reduce_scatter x4, waiting for transfers between devices: 146 us -> 111 us  [narrow_grad(): lax.psum_scatter(partial_rows.astype(jnp.bfloat16), 'tp', scatter_dimensi...]
    all_to_all x0 -> x1, blocking collectives: none -> 33.1 us  [exchange(): return lax.all_to_all(parts, axes, split_axis=0, concat_axis=0, tiled=True)]
    all_gather x4, waiting for transfers between devices: 158 us -> 140 us  [widen_grad(): return lax.all_gather(grad_branch, 'tp', axis=1, tiled=True)]
    all_to_all x0 -> x3, starting transfers between devices: none -> 14.2 us  [exchange(): return lax.all_to_all(parts, axes, split_axis=0, concat_axis=0, tiled=True)]
    unnamed x278 -> x294, local copies, waits for them, and re-layouts: 35.3 us -> 31 us
  transfers between devices with their start and end apart: 25 -> 25, of which waited for: 21 -> 21; matrix products, arithmetic and copies ran while one was open for 13% -> 10% of each run, Pallas kernels for 7% -> 7%
where the time goes in v7:
time: 1320 us; the launch traced here: 1310 us
  waiting for transfers between devices  700 us (53%)
  blocking collectives  162 us (12%)
  matrix products  134 us (10%)
  Pallas kernels  103 us (8%)
  local copies, waits for them, and re-layouts  88 us (7%)
  other arithmetic  81.8 us (6%)
  starting transfers between devices  19.6 us (1%)
  between operations  18.4 us (1%)
    all_gather x4, waiting for transfers between devices, widen(): return lax.all_gather(normed.astype(jnp.bfloat16), 'tp', axis=1, tiled=True)  157 us
    all_gather x4, waiting for transfers between devices, widen_grad(): return lax.all_gather(grad_branch, 'tp', axis=1, tiled=True)  140 us
    reduce_scatter x3, waiting for transfers between devices, narrow(): lax.psum_scatter(partial_rows.astype(jnp.bfloat16), 'tp', scatter_dimensi...  139 us
    reduce_scatter x4, waiting for transfers between devices, narrow_grad(): lax.psum_scatter(partial_rows.astype(jnp.bfloat16), 'tp', scatter_dimensi...  111 us
    all_to_all x3, waiting for transfers between devices, exchange(): return lax.all_to_all(parts, axes, split_axis=0, concat_axis=0, tiled=True)  83.1 us
    all_gather x8, blocking collectives, gather_rows(): return lax.all_gather(shard, ('fsdp', 'ctx'), axis=0, tiled=True)  77.1 us
    pallas_call x1, Pallas kernels, attend_back(): pl.pallas_call(functools.partial(attend_back_kernel, reach), out_shape=(j...  56.6 us
    dot_general x10, matrix products, rows_in(): jnp.einsum('zub,bx->zux', left_reach, right_reach, preferred_element_type...  48.6 us
  transfers between devices with their start and end apart: 25, of which 21 were waited for; matrix products, arithmetic and copies ran while one was open for 10% of the time, Pallas kernels for 7%

profile of v7, /device:TPU:0, one launch (start us, length us, event | category | flops | bytes accessed | tf_op | source)
XLA Modules:
  0.0 1306.9 jit_solution(40705610744031)
XLA Ops:
  51.1 12.9 all-gather.14.cloned.1.call-done
  71.0 21.5 %all-gather.16.cloned.1.call-done = bf16[1024,1024]{1,0:T(8,128)(2,1)} async-done(((bf16[128,1024]{1,0:T(8,128)(2,1)}), bf16[1024,1024]{1,0:T(8,128)(2,1)}) %all-gather.16.cloned.1.call-update) | async-done | bytes 2097168 | tf_op jit(solution)/shard_map/all_gather | solution.py:600
  152.0 48.2 %all-gather.18.cloned.1.call-done = bf16[3,384,1024]{2,1,0:T(8,128)(2,1)} async-done(((bf16[3,96,1024]{2,1,0:T(8,128)(2,1)}), bf16[3,384,1024]{2,1,0:T(8,128)(2,1)}) %all-gather.18.cloned.1.call-update) | async-done | bytes 2359312 | tf_op jit(solution)/shard_map/all_gather | solution.py:63
  207.9 32.8 %all-gather.20.cloned.1.call-done.key_ref.value_ref = bf16[3,1536,512]{2,1,0:T(8,128)(2,1)} async-done(((bf16[3,384,512]{2,1,0:T(8,128)(2,1)}), bf16[3,1536,512]{2,1,0:T(8,128)(2,1)}) %all-gather.20.cloned.1.call-update) | async-done | bytes 4718608 | tf_op jit(solution)/shard_map/all_gather | solution.py:368
  245.8 34.6 %attend.1 = (bf16[3,384,256]{2,1,0:T(8,128)(2,1)}, bf16[3,4,384,1536]{3,2,1,0:T(8,128)(2,1)}) custom-call(s32[1]{0:T(128)} %bitcast.2.start_ref, bf16[3,384,256]{2,1,0:T(8,128)(2,1)} %fusion.32.query_ref, bf16[3,1536,512]{2,1,0:T(8,128)(2,1)} %all-gather.20.cloned.1.call-done.key_ref.value_ref, ...), custom_call_target="tpu_custom_call" | custom-call | flops 3623878656 | bytes 8388608 | tf_op jit(solution)/shard_map/attend/pallas_call | solution.py:239
  289.0 47.8 %reduce-scatter.12.cloned.1.call-done = bf16[3,96,1024]{2,1,0:T(8,128)(2,1)} async-done(((bf16[3,384,1024]{2,1,0:T(8,128)(2,1)}), bf16[3,96,1024]{2,1,0:T(8,128)(2,1)}) %reduce-scatter.12.cloned.1.call-update) | async-done | bytes 589840 | tf_op jit(solution)/shard_map/reduce_scatter | solution.py:67
  342.1 47.5 %all-gather.24.cloned.1.call-done = bf16[3,384,1024]{2,1,0:T(8,128)(2,1)} async-done(((bf16[3,96,1024]{2,1,0:T(8,128)(2,1)}), bf16[3,384,1024]{2,1,0:T(8,128)(2,1)}) %all-gather.24.cloned.1.call-update) | async-done | bytes 2359312 | tf_op jit(solution)/shard_map/all_gather | solution.py:63
  407.6 13.9 %all-gather = f32[8,3,384]{2,1,0:T(4,128)} all-gather(f32[2,3,384]{2,1,0:T(4,128)S(1)} %pad_maximum_fusion.2), channel_id=2, replica_groups=mesh['fsdp'=2,'ctx'=4,'tp'=4] {'tp'}, dimensions={0}, use_global_device_ids=true | all-gather | bytes 46080 | tf_op jit(solution)/shard_map/all_gather | solution.py:440
  426.4 46.8 %reduce-scatter.14.cloned.1.call-done = bf16[3,96,1024]{2,1,0:T(8,128)(2,1)} async-done(((bf16[3,384,1024]{2,1,0:T(8,128)(2,1)}), bf16[3,96,1024]{2,1,0:T(8,128)(2,1)}) %reduce-scatter.14.cloned.1.call-update) | async-done | bytes 589840 | tf_op jit(solution)/shard_map/reduce_scatter | solution.py:67
  477.2 48.6 %all-gather.26.cloned.1.call-done = bf16[3,384,1024]{2,1,0:T(8,128)(2,1)} async-done(((bf16[3,96,1024]{2,1,0:T(8,128)(2,1)}), bf16[3,384,1024]{2,1,0:T(8,128)(2,1)}) %all-gather.26.cloned.1.call-update) | async-done | bytes 2359312 | tf_op jit(solution)/shard_map/all_gather | solution.py:63
  540.8 44.3 %reduce-scatter.16.cloned.1.call-done = bf16[3,96,1024]{2,1,0:T(8,128)(2,1)} async-done(((bf16[3,384,1024]{2,1,0:T(8,128)(2,1)}), bf16[3,96,1024]{2,1,0:T(8,128)(2,1)}) %reduce-scatter.16.cloned.1.call-update) | async-done | bytes 589840 | tf_op jit(solution)/shard_map/reduce_scatter | solution.py:67
  592.0 49.5 %all-gather.28.cloned.1.call-done = bf16[3,384,1024]{2,1,0:T(8,128)(2,1)} async-done(((bf16[3,96,1024]{2,1,0:T(8,128)(2,1)}), bf16[3,384,1024]{2,1,0:T(8,128)(2,1)}) %all-gather.28.cloned.1.call-update) | async-done | bytes 2359312 | tf_op jit(solution)/shard_map/all_gather | solution.py:73
  670.2 32.8 %reduce-scatter.18.cloned.1.call-done = bf16[3,96,1024]{2,1,0:T(8,128)(2,1)} async-done(((bf16[3,384,1024]{2,1,0:T(8,128)(2,1)}), bf16[3,96,1024]{2,1,0:T(8,128)(2,1)}) %reduce-scatter.18.cloned.1.call-update) | async-done | bytes 589840 | tf_op jit(solution)/shard_map/reduce_scatter | solution.py:77
  708.1 49.5 %all-gather.30.cloned.1.call-done = bf16[3,384,1024]{2,1,0:T(8,128)(2,1)} async-done(((bf16[3,96,1024]{2,1,0:T(8,128)(2,1)}), bf16[3,384,1024]{2,1,0:T(8,128)(2,1)}) %all-gather.30.cloned.1.call-update) | async-done | bytes 2359312 | tf_op jit(solution)/shard_map/all_gather | solution.py:73
  762.5 13.8 %all-gather.1 = f32[8,3,384]{2,1,0:T(4,128)} all-gather(f32[2,3,384]{2,1,0:T(4,128)S(1)} %pad_maximum_fusion.3), channel_id=3, replica_groups=mesh['fsdp'=2,'ctx'=4,'tp'=4] {'tp'}, dimensions={0}, use_global_device_ids=true | all-gather | bytes 46080 | tf_op jit(solution)/shard_map/all_gather | solution.py:440
  811.7 39.2 %reduce-scatter.20.cloned.1.call-done = bf16[3,96,1024]{2,1,0:T(8,128)(2,1)} async-done(((bf16[3,384,1024]{2,1,0:T(8,128)(2,1)}), bf16[3,96,1024]{2,1,0:T(8,128)(2,1)}) %reduce-scatter.20.cloned.1.call-update) | async-done | bytes 589840 | tf_op jit(solution)/shard_map/reduce_scatter | solution.py:77
  863.8 41.0 %all-gather.32.cloned.1.call-done = bf16[3,384,1024]{2,1,0:T(8,128)(2,1)} async-done(((bf16[3,96,1024]{2,1,0:T(8,128)(2,1)}), bf16[3,384,1024]{2,1,0:T(8,128)(2,1)}) %all-gather.32.cloned.1.call-update) | async-done | bytes 2359312 | tf_op jit(solution)/shard_map/all_gather | solution.py:73
  909.1 56.6 %attend_back.1 = (bf16[3,384,256]{2,1,0:T(8,128)(2,1)}, bf16[2,3,1536,256]{3,2,1,0:T(8,128)(2,1)}, f32[64,384]{1,0:T(8,128)}) custom-call(s32[1]{0:T(128)} %bitcast.2.start_ref, bf16[3,384,256]{2,1,0:T(8,128)(2,1)} %fusion.32.query_ref, bf16[3,1536,512]{2,1,0:T(8,128)(2,1)} %all-gather.20.cloned.1.call-done.key_ref.value_ref, ...), custom_call_target="tpu_custom_call" | custom-call | flops 9059696640 | bytes 16777216 | tf_op jit(solution)/shard_map/attend_back/pallas_call | solution.py:266
  979.0 50.8 %all-to-all-done = bf16[4,2,3,384,256]{4,3,2,1,0:T(8,128)(2,1)} async-done(((bf16[4,2,3,384,256]{4,3,2,1,0:T(8,128)(2,1)}), bf16[4,2,3,384,256]{4,3,2,1,0:T(8,128)(2,1)}, u32[]{:S(2)}, u32[]{:S(2)}) %all-to-all-start) | async-done | bytes 4718624 | tf_op jit(solution)/shard_map/all_to_all | solution.py:608
  1047.4 38.9 %reduce-scatter.24.cloned.1.call-done = bf16[3,96,1024]{2,1,0:T(8,128)(2,1)} async-done(((bf16[3,384,1024]{2,1,0:T(8,128)(2,1)}), bf16[3,96,1024]{2,1,0:T(8,128)(2,1)}) %reduce-scatter.24.cloned.1.call-update) | async-done | bytes 589840 | tf_op jit(solution)/shard_map/reduce_scatter | solution.py:77
  1119.3 33.1 %all_to_all.20 = bf16[8,128,1152]{2,1,0:T(8,128)(2,1)} all-to-all(bf16[8,128,1152]{2,1,0:T(8,128)(2,1)S(1)} %bitcast.234), channel_id=1, replica_groups=mesh['fsdp'=2,'ctx'=4,'tp'=4] {'fsdp','ctx'}, dimensions={0} | all-to-all | bytes 4718592 | tf_op jit(solution)/shard_map/all_to_all | solution.py:608
  1184.4 20.0 %all-to-all-done.3 = bf16[8,128,1024]{2,1,0:T(8,128)(2,1)} async-done(((bf16[8,128,1024]{2,1,0:T(8,128)(2,1)}), bf16[8,128,1024]{2,1,0:T(8,128)(2,1)}, u32[]{:S(2)}, u32[]{:S(2)}) %all-to-all-start.3) | async-done | bytes 2097184 | tf_op jit(solution)/shard_map/all_to_all | solution.py:608
  1223.5 12.3 all-to-all-done.2
  1241.1 13.3 %all_gather.98 = f32[4,58,128]{2,1,0:T(8,128)S(1)} all-gather(f32[1,58,128]{2,1,0:T(8,128)S(1)} %pad_bitcast_fusion), channel_id=1, replica_groups=mesh['fsdp'=2,'ctx'=4,'tp'=4] {'tp'}, dimensions={0}, use_global_device_ids=true | all-gather | bytes 148480 | tf_op jit(solution)/shard_map/all_gather | solution.py:641
  (510 shorter events, 438.9 us)
Async XLA Ops:
  7.2 56.8 %all-gather.14.cloned.1.call-start = ((), (), s32[]{:S(2)}) async-start(), calls=%async_computation.13 | async-start | bytes 2949120 | tf_op jit(solution)/shard_map/all_gather | solution.py:63
  11.2 81.3 %all-gather.16.cloned.1.call-start = ((), (), s32[]{:S(2)}) async-start(), calls=%async_computation.14 | async-start | bytes 2359296 | tf_op jit(solution)/shard_map/all_gather | solution.py:600
  64.1 83.5 %reduce-scatter.10.cloned.1.call-start = ((), (), s32[]{:S(2)}) async-start(), calls=%async_computation.15 | async-start | bytes 2949120 | tf_op jit(solution)/shard_map/reduce_scatter | solution.py:323
  99.7 100.5 %all-gather.18.cloned.1.call-start = ((), (), s32[]{:S(2)}) async-start(), calls=%async_computation.16 | async-start | bytes 2949120 | tf_op jit(solution)/shard_map/all_gather | solution.py:63
  150.7 90.0 %all-gather.20.cloned.1.call-start = ((), (), s32[]{:S(2)}) async-start(), calls=%async_computation.17 | async-start | bytes 5898240 | tf_op jit(solution)/shard_map/all_gather | solution.py:368
  204.3 81.3 %all-gather.22.cloned.1.call-start = ((), (), s32[]{:S(2)}) async-start(), calls=%async_computation.18 | async-start | bytes 6488064 | tf_op jit(solution)/shard_map/all_gather | solution.py:600
  240.7 96.1 %reduce-scatter.12.cloned.1.call-start = ((), (), s32[]{:S(2)}) async-start(), calls=%async_computation.19 | async-start | bytes 2949120 | tf_op jit(solution)/shard_map/reduce_scatter | solution.py:67
  288.9 100.7 %all-gather.24.cloned.1.call-start = ((), (), s32[]{:S(2)}) async-start(), calls=%async_computation.20 | async-start | bytes 2949120 | tf_op jit(solution)/shard_map/all_gather | solution.py:63
  340.1 133.1 %reduce-scatter.14.cloned.1.call-start = ((), (), s32[]{:S(2)}) async-start(), calls=%async_computation.21 | async-start | bytes 2949120 | tf_op jit(solution)/shard_map/reduce_scatter | solution.py:67
  395.6 5.6 collective-permute-start
  426.3 99.5 %all-gather.26.cloned.1.call-start = ((), (), s32[]{:S(2)}) async-start(), calls=%async_computation.22 | async-start | bytes 2949120 | tf_op jit(solution)/shard_map/all_gather | solution.py:63
  476.3 108.8 %reduce-scatter.16.cloned.1.call-start = ((), (), s32[]{:S(2)}) async-start(), calls=%async_computation.23 | async-start | bytes 2949120 | tf_op jit(solution)/shard_map/reduce_scatter | solution.py:67
  538.5 103.0 %all-gather.28.cloned.1.call-start = ((), (), s32[]{:S(2)}) async-start(), calls=%async_computation.24 | async-start | bytes 2949120 | tf_op jit(solution)/shard_map/all_gather | solution.py:73
  591.9 111.0 %reduce-scatter.18.cloned.1.call-start = ((), (), s32[]{:S(2)}) async-start(), calls=%async_computation.25 | async-start | bytes 2949120 | tf_op jit(solution)/shard_map/reduce_scatter | solution.py:77
  656.3 101.2 %all-gather.30.cloned.1.call-start = ((), (), s32[]{:S(2)}) async-start(), calls=%async_computation.26 | async-start | bytes 2949120 | tf_op jit(solution)/shard_map/all_gather | solution.py:73
  708.1 142.9 %reduce-scatter.20.cloned.1.call-start = ((), (), s32[]{:S(2)}) async-start(), calls=%async_computation.27 | async-start | bytes 2949120 | tf_op jit(solution)/shard_map/reduce_scatter | solution.py:77
  803.6 101.2 %all-gather.32.cloned.1.call-start = ((), (), s32[]{:S(2)}) async-start(), calls=%async_computation.28 | async-start | bytes 2949120 | tf_op jit(solution)/shard_map/all_gather | solution.py:73
  855.3 110.6 %reduce-scatter.22.cloned.1.call-start = ((), (), s32[]{:S(2)}) async-start(), calls=%async_computation.29 | async-start | bytes 6488064 | tf_op jit(solution)/shard_map/reduce_scatter | solution.py:391
  970.8 58.9 %all-to-all-start = ((bf16[4,2,3,384,256]{4,3,2,1,0:T(8,128)(2,1)}), bf16[4,2,3,384,256]{4,3,2,1,0:T(8,128)(2,1)}, u32[]{:S(2)}, u32[]{:S(2)}) async-start(bf16[4,2,3,384,256]{4,3,2,1,0:T(8,128)(2,1)} %bitcast.232), calls=%async_computation.7 | async-start | bytes 9437184 | tf_op jit(solution)/shard_map/all_to_all | solution.py:608
  975.9 110.3 %reduce-scatter.24.cloned.1.call-start = ((), (), s32[]{:S(2)}) async-start(), calls=%async_computation.30 | async-start | bytes 2949120 | tf_op jit(solution)/shard_map/reduce_scatter | solution.py:77
  1038.4 114.0 %all-gather.34.cloned.1.call-start = ((), (), s32[]{:S(2)}) async-start(), calls=%async_computation.31 | async-start | bytes 2949120 | tf_op jit(solution)/shard_map/all_gather | solution.py:73
  1090.9 130.4 %reduce-scatter.26.cloned.1.call-start = ((), (), s32[]{:S(2)}) async-start(), calls=%async_computation.32 | async-start | bytes 2949120 | tf_op jit(solution)/shard_map/reduce_scatter | solution.py:77
  1173.4 31.0 %all-to-all-start.3 = ((bf16[8,128,1024]{2,1,0:T(8,128)(2,1)}), bf16[8,128,1024]{2,1,0:T(8,128)(2,1)}, u32[]{:S(2)}, u32[]{:S(2)}) async-start(bf16[8,128,1024]{2,1,0:T(8,128)(2,1)} %bitcast.236), calls=%async_computation.12 | async-start | bytes 4194304 | tf_op jit(solution)/shard_map/all_to_all | solution.py:608
  1204.4 31.4 %all-to-all-start.2 = ((bf16[8,128,1024]{2,1,0:T(8,128)(2,1)}), bf16[8,128,1024]{2,1,0:T(8,128)(2,1)}, u32[]{:S(2)}, u32[]{:S(2)}) async-start(bf16[8,128,1024]{2,1,0:T(8,128)(2,1)} %bitcast.235), calls=%async_computation.11 | async-start | bytes 4194304 | tf_op jit(solution)/shard_map/all_to_all | solution.py:608
  (136 other events, 1600.4 us)
Sparse Core Ops, SparseCore 0:
  11.3 52.6 all-gather.13
  65.9 26.5 all-gather.15
  99.8 47.6 reduce-scatter.9
  150.8 49.3 all-gather.17
  204.5 36.1 all-gather.19
  242.4 43.1 all-gather.21
  289.0 47.6 reduce-scatter.11
  340.2 49.3 all-gather.23
  426.4 46.7 reduce-scatter.13
  476.4 49.3 all-gather.25
  538.6 46.4 reduce-scatter.15
  592.0 49.3 all-gather.27
  656.4 46.4 reduce-scatter.17
  708.2 49.3 all-gather.29
  803.7 47.1 reduce-scatter.19
  855.4 49.3 all-gather.31
  908.1 57.7 reduce-scatter.21
  1038.5 47.6 reduce-scatter.23
  1091.0 49.3 all-gather.33
  1166.1 45.3 reduce-scatter.25
